TPU v7x, 128 devices: a whole 4x4x4 slice. The times are simulated.
128 devices in a mesh: bl: 8 (over x, y_lo), freq: 16 (over z, y_hi, core).
Axes of the slice: x: 4, y: 4 (y_hi: 2, y_lo: 2; y = y_hi * 2 + y_lo), z: 4, core: 2. Of those that a mesh axis runs over, the one named last changes fastest.
Arguments:
- visibilities: float32 [2, 2, 256, 16384], P(None, None, 'freq', 'bl'), may hold values from -8 to 8
- sample_flag_weight: int32 [2, 256, 16384], P(None, 'freq', 'bl'), may hold values from 0 to 4
- baseline_station_pair: int32 [2, 16384], P(None, 'bl'), may hold values from 0 to 511, as said below
- baseline_spatial_coords: float32 [2, 2, 16384], P(None, None, 'bl'), may hold values from -6 to 6
- directions: float32 [2, 8], replicated, may hold values from -0.5 to 0.5
- source_flux: float32 [8, 256], P(None, 'freq'), may hold values from 0.5 to 2
- channel_ratio: float32 [256], P('freq'), may hold values from 0.7 to 1.4
- jones_gains: float32 [2, 8, 256, 512], P(None, None, 'freq'), may hold values from -4 to 4
- scaled_dual: float32 [2, 8, 256, 512], P(None, None, 'freq'), may hold values from -2 to 2
- consensus: float32 [2, 3, 8, 512], replicated, may hold values from -3 to 3
- penalty: float32 [8], replicated, may hold values from 0.3 to 3
Outputs:
- new_gains: float32 [2, 8, 256, 512], P(None, None, 'freq')
- new_consensus: float32 [2, 3, 8, 512], replicated
- new_dual: float32 [2, 8, 256, 512], P(None, None, 'freq')
- residuals: float32 [2, 2, 256, 16384], P(None, None, 'freq', 'bl')
Inputs may be any that keep to these rules, and one draw needn't show every extreme that they name: `baseline_station_pair`: the two stations of every baseline differ.
All inputs are finite; a program needn't handle non-finite values.
Results may differ from a plain program's by a relative error of at most 0.00016.
Values sent between devices are 32-bit elements; how exact they have to be, the bound alone decides.
No kernel may reach another device: no remote copies, remote signals or barrier semaphores. Data moves between devices by JAX's collectives and lax.ppermute only.
A program may use at most 64 MiB of HBM per device.

v0:
```python
import math

import jax
import jax.numpy as jnp
from jax import lax
from jax.sharding import Mesh
from jax.sharding import PartitionSpec as P

NPOLY = 3
ITERS = 3
BL = ("bl_0", "bl_1")
BL_FREQ = ("bl_0", "bl_1", "freq_0", "freq_1", "freq_2")
FREQ = ("freq_0", "freq_1", "freq_2")


robust_dof = 2.0
small_term = 1e-06
two_pi = 2.0 * math.pi


def by_axis(array, axes):
    for axis in axes:
        array = lax.psum(array, axis)
    return array


def split_up(array, dim, count):
    dims = array.shape
    pieces = array.reshape(*dims[:dim], count, dims[dim] // count, *dims[dim + 1 :])
    return jnp.moveaxis(pieces, dim, 0)


def sent_and_summed(array, axis, dim):
    pieces = split_up(array, dim, lax.axis_size(axis))
    arrived = lax.all_to_all(pieces, axis, split_axis=0, concat_axis=0, tiled=True)
    return arrived.sum(axis=0)


def copy_for_each(array, axis):
    count = lax.axis_size(axis)
    return lax.all_to_all(
        jnp.broadcast_to(array[None], (count, *array.shape)), axis, 0, 0, tiled=True
    )


def laid_out(pieces, dim):
    dims = list(pieces.shape[1:])
    dims[dim] *= pieces.shape[0]
    return jnp.moveaxis(pieces, 0, dim).reshape(dims)


def gathered_copies(array, axis, dim):
    pieces = copy_for_each(array, axis)
    return laid_out(pieces, dim)


def taken_together(array, axis):
    everything = copy_for_each(array, axis)
    return jnp.sum(everything, axis=0)


def together(arrays, axis):
    ends = [0]
    for a in arrays:
        ends.append(ends[-1] + a.size)
    subtotal = taken_together(jnp.concatenate([a.ravel() for a in arrays]), axis)
    return tuple((subtotal[b:e].reshape(a.shape) for a, b, e in zip(arrays, ends, ends[1:])))


def legendre(ratios):
    scaled = (ratios - 1.05) / 0.35
    values = [jnp.ones_like(scaled), scaled]
    values.append((3 * scaled * values[1] - 1 * values[0]) / 2)
    return jnp.stack(values[:NPOLY])


def coherency(coords, sky_dirs, fluxes, ratios):
    project = (
        sky_dirs[0][:, None, None] * coords[0][None] + sky_dirs[1][:, None, None] * coords[1][None]
    )
    phases = two_pi * project[:, :, None, :] * ratios[None, None, :, None]
    amplitude = fluxes[:, None, :, None]
    return (amplitude * jnp.cos(phases), amplitude * jnp.sin(phases))


def station_table(pair_row, station_list):
    positions = lax.broadcasted_iota(jnp.int32, (station_list, pair_row.shape[0]), 0)
    return (positions == pair_row[None, :]).astype(jnp.float32)


def pick_stations(gain_re, gain_im, table):
    stacked = jnp.stack([gain_re, gain_im])
    lead_shape = stacked.shape[:3]
    flat = stacked.reshape(-1, stacked.shape[3])
    picked = jnp.dot(
        flat, table, precision=lax.Precision.HIGHEST, preferred_element_type=jnp.float32
    )
    picked = picked.reshape(lead_shape + (table.shape[1],))
    return (picked[0], picked[1])


def predict(gain_re, gain_im, left_table, right_table, sky_re, sky_im):
    left_re, left_im = pick_stations(gain_re, gain_im, left_table)
    right_re, right_im = pick_stations(gain_re, gain_im, right_table)
    pair_re = left_re * right_re + left_im * right_im
    pair_im = left_im * right_re - left_re * right_im
    model_re = pair_re[:, None] * sky_re - pair_im[:, None] * sky_im
    model_im = pair_re[:, None] * sky_im + pair_im[:, None] * sky_re
    return ((left_re, left_im, right_re, right_im), model_re, model_im)


def residual_of(observed, model_re, model_im):
    return (observed[0] - jnp.sum(model_re, axis=0), observed[1] - jnp.sum(model_im, axis=0))


def robust_weights(flagged, error_re, error_im, sigma_sq):
    return (
        flagged
        * (robust_dof + 1.0)
        / (robust_dof + (error_re * error_re + error_im * error_im) / sigma_sq)
    )


def normal_terms(
    error_re,
    error_im,
    model_re,
    model_im,
    weights,
    sky_re,
    sky_im,
    side_gains,
    left_table,
    right_table,
):
    target_re = error_re[None] + model_re
    target_im = error_im[None] + model_im
    cross_re = sky_re * target_re + sky_im * target_im
    cross_im = sky_re * target_im - sky_im * target_re
    weight_wide = weights[None]
    summed_re = jnp.sum(weight_wide * cross_re, axis=1)
    summed_im = jnp.sum(weight_wide * cross_im, axis=1)
    powers = jnp.sum(weight_wide * (sky_re * sky_re + sky_im * sky_im), axis=1)
    left_re, left_im, right_re, right_im = side_gains
    first_re = right_re * summed_re - right_im * summed_im
    first_im = right_re * summed_im + right_im * summed_re
    second_re = left_re * summed_re + left_im * summed_im
    second_im = left_im * summed_re - left_re * summed_im
    first_norm = (right_re * right_re + right_im * right_im) * powers
    second_norm = (left_re * left_re + left_im * left_im) * powers
    stacked_first = jnp.stack([first_re, first_im, first_norm])
    stacked_second = jnp.stack([second_re, second_im, second_norm])
    lead_shape = stacked_first.shape[:3]
    baseline_count = stacked_first.shape[3]
    contract = (((1,), (1,)), ((), ()))
    into_first = lax.dot_general(
        stacked_first.reshape(-1, baseline_count),
        left_table,
        contract,
        precision=lax.Precision.HIGHEST,
        preferred_element_type=jnp.float32,
    )
    into_second = lax.dot_general(
        stacked_second.reshape(-1, baseline_count),
        right_table,
        contract,
        precision=lax.Precision.HIGHEST,
        preferred_element_type=jnp.float32,
    )
    return (into_first + into_second).reshape(lead_shape + (left_table.shape[0],))


def update_gains(gain_re, gain_im, normal_sums, anchor_re, anchor_im, effective_penalty):
    penalty_wide = effective_penalty[:, None, None]
    divisor = normal_sums[2] + penalty_wide
    solved_re = (normal_sums[0] + penalty_wide * anchor_re) / divisor
    solved_im = (normal_sums[1] + penalty_wide * anchor_im) / divisor
    return (0.5 * (gain_re + solved_re), 0.5 * (gain_im + solved_im))


def cholesky_solve(gram_total, flat_rhs):
    factor = jnp.linalg.cholesky(gram_total)
    matrix_order = gram_total.shape[0]
    forward = []
    for row_index in range(matrix_order):
        running = flat_rhs[row_index]
        for col_index in range(row_index):
            running = running - factor[row_index, col_index] * forward[col_index]
        forward.append(running / factor[row_index, row_index])
    backward = [None] * matrix_order
    for row_index in reversed(range(matrix_order)):
        running = forward[row_index]
        for col_index in range(row_index + 1, matrix_order):
            running = running - factor[col_index, row_index] * backward[col_index]
        backward[row_index] = running / factor[row_index, row_index]
    return jnp.stack(backward)


def solve_consensus(gram_total, rhs_total):
    matrix_order = gram_total.shape[0]
    flat_rhs = jnp.moveaxis(rhs_total, 1, 0).reshape(matrix_order, -1)
    solved = cholesky_solve(gram_total, flat_rhs)
    return jnp.moveaxis(
        solved.reshape((matrix_order, rhs_total.shape[0]) + rhs_total.shape[2:]), 0, 1
    )


def body(
    visibilities,
    sample_flag_weight,
    baseline_station_pair,
    baseline_spatial_coords,
    directions,
    source_flux,
    channel_ratio,
    jones_gains,
    scaled_dual,
    consensus,
    penalty,
):
    station_list = jones_gains.shape[3]
    baseline_list = baseline_station_pair.shape[1] * lax.axis_size(BL)
    solution_time_slots = visibilities.shape[1]
    effective_penalty = penalty * (2.0 * baseline_list * solution_time_slots / station_list)
    left_table = station_table(baseline_station_pair[0], station_list)
    right_table = station_table(baseline_station_pair[1], station_list)
    sky_re, sky_im = coherency(baseline_spatial_coords, directions, source_flux, channel_ratio)
    poly_basis = legendre(channel_ratio)
    gram_local = jnp.dot(poly_basis, poly_basis.T, precision=lax.Precision.HIGHEST)
    anchor = (
        jnp.einsum("jc,xjks->xkcs", poly_basis, consensus, precision=lax.Precision.HIGHEST)
        - scaled_dual
    )
    anchor_re, anchor_im = (anchor[0], anchor[1])
    flagged = sample_flag_weight.astype(jnp.float32)
    count_local = jnp.sum(flagged)
    gain_re, gain_im = (jones_gains[0], jones_gains[1])
    for iteration in range(ITERS):
        side_gains, model_re, model_im = predict(
            gain_re, gain_im, left_table, right_table, sky_re, sky_im
        )
        error_re, error_im = residual_of(visibilities, model_re, model_im)
        misfit_local = jnp.sum(flagged * (error_re * error_re + error_im * error_im))
        squares, weight_total = (by_axis(misfit_local, BL_FREQ), by_axis(count_local, BL_FREQ))
        sigma_sq = squares / (weight_total + 1.0) + small_term
        weights = robust_weights(flagged, error_re, error_im, sigma_sq)
        partial_value = normal_terms(
            error_re,
            error_im,
            model_re,
            model_im,
            weights,
            sky_re,
            sky_im,
            side_gains,
            left_table,
            right_table,
        )
        owned_sums = sent_and_summed(partial_value, BL, 3)
        own_width = owned_sums.shape[3]
        offset = lax.axis_index(BL) * own_width
        own_gain_re = lax.dynamic_slice_in_dim(gain_re, offset, own_width, 2)
        own_gain_im = lax.dynamic_slice_in_dim(gain_im, offset, own_width, 2)
        own_anchor_re = lax.dynamic_slice_in_dim(anchor_re, offset, own_width, 2)
        own_anchor_im = lax.dynamic_slice_in_dim(anchor_im, offset, own_width, 2)
        new_re, new_im = update_gains(
            own_gain_re, own_gain_im, owned_sums, own_anchor_re, own_anchor_im, effective_penalty
        )
        gathered = gathered_copies(jnp.stack([new_re, new_im]), BL, 3)
        gain_re, gain_im = (gathered[0], gathered[1])
    side_gains, model_re, model_im = predict(
        gain_re, gain_im, left_table, right_table, sky_re, sky_im
    )
    error_re, error_im = residual_of(visibilities, model_re, model_im)
    residuals = jnp.stack([error_re, error_im])
    new_gains = jnp.stack([gain_re, gain_im])
    rhs_local = jnp.einsum(
        "jc,xkcs->xjks", poly_basis, new_gains + scaled_dual, precision=lax.Precision.HIGHEST
    )
    rhs_total, gram_total = together((rhs_local, gram_local), FREQ)
    new_consensus = solve_consensus(gram_total, rhs_total)
    new_dual = (
        scaled_dual
        + new_gains
        - jnp.einsum("jc,xjks->xkcs", poly_basis, new_consensus, precision=lax.Precision.HIGHEST)
    )
    return (new_gains, new_consensus, new_dual, residuals)


def solution(mesh):
    split = Mesh(
        mesh.devices.reshape(4, 2, 4, 2, 2), ("bl_0", "bl_1", "freq_0", "freq_1", "freq_2")
    )
    in_specs = (
        P(None, None, FREQ, BL),
        P(None, FREQ, BL),
        P(None, BL),
        P(None, None, BL),
        P(),
        P(None, FREQ),
        P(FREQ),
        P(None, None, FREQ, None),
        P(None, None, FREQ, None),
        P(),
        P(),
    )
    out_specs = (P(None, None, FREQ, None), P(), P(None, None, FREQ, None), P(None, None, FREQ, BL))
    return jax.shard_map(body, mesh=split, in_specs=in_specs, out_specs=out_specs, check_vma=False)
```

profile of v0, /device:TPU:1, one launch (start us, length us, event | category | flops | bytes accessed | tf_op | source)
XLA Modules:
  0.0 416.6 jit_solution(2117024783144175393)
XLA Ops:
  10.9 9.0 %fusion.102 = (f32[2,16,2048]{2,1,0:T(8,128)S(1)}, f32[2,16,2048]{2,1,0:T(8,128)S(1)}) fusion(f32[8,16,2048]{2,1,0:T(8,128)S(1)} %bitcast.383, f32[16]{0:T(128)S(1)} %copy-done.32, f32[8,2,2048]{2,1,0:T(2,128)S(1)} %add_multiply_fusion, f32[8,16]{1,0:T(8,128)S(1)} %copy-done.31, f32[8,16,2048]{2,1,0:T(8,128)S(1)} %bitcast.381), kind=kLoop, calls=%fused_computation.115 | loop fusion | flops 5636096 | bytes 2753088 | tf_op jit(solution)/shard_map/reduce_sum | solution.py:113
  22.1 9.9 %all-reduce.1 = (f32[]{:T(128)}, f32[]{:T(128)}) all-reduce(f32[]{:T(128)} %get-tuple-element.50, f32[]{:T(128)} %get-tuple-element.49), channel_id=1, replica_groups=mesh['bl_0'=4,'bl_1'=2,'freq_0'=4,'freq_1'=2,'freq_2'=2] {'bl_0'}, use_global_device_ids=true, to_apply=%region_3.0 | all-reduce | flops 2 | bytes 16 | tf_op jit(solution)/shard_map/psum | solution.py:23
  36.4 10.4 %all-reduce = (f32[]{:T(128)}, f32[]{:T(128)}) all-reduce(f32[]{:T(128)} %get-tuple-element.59, f32[]{:T(128)} %get-tuple-element.60), channel_id=1, replica_groups=mesh['bl_0'=4,'bl_1'=2,'freq_0'=4,'freq_1'=2,'freq_2'=2] {'freq_0'}, use_global_device_ids=true, to_apply=%region_5.0 | all-reduce | flops 2 | bytes 16 | tf_op jit(solution)/shard_map/psum | solution.py:23
  52.6 10.3 %all-reduce.2 = (f32[]{:T(128)}, f32[]{:T(128)}) all-reduce(f32[]{:T(128)} %get-tuple-element.57, f32[]{:T(128)} %get-tuple-element.58), channel_id=1, replica_groups=mesh['bl_0'=4,'bl_1'=2,'freq_0'=4,'freq_1'=2,'freq_2'=2] {'freq_2'}, use_global_device_ids=true, to_apply=%region_7.0 | all-reduce | flops 2 | bytes 16 | tf_op jit(solution)/shard_map/psum | solution.py:23
  65.3 10.9 %fusion.36 = (f32[8,16,2048]{2,1,0:T(8,128)S(1)}, f32[8,16,2048]{2,1,0:T(8,128)S(1)}, f32[8,16,2048]{2,1,0:T(8,128)S(1)}) fusion(f32[2,16,2048]{2,1,0:T(8,128)} %get-tuple-element.130, f32[2,16,2048]{2,1,0:T(8,128)S(1)} %get-tuple-element.129, f32[2,16,2048]{2,1,0:T(8,128)S(1)} %add_divide_fusion.2, f32[8,16,2048]{2,1,0:T(8,128)S(1)} %bitcast.384, ...), kind=kLoop, calls=%fused_computation.46 | loop fusion | flops 12845056 | bytes 6160960 | tf_op jit(solution)/shard_map/reduce_sum | solution.py:141
  95.1 10.6 %all-to-all-done = f32[8,1,24576]{2,1,0:T(1,128)S(1)} async-done(((f32[8,1,24576]{2,1,0:T(1,128)}), f32[8,1,24576]{2,1,0:T(1,128)S(1)}, u32[]{:S(2)}, u32[]{:S(2)}) %all-to-all-start) | async-done | bytes 786464 | tf_op jit(solution)/shard_map/all_to_all | solution.py:35
  111.3 10.8 %all_to_all.36 = f32[8,1,16384]{2,1,0:T(1,128)S(1)} all-to-all(f32[8,1,16384]{2,1,0:T(1,128)S(1)} %reshape.925), channel_id=1, replica_groups=mesh['bl_0'=4,'bl_1'=2,'freq_0'=4,'freq_1'=2,'freq_2'=2] {'bl_0','bl_1'}, dimensions={0} | all-to-all | bytes 1048576 | tf_op jit(solution)/shard_map/all_to_all | solution.py:41
  132.2 8.9 %fusion.98 = (f32[2,16,2048]{2,1,0:T(8,128)S(1)}, f32[2,16,2048]{2,1,0:T(8,128)S(1)}) fusion(f32[8,16,2048]{2,1,0:T(8,128)S(1)} %bitcast.391, f32[8,16,2048]{2,1,0:T(8,128)S(1)} %bitcast.389, f32[16]{0:T(128)S(1)} %copy-done.32, f32[8,2,2048]{2,1,0:T(2,128)S(1)} %add_multiply_fusion, f32[8,16]{1,0:T(8,128)S(1)} %copy-done.31), kind=kLoop, calls=%fused_computation.111 | loop fusion | flops 5636096 | bytes 2753088 | tf_op jit(solution)/shard_map/reduce_sum | solution.py:113
  143.2 7.3 %psum.180 = f32[]{:T(128)} all-reduce(f32[]{:T(128)} %get-tuple-element.66), channel_id=1, replica_groups=mesh['bl_0'=4,'bl_1'=2,'freq_0'=4,'freq_1'=2,'freq_2'=2] {'bl_0'}, use_global_device_ids=true, to_apply=%region_21.0 | all-reduce | flops 1 | bytes 8 | tf_op jit(solution)/shard_map/psum | solution.py:23
  154.8 6.6 %psum.182 = f32[]{:T(128)} all-reduce(f32[]{:T(128)} %psum.181), channel_id=1, replica_groups=mesh['bl_0'=4,'bl_1'=2,'freq_0'=4,'freq_1'=2,'freq_2'=2] {'freq_0'}, use_global_device_ids=true, to_apply=%region_23.0 | all-reduce | flops 1 | bytes 8 | tf_op jit(solution)/shard_map/psum | solution.py:23
  169.0 11.8 %psum.184 = f32[]{:T(128)} all-reduce(f32[]{:T(128)} %psum.183), channel_id=1, replica_groups=mesh['bl_0'=4,'bl_1'=2,'freq_0'=4,'freq_1'=2,'freq_2'=2] {'freq_2'}, use_global_device_ids=true, to_apply=%region_25.0 | all-reduce | flops 1 | bytes 8 | tf_op jit(solution)/shard_map/psum | solution.py:23
  182.4 10.9 %fusion.45 = (f32[8,16,2048]{2,1,0:T(8,128)S(1)}, f32[8,16,2048]{2,1,0:T(8,128)S(1)}, f32[8,16,2048]{2,1,0:T(8,128)S(1)}) fusion(f32[2,16,2048]{2,1,0:T(8,128)} %get-tuple-element.124, f32[2,16,2048]{2,1,0:T(8,128)} %get-tuple-element.123, f32[2,16,2048]{2,1,0:T(8,128)S(1)} %add_divide_fusion.1, f32[8,16,2048]{2,1,0:T(8,128)S(1)} %bitcast.392, ...), kind=kLoop, calls=%fused_computation.55 | loop fusion | flops 12845056 | bytes 6160960 | tf_op jit(solution)/shard_map/reduce_sum | solution.py:141
  210.5 12.1 %all-to-all-done.2 = f32[8,1,24576]{2,1,0:T(1,128)S(1)} async-done(((f32[8,1,24576]{2,1,0:T(1,128)}), f32[8,1,24576]{2,1,0:T(1,128)S(1)}, u32[]{:S(2)}, u32[]{:S(2)}) %all-to-all-start.2) | async-done | bytes 786464 | tf_op jit(solution)/shard_map/all_to_all | solution.py:35
  229.9 10.8 %all_to_all.37 = f32[8,1,16384]{2,1,0:T(1,128)S(1)} all-to-all(f32[8,1,16384]{2,1,0:T(1,128)S(1)} %reshape.929), channel_id=1, replica_groups=mesh['bl_0'=4,'bl_1'=2,'freq_0'=4,'freq_1'=2,'freq_2'=2] {'bl_0','bl_1'}, dimensions={0} | all-to-all | bytes 1048576 | tf_op jit(solution)/shard_map/all_to_all | solution.py:41
  250.8 8.9 %fusion.94 = (f32[2,16,2048]{2,1,0:T(8,128)S(1)}, f32[2,16,2048]{2,1,0:T(8,128)S(1)}) fusion(f32[8,16,2048]{2,1,0:T(8,128)S(1)} %bitcast.387, f32[8,16,2048]{2,1,0:T(8,128)S(1)} %bitcast.385, f32[16]{0:T(128)S(1)} %copy-done.32, f32[8,2,2048]{2,1,0:T(2,128)S(1)} %add_multiply_fusion, f32[8,16]{1,0:T(8,128)S(1)} %copy-done.31), kind=kLoop, calls=%fused_computation.107 | loop fusion | flops 5636096 | bytes 2753088 | tf_op jit(solution)/shard_map/reduce_sum | solution.py:113
  261.8 7.2 %psum.185 = f32[]{:T(128)} all-reduce(f32[]{:T(128)} %get-tuple-element.64), channel_id=1, replica_groups=mesh['bl_0'=4,'bl_1'=2,'freq_0'=4,'freq_1'=2,'freq_2'=2] {'bl_0'}, use_global_device_ids=true, to_apply=%region_33.0 | all-reduce | flops 1 | bytes 8 | tf_op jit(solution)/shard_map/psum | solution.py:23
  273.4 8.3 %psum.187 = f32[]{:T(128)} all-reduce(f32[]{:T(128)} %psum.186), channel_id=1, replica_groups=mesh['bl_0'=4,'bl_1'=2,'freq_0'=4,'freq_1'=2,'freq_2'=2] {'freq_0'}, use_global_device_ids=true, to_apply=%region_35.0 | all-reduce | flops 1 | bytes 8 | tf_op jit(solution)/shard_map/psum | solution.py:23
  289.4 12.0 %psum.189 = f32[]{:T(128)} all-reduce(f32[]{:T(128)} %psum.188), channel_id=1, replica_groups=mesh['bl_0'=4,'bl_1'=2,'freq_0'=4,'freq_1'=2,'freq_2'=2] {'freq_2'}, use_global_device_ids=true, to_apply=%region_37.0 | all-reduce | flops 1 | bytes 8 | tf_op jit(solution)/shard_map/psum | solution.py:23
  303.0 10.9 %fusion.53 = (f32[8,16,2048]{2,1,0:T(8,128)S(1)}, f32[8,16,2048]{2,1,0:T(8,128)S(1)}, f32[8,16,2048]{2,1,0:T(8,128)S(1)}) fusion(f32[2,16,2048]{2,1,0:T(8,128)} %get-tuple-element.122, f32[2,16,2048]{2,1,0:T(8,128)} %get-tuple-element.121, f32[2,16,2048]{2,1,0:T(8,128)S(1)} %add_divide_fusion, f32[8,16,2048]{2,1,0:T(8,128)S(1)} %bitcast.388, ...), kind=kLoop, calls=%fused_computation.63 | loop fusion | flops 12845056 | bytes 6160960 | tf_op jit(solution)/shard_map/reduce_sum | solution.py:141
  331.1 12.1 %all-to-all-done.4 = f32[8,1,24576]{2,1,0:T(1,128)S(1)} async-done(((f32[8,1,24576]{2,1,0:T(1,128)}), f32[8,1,24576]{2,1,0:T(1,128)S(1)}, u32[]{:S(2)}, u32[]{:S(2)}) %all-to-all-start.4) | async-done | bytes 786464 | tf_op jit(solution)/shard_map/all_to_all | solution.py:35
  355.1 8.3 %all-to-all-done.5 = f32[8,1,16384]{2,1,0:T(1,128)S(1)} async-done(((f32[8,1,16384]{2,1,0:T(1,128)}), f32[8,1,16384]{2,1,0:T(1,128)S(1)}, u32[]{:S(2)}, u32[]{:S(2)}) %all-to-all-start.5) | async-done | bytes 524320 | tf_op jit(solution)/shard_map/all_to_all | solution.py:41
  376.6 6.8 %all-to-all-start.6 = ((f32[16,1,24585]{2,1,0:T(1,128)}), f32[16,1,24585]{2,1,0:T(1,128)S(1)}, u32[]{:S(2)}, u32[]{:S(2)}) async-start(f32[16,1,24585]{2,1,0:T(1,128)} %broadcast_in_dim.11), calls=%async_computation.6 | async-start | bytes 3162112 | tf_op jit(solution)/shard_map/all_to_all | solution.py:41
  386.0 8.9 %fusion.58 = (f32[2,16,2048]{2,1,0:T(8,128)S(1)}, f32[2,16,2048]{2,1,0:T(8,128)S(1)}) fusion(f32[8,16,2048]{2,1,0:T(8,128)S(1)} %bitcast.400, f32[8,16,2048]{2,1,0:T(8,128)S(1)} %bitcast.399, f32[16]{0:T(128)S(1)} %copy-done.32, f32[8,2,2048]{2,1,0:T(2,128)S(1)} %add_multiply_fusion, f32[8,16]{1,0:T(8,128)S(1)} %copy-done.31), kind=kLoop, calls=%fused_computation.68 | loop fusion | flops 5636096 | bytes 2753088 | tf_op jit(solution)/shard_map/reduce_sum | solution.py:113
  395.9 10.3 %all-to-all-done.6 = f32[16,1,24585]{2,1,0:T(1,128)S(1)} async-done(((f32[16,1,24585]{2,1,0:T(1,128)}), f32[16,1,24585]{2,1,0:T(1,128)S(1)}, u32[]{:S(2)}, u32[]{:S(2)}) %all-to-all-start.6) | async-done | bytes 1573472 | tf_op jit(solution)/shard_map/all_to_all | solution.py:41
  (209 shorter events, 176.9 us)
Async XLA Ops:
  0.6 92.7 %copy-start = (f32[2,3,8,512]{3,2,1,0:T(8,128)S(1)}, f32[2,3,8,512]{3,2,1,0:T(8,128)}, u32[]{:S(2)}) copy-start(f32[2,3,8,512]{3,2,1,0:T(8,128)} %param.20) | copy-start | bytes 294916
  10.7 9.2 %copy-start.2 = (f32[2,2,16,2048]{3,2,1,0:T(8,128)S(1)}, f32[2,2,16,2048]{3,2,1,0:T(8,128)}, u32[]{:S(2)}) copy-start(f32[2,2,16,2048]{3,2,1,0:T(8,128)} %param.11) | copy-start | bytes 1572868
  10.9 9.8 %copy-start.3 = (s32[2,16,2048]{2,1,0:T(8,128)S(1)}, s32[2,16,2048]{2,1,0:T(8,128)}, u32[]{:S(2)}) copy-start(s32[2,16,2048]{2,1,0:T(8,128)} %param.12) | copy-start | bytes 786436
  65.2 10.9 %copy-start.12 = (f32[128,2048]{1,0:T(8,128)S(1)}, f32[128,2048]{1,0:T(8,128)}, u32[]{:S(2)}) copy-start(f32[128,2048]{1,0:T(8,128)} %get-tuple-element.109) | copy-start | bytes 3145732
  65.2 10.9 %copy-start.13 = (f32[128,2048]{1,0:T(8,128)S(1)}, f32[128,2048]{1,0:T(8,128)}, u32[]{:S(2)}) copy-start(f32[128,2048]{1,0:T(8,128)} %get-tuple-element.110) | copy-start | bytes 3145732
  65.3 10.9 %copy-start.14 = (f32[128,2048]{1,0:T(8,128)S(1)}, f32[128,2048]{1,0:T(8,128)}, u32[]{:S(2)}) copy-start(f32[128,2048]{1,0:T(8,128)} %get-tuple-element.111) | copy-start | bytes 3145732
  65.3 10.9 %copy-start.15 = (f32[128,2048]{1,0:T(8,128)S(1)}, f32[128,2048]{1,0:T(8,128)}, u32[]{:S(2)}) copy-start(f32[128,2048]{1,0:T(8,128)} %get-tuple-element.112) | copy-start | bytes 3145732
  86.3 7.8 %copy-start.30 = (f32[2,8,16,512]{3,2,1,0:T(8,128)S(1)}, f32[2,8,16,512]{3,2,1,0:T(8,128)}, u32[]{:S(2)}) copy-start(f32[2,8,16,512]{3,2,1,0:T(8,128)} %param.18) | copy-start | bytes 1572868
  89.5 16.1 %all-to-all-start = ((f32[8,1,24576]{2,1,0:T(1,128)}), f32[8,1,24576]{2,1,0:T(1,128)S(1)}, u32[]{:S(2)}, u32[]{:S(2)}) async-start(f32[8,1,24576]{2,1,0:T(1,128)} %reshape.923), calls=%async_computation | async-start | bytes 1572864 | tf_op jit(solution)/shard_map/all_to_all | solution.py:35
  182.4 11.0 %copy-start.20 = (f32[128,2048]{1,0:T(8,128)S(1)}, f32[128,2048]{1,0:T(8,128)}, u32[]{:S(2)}) copy-start(f32[128,2048]{1,0:T(8,128)} %get-tuple-element.101) | copy-start | bytes 3145732
  182.4 11.0 %copy-start.21 = (f32[128,2048]{1,0:T(8,128)S(1)}, f32[128,2048]{1,0:T(8,128)}, u32[]{:S(2)}) copy-start(f32[128,2048]{1,0:T(8,128)} %get-tuple-element.102) | copy-start | bytes 3145732
  182.4 11.0 %copy-start.22 = (f32[128,2048]{1,0:T(8,128)S(1)}, f32[128,2048]{1,0:T(8,128)}, u32[]{:S(2)}) copy-start(f32[128,2048]{1,0:T(8,128)} %get-tuple-element.103) | copy-start | bytes 3145732
  182.4 11.0 %copy-start.23 = (f32[128,2048]{1,0:T(8,128)S(1)}, f32[128,2048]{1,0:T(8,128)}, u32[]{:S(2)}) copy-start(f32[128,2048]{1,0:T(8,128)} %get-tuple-element.104) | copy-start | bytes 3145732
  203.2 7.1 %copy-start.11 = (f32[1,8,16,8,64]{4,3,2,1,0:T(8,128)S(1)}, f32[1,8,16,8,64]{4,3,2,1,0:T(8,128)}, u32[]{:S(2)}) copy-start(f32[1,8,16,8,64]{4,3,2,1,0:T(8,128)} %copy-done.10) | copy-start | bytes 786436
  206.4 16.1 %all-to-all-start.2 = ((f32[8,1,24576]{2,1,0:T(1,128)}), f32[8,1,24576]{2,1,0:T(1,128)S(1)}, u32[]{:S(2)}, u32[]{:S(2)}) async-start(f32[8,1,24576]{2,1,0:T(1,128)} %reshape.927), calls=%async_computation.2 | async-start | bytes 1572864 | tf_op jit(solution)/shard_map/all_to_all | solution.py:35
  303.0 11.0 %copy-start.16 = (f32[128,2048]{1,0:T(8,128)S(1)}, f32[128,2048]{1,0:T(8,128)}, u32[]{:S(2)}) copy-start(f32[128,2048]{1,0:T(8,128)} %get-tuple-element.93) | copy-start | bytes 3145732
  303.0 11.0 %copy-start.17 = (f32[128,2048]{1,0:T(8,128)S(1)}, f32[128,2048]{1,0:T(8,128)}, u32[]{:S(2)}) copy-start(f32[128,2048]{1,0:T(8,128)} %get-tuple-element.94) | copy-start | bytes 3145732
  303.0 11.0 %copy-start.18 = (f32[128,2048]{1,0:T(8,128)S(1)}, f32[128,2048]{1,0:T(8,128)}, u32[]{:S(2)}) copy-start(f32[128,2048]{1,0:T(8,128)} %get-tuple-element.95) | copy-start | bytes 3145732
  303.0 11.0 %copy-start.19 = (f32[128,2048]{1,0:T(8,128)S(1)}, f32[128,2048]{1,0:T(8,128)}, u32[]{:S(2)}) copy-start(f32[128,2048]{1,0:T(8,128)} %get-tuple-element.96) | copy-start | bytes 3145732
  323.8 7.1 %copy-start.9 = (f32[1,8,16,8,64]{4,3,2,1,0:T(8,128)S(1)}, f32[1,8,16,8,64]{4,3,2,1,0:T(8,128)}, u32[]{:S(2)}) copy-start(f32[1,8,16,8,64]{4,3,2,1,0:T(8,128)} %copy-done.8) | copy-start | bytes 786436
  327.1 16.1 %all-to-all-start.4 = ((f32[8,1,24576]{2,1,0:T(1,128)}), f32[8,1,24576]{2,1,0:T(1,128)S(1)}, u32[]{:S(2)}, u32[]{:S(2)}) async-start(f32[8,1,24576]{2,1,0:T(1,128)} %reshape.931), calls=%async_computation.4 | async-start | bytes 1572864 | tf_op jit(solution)/shard_map/all_to_all | solution.py:35
  351.3 12.1 %all-to-all-start.5 = ((f32[8,1,16384]{2,1,0:T(1,128)}), f32[8,1,16384]{2,1,0:T(1,128)S(1)}, u32[]{:S(2)}, u32[]{:S(2)}) async-start(f32[8,1,16384]{2,1,0:T(1,128)} %reshape.933), calls=%async_computation.5 | async-start | bytes 1048576 | tf_op jit(solution)/shard_map/all_to_all | solution.py:41
  376.6 29.6 %all-to-all-start.6 = ((f32[16,1,24585]{2,1,0:T(1,128)}), f32[16,1,24585]{2,1,0:T(1,128)S(1)}, u32[]{:S(2)}, u32[]{:S(2)}) async-start(f32[16,1,24585]{2,1,0:T(1,128)} %broadcast_in_dim.11), calls=%async_computation.6 | async-start | bytes 3162112 | tf_op jit(solution)/shard_map/all_to_all | solution.py:41
  395.0 21.3 %copy-start.1 = (f32[2,3,8,512]{3,2,1,0:T(8,128)S(1)}, f32[2,3,8,512]{3,2,1,0:T(8,128)}, u32[]{:S(2)}) copy-start(f32[2,3,8,512]{3,2,1,0:T(8,128)} %param.20) | copy-start | bytes 294916
  (15 other events, 52.5 us)
where the time goes:
time: 424 us; the launch traced here: 417 us
  blocking collectives  136 us (32%)
  other arithmetic  122 us (29%)
  waiting for transfers between devices  53.4 us (13%)
  matrix products  41.8 us (10%)
  local copies, waits for them, and re-layouts  36.2 us (9%)
  starting transfers between devices  21.5 us (5%)
  between operations  5.82 us (1%)
    psum x15, blocking collectives, by_axis(): array = lax.psum(array, axis)  114 us
    reduce_sum x4, other arithmetic, residual_of(): jnp.sum(model_re, axis=0)  35.8 us
    all_to_all x3, waiting for transfers between devices, sent_and_summed(): lax.all_to_all(pieces, axis, split_axis=0, concat_axis=0, tiled=True)  34.7 us
    reduce_sum x3, other arithmetic, normal_terms(): summed_re = jnp.sum(weight_wide * cross_re, axis=1)  32.7 us
    all_to_all x2, blocking collectives, copy_for_each(): lax.all_to_all(jnp.broadcast_to(array[None], (count, *array.shape)), axis...  21.5 us
    dot_general x8, matrix products, pick_stations(): jnp.dot(flat, table, precision=lax.Precision.HIGHEST, preferred_element_t...  20.6 us
    unnamed x83, local copies, waits for them, and re-layouts  20.3 us
    all_to_all x2, waiting for transfers between devices, copy_for_each(): lax.all_to_all(jnp.broadcast_to(array[None], (count, *array.shape)), axis...  18.6 us
  transfers between devices with their start and end apart: 5, of which 5 were waited for; matrix products, arithmetic and copies ran while one was open for 4% of the time, Pallas kernels for 0%

commit v1 on v0

v1 whole, which is shorter than its diff:
```python
import functools

import jax
import jax.numpy as jnp
from jax import lax
from jax.experimental import pallas as pl
from jax.experimental.pallas import tpu as pltpu
from jax.sharding import Mesh
from jax.sharding import PartitionSpec as P

NPOLY = 3
ITERS = 3
BL = ("bl_0", "bl_1")
FREQ = ("freq_0", "freq_1", "freq_2")
ALL = BL + FREQ

STATIONS = 512
DIRS = 8
TIMES = 2
BASELINES = 16384
PARTS = 8
FEW = 2
LOCAL = BASELINES // PARTS
SUB = 256

robust_dof = 2.0
small_term = 1e-06

SIN_TERMS = (
    3.1415926401307086,
    -5.167710083507905,
    2.5500775232148403,
    -0.5982912856219295,
    0.07765766030867731,
)
COS_TERMS = (
    0.9999999997799046,
    -4.934802137078821,
    4.058709159556128,
    -1.3352120030477381,
    0.23493731380150681,
    -0.024396324323359975,
)

F32 = jnp.float32
BF16 = jnp.bfloat16


def horner(terms, w):
    value = jnp.full_like(w, terms[-1])
    for term in terms[-2::-1]:
        value = value * w + term
    return value


def turn_parts(turns):
    f = turns - jnp.floor(turns + 0.5)
    w = f * f
    half_sin = f * horner(SIN_TERMS, w)
    half_cos = horner(COS_TERMS, w)
    twice = half_sin + half_sin
    return 1.0 - twice * half_sin, twice * half_cos


def two_parts(value):
    high = value.astype(BF16)
    low = (value - high.astype(F32)).astype(BF16)
    return high, low


def wide_kernel(
    gains_ref,
    vis_ref,
    flag_ref,
    pair_ref,
    coord_ref,
    dirs_ref,
    flux_ref,
    ratio_ref,
    *rest,
    residual_out,
    channels,
    block,
):
    outs, (high_ref, low_ref, left_ref, right_ref) = rest[:-4], rest[-4:]
    step = pl.program_id(0)

    @pl.when(step == 0)
    def _():
        high, low = two_parts(gains_ref[...])
        high_ref[...] = high
        low_ref[...] = low

    stations = lax.broadcasted_iota(jnp.int32, (STATIONS, block), 0)
    for row, target in ((0, left_ref), (1, right_ref)):
        hot = (stations == pair_ref[row : row + 1, :]).astype(F32).astype(BF16)
        target[...] = jnp.dot(high_ref[...], hot, preferred_element_type=F32) + jnp.dot(
            low_ref[...], hot, preferred_element_type=F32
        )
    ratio = ratio_ref[:, :1]
    total = [[None, None] for _ in range(TIMES)]
    for k in range(DIRS):
        re = pl.ds(k * channels, channels)
        im = pl.ds((DIRS + k) * channels, channels)
        left_re, left_im = left_ref[re, :], left_ref[im, :]
        right_re, right_im = right_ref[re, :], right_ref[im, :]
        flux = flux_ref[re, :1]
        pair_re = (left_re * right_re + left_im * right_im) * flux
        pair_im = (left_im * right_re - left_re * right_im) * flux
        for t in range(TIMES):
            project = (
                dirs_ref[0, k] * coord_ref[t : t + 1, :]
                + dirs_ref[1, k] * coord_ref[TIMES + t : TIMES + t + 1, :]
            )
            sky_re, sky_im = turn_parts(project * ratio)
            model_re = pair_re * sky_re - pair_im * sky_im
            model_im = pair_re * sky_im + pair_im * sky_re
            if k == 0:
                total[t] = [model_re, model_im]
            else:
                total[t] = [total[t][0] + model_re, total[t][1] + model_im]
    if residual_out:
        (residual_ref,) = outs
        for t in range(TIMES):
            residual_ref[0, t] = vis_ref[0, t] - total[t][0]
            residual_ref[1, t] = vis_ref[1, t] - total[t][1]
    else:
        (sums_ref,) = outs
        misfit = jnp.zeros((8, 128), F32)
        count = jnp.zeros((8, 128), F32)
        for t in range(TIMES):
            error_re = vis_ref[0, t] - total[t][0]
            error_im = vis_ref[1, t] - total[t][1]
            flagged = flag_ref[t].astype(F32)
            part = flagged * (error_re * error_re + error_im * error_im)
            for r in range(0, channels, 8):
                for c in range(0, block, 128):
                    misfit += part[r : r + 8, c : c + 128]
                    count += flagged[r : r + 8, c : c + 128]
        sums = jnp.concatenate(
            [jnp.sum(misfit, axis=0, keepdims=True), jnp.sum(count, axis=0, keepdims=True)], axis=1
        )

        @pl.when(step == 0)
        def _():
            sums_ref[...] = sums

        @pl.when(step > 0)
        def _():
            sums_ref[...] += sums


def wide_model(gains, vis, flags, pairs, coords, directions, flux, ratio, residual_out):
    channels = vis.shape[2]
    count = vis.shape[3]
    block = SUB
    rows = 2 * DIRS * channels
    whole = lambda shape: pl.BlockSpec(shape, lambda i: (0,) * len(shape))
    vis_spec = pl.BlockSpec((2, TIMES, channels, block), lambda i: (0, 0, 0, i))
    if residual_out:
        out_shape = jax.ShapeDtypeStruct(vis.shape, F32)
        out_spec = vis_spec
    else:
        out_shape = jax.ShapeDtypeStruct((1, 256), F32)
        out_spec = whole((1, 256))
    return pl.pallas_call(
        functools.partial(
            wide_kernel, residual_out=residual_out, channels=channels, block=block
        ),
        grid=(count // block,),
        in_specs=[
            whole((rows, STATIONS)),
            vis_spec,
            pl.BlockSpec((TIMES, channels, block), lambda i: (0, 0, i)),
            pl.BlockSpec((2, block), lambda i: (0, i)),
            pl.BlockSpec((2 * TIMES, block), lambda i: (0, i)),
            pl.BlockSpec(memory_space=pltpu.SMEM),
            whole((DIRS * channels, 1)),
            whole((channels, 1)),
        ],
        out_specs=out_spec,
        out_shape=out_shape,
        scratch_shapes=[
            pltpu.VMEM((rows, STATIONS), BF16),
            pltpu.VMEM((rows, STATIONS), BF16),
            pltpu.VMEM((rows, block), F32),
            pltpu.VMEM((rows, block), F32),
        ],
        name="wide_residual" if residual_out else "wide_misfit",
    )(gains, vis, flags, pairs, coords, directions, flux.reshape(-1, 1), ratio.reshape(-1, 1))


def swap_sum(rows):
    place = lax.broadcasted_iota(jnp.int32, rows[0].shape, 0)
    for bit in (4, 2, 1):
        mine = (place & bit) == 0
        merged = []
        for i in range(len(rows) // 2):
            a, b = rows[i], rows[i + len(rows) // 2]
            low = a + pltpu.roll(a, 8 - bit, axis=0)
            high = b + pltpu.roll(b, bit, axis=0)
            merged.append(jnp.where(mine, low, high))
        rows = merged
    return rows[0]


def model_block(data_ref, table_ref, sky_in, geo, outs, at, misfit):
    left_out, right_out, error_out, sky_out = outs
    lanes = pl.ds(at, SUB)
    place = lax.broadcasted_iota(jnp.int32, (128, SUB), 0)
    picked = []
    for row in (16, 17):
        station = data_ref[0, row : row + 1, lanes].astype(jnp.int32)
        hot = (place == (station & 127)).astype(F32).astype(BF16)
        got = jnp.dot(
            table_ref[...], jnp.concatenate([hot, hot], axis=0), preferred_element_type=F32
        )
        quarter = jnp.broadcast_to(station >> 7, (32, SUB))
        picked.append(
            jnp.where(
                quarter < 2,
                jnp.where(quarter == 0, got[0:32], got[32:64]),
                jnp.where(quarter == 2, got[64:96], got[96:128]),
            )
        )
    left, right = picked
    left_out[0, :, lanes] = left
    right_out[0, :, lanes] = right
    pieces = [None] * 8
    for f in range(FEW):
        lr, li = left[16 * f : 16 * f + 8], left[16 * f + 8 : 16 * f + 16]
        rr, ri = right[16 * f : 16 * f + 8], right[16 * f + 8 : 16 * f + 16]
        pair_re = lr * rr + li * ri
        pair_im = li * rr - lr * ri
        for t in range(TIMES):
            if sky_in is None:
                dirs, flux, ratio = geo
                project = dirs[0] * data_ref[0, 12 + t : 13 + t, lanes] + dirs[1] * data_ref[
                    0, 14 + t : 15 + t, lanes
                ]
                sky_re, sky_im = turn_parts(project * ratio[f])
                sky_re = sky_re * flux[f]
                sky_im = sky_im * flux[f]
                sky_out[0, t, f, 0, :, lanes] = sky_re
                sky_out[0, t, f, 1, :, lanes] = sky_im
            else:
                sky_re = sky_in[0, t, f, 0, :, lanes]
                sky_im = sky_in[0, t, f, 1, :, lanes]
            pieces[2 * t + f] = pair_re * sky_re - pair_im * sky_im
            pieces[4 + 2 * t + f] = pair_re * sky_im + pair_im * sky_re
    error = data_ref[0, 0:8, lanes] - swap_sum(pieces)
    error_out[0, :, lanes] = error
    flagged = data_ref[0, 8:12, lanes]
    part = jnp.concatenate([flagged, flagged], axis=0) * (error * error)
    return misfit + part


def build_table(table_ref, gains):
    high, low = two_parts(gains)
    for q in range(4):
        table_ref[32 * q : 32 * q + 32, 0:128] = high[:, 128 * q : 128 * q + 128]
        table_ref[32 * q : 32 * q + 32, 128:256] = low[:, 128 * q : 128 * q + 128]


def first_kernel(
    data_ref, gains_ref, geo_ref, left_out, right_out, error_out, sky_out, table_ref
):
    @pl.when(pl.program_id(0) == 0)
    def _():
        build_table(table_ref, gains_ref[...])

    col = lambda i: geo_ref[:, i : i + 1]
    geo = ((col(0), col(1)), (col(2), col(3)), (col(4), col(5)))

    def run(i, carry):
        at = pl.multiple_of(i * SUB, SUB)
        model_block(
            data_ref, table_ref, None, geo, (left_out, right_out, error_out, sky_out), at,
            jnp.zeros((8, SUB), F32),
        )
        return carry

    lax.fori_loop(0, LOCAL // SUB, run, 0)


def normal_block(data_ref, left_ref, right_ref, error_ref, sky_ref, total_ref, at, inverse):
    lanes = pl.ds(at, SUB)
    error = error_ref[0, :, lanes]
    square = error * error
    square = square + pltpu.roll(square, 4, axis=0)
    flagged = data_ref[0, 8:12, lanes]
    flagged = jnp.concatenate([flagged, flagged], axis=0)
    weight = flagged * (robust_dof + 1.0) / (robust_dof + square * inverse)
    scaled = weight * error
    left = left_ref[0, :, lanes]
    right = right_ref[0, :, lanes]
    first, second = [], []
    wide = lambda row: jnp.broadcast_to(row, (DIRS, SUB))
    for f in range(FEW):
        z_re, z_im = None, None
        for t in range(TIMES):
            i = 2 * t + f
            y_re, y_im = wide(scaled[i : i + 1]), wide(scaled[4 + i : 5 + i])
            sky_re = sky_ref[0, t, f, 0, :, lanes]
            sky_im = sky_ref[0, t, f, 1, :, lanes]
            a = sky_re * y_re + sky_im * y_im
            b = sky_re * y_im - sky_im * y_re
            z_re, z_im = (a, b) if t == 0 else (z_re + a, z_im + b)
        power = wide(weight[f : f + 1] + weight[2 + f : 3 + f])
        lr, li = left[16 * f : 16 * f + 8], left[16 * f + 8 : 16 * f + 16]
        rr, ri = right[16 * f : 16 * f + 8], right[16 * f + 8 : 16 * f + 16]
        first += [rr * z_re - ri * z_im, rr * z_im + ri * z_re, (rr * rr + ri * ri) * power]
        second += [lr * z_re + li * z_im, li * z_re - lr * z_im, (lr * lr + li * li) * power]
    place = lax.broadcasted_iota(jnp.int32, (256, SUB), 0)
    total = None
    for row, pieces in ((16, first), (17, second)):
        station = data_ref[0, row : row + 1, lanes].astype(jnp.int32)
        hot = (place == (station & 255)).astype(F32).astype(BF16)
        values = jnp.concatenate(pieces, axis=0)
        upper = jnp.broadcast_to(station, (48, SUB)) >= 256
        parts = []
        for half in (jnp.where(upper, 0.0, values), jnp.where(upper, values, 0.0)):
            parts += list(two_parts(half))
        got = lax.dot_general(
            jnp.concatenate(parts, axis=0),
            hot,
            (((1,), (1,)), ((), ())),
            preferred_element_type=F32,
        )
        total = got if total is None else total + got
    total_ref[...] += total


def renew_gains(gains, anchor, total, columns):
    halves = [total[0:48] + total[48:96], total[96:144] + total[144:192]]
    sums = jnp.concatenate(halves, axis=1)
    rows = []
    for f in range(FEW):
        flux = columns[:, 2 + f : 3 + f]
        rho = columns[:, 6:7]
        norm = sums[24 * f + 16 : 24 * f + 24] * (flux * flux)
        divisor = norm + rho
        for c in range(2):
            g = gains[16 * f + 8 * c : 16 * f + 8 * c + 8]
            a = anchor[16 * f + 8 * c : 16 * f + 8 * c + 8]
            n = sums[24 * f + 8 * c : 24 * f + 8 * c + 8] + g * norm
            rows.append(0.5 * (g + (n + rho * a) / divisor))
    return jnp.concatenate(rows, axis=0)


def middle_kernel(
    sigma_ref,
    data_ref,
    left_ref,
    right_ref,
    error_ref,
    sky_ref,
    gains_ref,
    anchor_ref,
    geo_ref,
    gains_out,
    left_out,
    right_out,
    error_out,
    misfit_out,
    table_ref,
    total_ref,
):
    phase, step = pl.program_id(0), pl.program_id(1)
    last = pl.num_programs(1) - 1

    @pl.when((phase == 0) & (step == 0))
    def _():
        total_ref[...] = jnp.zeros_like(total_ref)

    @pl.when(phase == 0)
    def _():
        inverse = sigma_ref[0, 0]

        def run(i, carry):
            at = pl.multiple_of(i * SUB, SUB)
            normal_block(
                data_ref, left_ref, right_ref, error_ref, sky_ref, total_ref, at, inverse
            )
            return carry

        lax.fori_loop(0, LOCAL // SUB, run, 0)

    @pl.when((phase == 0) & (step == last))
    def _():
        gains = renew_gains(gains_ref[...], anchor_ref[...], total_ref[...], geo_ref[...])
        gains_out[...] = gains
        build_table(table_ref, gains)

    @pl.when(phase == 1)
    def _():
        def run(i, misfit):
            at = pl.multiple_of(i * SUB, SUB)
            return model_block(
                data_ref, table_ref, sky_ref, None, (left_out, right_out, error_out, None), at,
                misfit,
            )

        misfit = lax.fori_loop(0, LOCAL // SUB, run, jnp.zeros((8, SUB), F32))
        misfit = jnp.sum(misfit[:, :128] + misfit[:, 128:], axis=0, keepdims=True)

        @pl.when(step == 0)
        def _():
            misfit_out[...] = misfit

        @pl.when(step > 0)
        def _():
            misfit_out[...] += misfit


def last_kernel(
    sigma_ref,
    data_ref,
    left_ref,
    right_ref,
    error_ref,
    sky_ref,
    gains_ref,
    anchor_ref,
    geo_ref,
    gains_out,
    total_ref,
):
    step = pl.program_id(0)

    @pl.when(step == 0)
    def _():
        total_ref[...] = jnp.zeros_like(total_ref)

    inverse = sigma_ref[0, 0]

    def run(i, carry):
        at = pl.multiple_of(i * SUB, SUB)
        normal_block(data_ref, left_ref, right_ref, error_ref, sky_ref, total_ref, at, inverse)
        return carry

    lax.fori_loop(0, LOCAL // SUB, run, 0)

    @pl.when(step == pl.num_programs(0) - 1)
    def _():
        gains_out[...] = renew_gains(
            gains_ref[...], anchor_ref[...], total_ref[...], geo_ref[...]
        )


ROWS = 18
GAIN_ROWS = 2 * FEW * DIRS
SKY = (TIMES, FEW, 2, DIRS)


def shapes_of(rows):
    return jax.ShapeDtypeStruct((PARTS, rows, LOCAL), F32)


def first_call(data, gains, geo):
    at = lambda i: (i, 0, 0)
    return pl.pallas_call(
        first_kernel,
        grid=(PARTS,),
        in_specs=[
            pl.BlockSpec((1, ROWS, LOCAL), at),
            pl.BlockSpec((GAIN_ROWS, STATIONS), lambda i: (0, 0)),
            pl.BlockSpec((DIRS, 8), lambda i: (0, 0)),
        ],
        out_specs=[
            pl.BlockSpec((1, GAIN_ROWS, LOCAL), at),
            pl.BlockSpec((1, GAIN_ROWS, LOCAL), at),
            pl.BlockSpec((1, 8, LOCAL), at),
            pl.BlockSpec((1,) + SKY + (LOCAL,), lambda i: (i, 0, 0, 0, 0, 0)),
        ],
        out_shape=[
            shapes_of(GAIN_ROWS),
            shapes_of(GAIN_ROWS),
            shapes_of(8),
            jax.ShapeDtypeStruct((PARTS,) + SKY + (LOCAL,), F32),
        ],
        scratch_shapes=[pltpu.VMEM((128, 256), BF16)],
        name="first_model",
    )(data, gains, geo)


def middle_call(sigma, data, left, right, error, sky, gains, anchor, geo):
    at = lambda p, i: (i, 0, 0)
    held = lambda p, i: ((1 - p) * i + p * (PARTS - 1), 0, 0)
    made = lambda p, i: (p * i, 0, 0)
    small = lambda p, i: (0, 0)
    return pl.pallas_call(
        middle_kernel,
        grid=(2, PARTS),
        in_specs=[
            pl.BlockSpec(memory_space=pltpu.SMEM),
            pl.BlockSpec((1, ROWS, LOCAL), at),
            pl.BlockSpec((1, GAIN_ROWS, LOCAL), held),
            pl.BlockSpec((1, GAIN_ROWS, LOCAL), held),
            pl.BlockSpec((1, 8, LOCAL), held),
            pl.BlockSpec((1,) + SKY + (LOCAL,), lambda p, i: (i, 0, 0, 0, 0, 0)),
            pl.BlockSpec((GAIN_ROWS, STATIONS), small),
            pl.BlockSpec((GAIN_ROWS, STATIONS), small),
            pl.BlockSpec((DIRS, 8), small),
        ],
        out_specs=[
            pl.BlockSpec((GAIN_ROWS, STATIONS), small),
            pl.BlockSpec((1, GAIN_ROWS, LOCAL), made),
            pl.BlockSpec((1, GAIN_ROWS, LOCAL), made),
            pl.BlockSpec((1, 8, LOCAL), made),
            pl.BlockSpec((1, 128), small),
        ],
        out_shape=[
            jax.ShapeDtypeStruct((GAIN_ROWS, STATIONS), F32),
            shapes_of(GAIN_ROWS),
            shapes_of(GAIN_ROWS),
            shapes_of(8),
            jax.ShapeDtypeStruct((1, 128), F32),
        ],
        scratch_shapes=[pltpu.VMEM((128, 256), BF16), pltpu.VMEM((192, 256), F32)],
        name="normal_and_model",
    )(sigma, data, left, right, error, sky, gains, anchor, geo)


def last_call(sigma, data, left, right, error, sky, gains, anchor, geo):
    at = lambda i: (i, 0, 0)
    small = lambda i: (0, 0)
    return pl.pallas_call(
        last_kernel,
        grid=(PARTS,),
        in_specs=[
            pl.BlockSpec(memory_space=pltpu.SMEM),
            pl.BlockSpec((1, ROWS, LOCAL), at),
            pl.BlockSpec((1, GAIN_ROWS, LOCAL), at),
            pl.BlockSpec((1, GAIN_ROWS, LOCAL), at),
            pl.BlockSpec((1, 8, LOCAL), at),
            pl.BlockSpec((1,) + SKY + (LOCAL,), lambda i: (i, 0, 0, 0, 0, 0)),
            pl.BlockSpec((GAIN_ROWS, STATIONS), small),
            pl.BlockSpec((GAIN_ROWS, STATIONS), small),
            pl.BlockSpec((DIRS, 8), small),
        ],
        out_specs=pl.BlockSpec((GAIN_ROWS, STATIONS), small),
        out_shape=jax.ShapeDtypeStruct((GAIN_ROWS, STATIONS), F32),
        scratch_shapes=[pltpu.VMEM((192, 256), F32)],
        name="normal_last",
    )(sigma, data, left, right, error, sky, gains, anchor, geo)


def legendre(ratios):
    scaled = (ratios - 1.05) / 0.35
    values = [jnp.ones_like(scaled), scaled]
    values.append((3 * scaled * values[1] - 1 * values[0]) / 2)
    return jnp.stack(values[:NPOLY])


def sent_to_all(array, axes):
    count = lax.axis_size(axes)
    return lax.all_to_all(
        jnp.broadcast_to(array[None], (count, *array.shape)), axes, 0, 0, tiled=True
    )


def cholesky_solve(gram, rhs):
    order = len(rhs)
    factor = [[None] * order for _ in range(order)]
    for i in range(order):
        for j in range(i + 1):
            value = gram[i, j]
            for m in range(j):
                value = value - factor[i][m] * factor[j][m]
            factor[i][j] = jnp.sqrt(value) if i == j else value / factor[j][j]
    forward = []
    for i in range(order):
        running = rhs[i]
        for j in range(i):
            running = running - factor[i][j] * forward[j]
        forward.append(running / factor[i][i])
    backward = [None] * order
    for i in reversed(range(order)):
        running = forward[i]
        for j in range(i + 1, order):
            running = running - factor[j][i] * backward[j]
        backward[i] = running / factor[i][i]
    return backward


def own_channels(array, axis, own):
    return lax.dynamic_slice_in_dim(array, own * FEW, FEW, axis)


def packed(vis, flags, pairs, coords):
    vis = vis.reshape(4, PARTS, FEW, LOCAL).transpose(1, 0, 2, 3).reshape(PARTS, 8, LOCAL)
    flags = flags.astype(F32).reshape(TIMES, PARTS, FEW, LOCAL).transpose(1, 0, 2, 3)
    flags = flags.reshape(PARTS, 4, LOCAL)
    coords = jnp.broadcast_to(coords.reshape(1, 4, LOCAL), (PARTS, 4, LOCAL))
    pairs = jnp.broadcast_to(pairs.astype(F32)[None], (PARTS, 2, LOCAL))
    return jnp.concatenate([vis, flags, coords, pairs], axis=1)


def body(
    visibilities,
    sample_flag_weight,
    baseline_station_pair,
    baseline_spatial_coords,
    directions,
    source_flux,
    channel_ratio,
    jones_gains,
    scaled_dual,
    consensus,
    penalty,
):
    devices = lax.axis_size(ALL)
    own = lax.axis_index(BL)
    channels = channel_ratio.shape[0]
    rho = penalty * (2.0 * BASELINES * TIMES / STATIONS)

    send = packed(
        visibilities, sample_flag_weight, baseline_station_pair, baseline_spatial_coords
    )
    send = send.reshape(PARTS, ROWS * LOCAL // 128, 128)
    data = lax.all_to_all(send, BL, 0, 0, tiled=True).reshape(PARTS, ROWS, LOCAL)

    coords = baseline_spatial_coords.reshape(2 * TIMES, LOCAL)
    wide = functools.partial(
        wide_model,
        vis=visibilities,
        flags=sample_flag_weight,
        pairs=baseline_station_pair,
        coords=coords,
        directions=directions,
        flux=source_flux,
        ratio=channel_ratio,
    )
    sums = wide(jones_gains.reshape(-1, STATIONS), residual_out=False)

    ratio = own_channels(channel_ratio, 0, own)
    flux = own_channels(source_flux, 1, own)
    basis = legendre(ratio)
    gram_own = (basis[:, None, :] * basis[None, :, :]).sum(-1)
    payload = jnp.concatenate([sums, jnp.pad(gram_own.reshape(1, 9), ((0, 0), (0, 119)))], axis=1)
    arrived = sent_to_all(payload, ALL)
    arrived = arrived.sum(axis=0)[0]
    squares, weight_count = arrived[:128].sum(), arrived[128:256].sum()
    gram = arrived[256:265].reshape(3, 3)

    def inverse_sigma(squares):
        return (1.0 / (squares / (weight_count + 1.0) + small_term)).reshape(1, 1)

    def rows_of(array):
        part = own_channels(array, 2, own)
        return part.transpose(2, 0, 1, 3)

    dual = rows_of(scaled_dual)
    anchor = (
        sum(
            basis[j][:, None, None, None] * consensus[:, j][None] for j in range(NPOLY)
        )
        - dual
    ).reshape(GAIN_ROWS, STATIONS)
    gains = rows_of(jones_gains).reshape(GAIN_ROWS, STATIONS)
    geo = jnp.concatenate(
        [
            directions.T,
            flux,
            jnp.broadcast_to(ratio[None], (DIRS, FEW)),
            rho[:, None],
            jnp.zeros((DIRS, 1), F32),
        ],
        axis=1,
    )

    left, right, error, sky = first_call(data, gains, geo)
    sigma = inverse_sigma(squares)
    for iteration in range(ITERS - 1):
        gains, left, right, error, misfit = middle_call(
            sigma, data, left, right, error, sky, gains, anchor, geo
        )
        sigma = inverse_sigma(sent_to_all(misfit, ALL).sum())
    gains = last_call(sigma, data, left, right, error, sky, gains, anchor, geo)

    new_rows = gains.reshape(FEW, 2, DIRS, STATIONS)
    lifted = new_rows + dual
    part = 2 * DIRS * STATIONS // devices
    rhs = (basis[:, :, None] * lifted.reshape(1, FEW, -1)).sum(axis=1)
    rhs = rhs.reshape(NPOLY, devices, part).transpose(1, 0, 2)
    rhs = lax.all_to_all(rhs, ALL, 0, 0, tiled=True).sum(axis=0)
    solved = jnp.stack(cholesky_solve(gram, [rhs[j] for j in range(NPOLY)]))
    everyone = sent_to_all(solved, ALL)
    new_consensus = (
        everyone.transpose(1, 0, 2).reshape(NPOLY, 2, DIRS, STATIONS).transpose(1, 0, 2, 3)
    )

    gathered = sent_to_all(gains.reshape(GAIN_ROWS * STATIONS // 128, 128), BL)
    new_gains = (
        gathered.reshape(PARTS * FEW, 2, DIRS, STATIONS).transpose(1, 2, 0, 3)
    )
    residuals = wide(new_gains.reshape(-1, STATIONS), residual_out=True)

    all_basis = legendre(channel_ratio)
    fitted = sum(
        all_basis[j][None, None, :, None] * new_consensus[:, j][:, :, None, :]
        for j in range(NPOLY)
    )
    new_dual = scaled_dual + new_gains - fitted
    return (new_gains, new_consensus, new_dual, residuals)


def solution(mesh):
    split = Mesh(
        mesh.devices.reshape(4, 2, 4, 2, 2), ("bl_0", "bl_1", "freq_0", "freq_1", "freq_2")
    )
    in_specs = (
        P(None, None, FREQ, BL),
        P(None, FREQ, BL),
        P(None, BL),
        P(None, None, BL),
        P(),
        P(None, FREQ),
        P(FREQ),
        P(None, None, FREQ, None),
        P(None, None, FREQ, None),
        P(),
        P(),
    )
    out_specs = (P(None, None, FREQ, None), P(), P(None, None, FREQ, None), P(None, None, FREQ, BL))
    return jax.shard_map(body, mesh=split, in_specs=in_specs, out_specs=out_specs, check_vma=False)
```

time: 424 us -> 266 us (0.63); the launches traced: 417 us -> 264 us
  Pallas kernels: 0 us -> 129 us
  blocking collectives: 136 us -> 14 us
  other arithmetic: 122 us -> 7.74 us
  matrix products: 41.8 us -> 0 us
  local copies, waits for them, and re-layouts: 36.2 us -> 22.1 us
  starting transfers between devices: 21.5 us -> 31.9 us
    pallas_call x0 -> x6, Pallas kernels: none -> 129 us  [the longest x2 74.6 us: middle_call(): pl.pallas_call(middle_kernel, grid=(2, PARTS), in_specs=[pl.BlockSpec(mem...]
    psum x15 -> x0, blocking collectives: 114 us -> none  [by_axis(): array = lax.psum(array, axis)]
    reduce_sum x14 -> x7, other arithmetic: 74 us -> 2.57 us  [the longest x2 1.23 us: body(): sigma = inverse_sigma(sent_to_all(misfit, ALL).sum())]
    dot_general x18 -> x0, matrix products: 41.8 us -> none  [the longest x8 20.6 us: pick_stations(): jnp.dot(flat, table, precision=lax.Precision.HIGHEST, preferred_element_t...]
    add x11 -> x1, other arithmetic: 18.7 us -> 0.91 us  [body(): lifted = new_rows + dual]
    unnamed x83 -> x30, local copies, waits for them, and re-layouts: 20.3 us -> 5.07 us
    all_to_all x6 -> x2, other arithmetic: 15.5 us -> 1.93 us  [the longest x1 0.97 us: body(): rhs = lax.all_to_all(rhs, ALL, 0, 0, tiled=True).sum(axis=0)]
    all_to_all x5 -> x6, starting transfers between devices: 21.5 us -> 31.9 us  [the longest x4 23.8 us: sent_to_all(): lax.all_to_all(jnp.broadcast_to(array[None], (count, *array.shape)), axes...]
  transfers between devices with their start and end apart: 5 -> 6, of which waited for: 5 -> 6; matrix products, arithmetic and copies ran while one was open for 4% -> 4% of each run, Pallas kernels for 0% -> 0%
where the time goes in v1:
time: 266 us; the launch traced here: 264 us
  Pallas kernels  129 us (48%)
  waiting for transfers between devices  51.8 us (19%)
  starting transfers between devices  31.9 us (12%)
  local copies, waits for them, and re-layouts  22.1 us (8%)
  blocking collectives  14 us (5%)
  other arithmetic  7.74 us (3%)
  between operations  7.7 us (3%)
    pallas_call x2, Pallas kernels, middle_call(): pl.pallas_call(middle_kernel, grid=(2, PARTS), in_specs=[pl.BlockSpec(mem...  74.6 us
    all_to_all x4, waiting for transfers between devices, sent_to_all(): lax.all_to_all(jnp.broadcast_to(array[None], (count, *array.shape)), axes...  34.1 us
    all_to_all x4, starting transfers between devices, sent_to_all(): lax.all_to_all(jnp.broadcast_to(array[None], (count, *array.shape)), axes...  23.8 us
    pallas_call x1, Pallas kernels, last_call(): pl.pallas_call(last_kernel, grid=(PARTS,), in_specs=[pl.BlockSpec(memory_...  21.1 us
    pallas_call x1, Pallas kernels, first_call(): pl.pallas_call(first_kernel, grid=(PARTS,), in_specs=[pl.BlockSpec((1, RO...  16.7 us
    pallas_call x2, Pallas kernels, wide_model(): pl.pallas_call(functools.partial(wide_kernel, residual_out=residual_out,...  16.7 us
    all_to_all x1, blocking collectives, sent_to_all(): lax.all_to_all(jnp.broadcast_to(array[None], (count, *array.shape)), axes...  14 us
    all_to_all x1, waiting for transfers between devices, body(): lax.all_to_all(send, BL, 0, 0, tiled=True).reshape(PARTS, ROWS, LOCAL)  12.2 us
  transfers between devices with their start and end apart: 6, of which 6 were waited for; matrix products, arithmetic and copies ran while one was open for 4% of the time, Pallas kernels for 0%

profile of v1, /device:TPU:1, one launch (start us, length us, event | category | flops | bytes accessed | tf_op | source)
XLA Modules:
  0.0 264.4 jit_solution(10785899676162701922)
XLA Ops:
  1.8 1.4 reshape.113.coord_ref
  3.2 1.4 reshape.134.flux_ref
  4.6 1.3 copy.99.ratio_ref
  5.9 8.3 %wide_misfit.1 = f32[1,256]{1,0:T(1,128)} custom-call(f32[256,512]{1,0:T(8,128)} %bitcast.70, f32[2,2,16,2048]{3,2,1,0:T(8,128)} %vis_ref.3, s32[2,16,2048]{2,1,0:T(8,128)} %flag_ref.3, s32[2,2048]{1,0:T(2,128)} %pair_ref.3, f32[4,2048]{1,0:T(4,128)} %reshape.113.coord_ref, f32[2,8]{1,0:T(2,128)} %dirs_ref.3, f32[128,1]{1,0:T(8,128)} %reshape.134.flux_ref, ...), custom_call_target="tpu_custom_call" | custom-call | tf_op jit(solution)/shard_map/wide_misfit/pallas_call | solution.py:166
  15.8 11.5 %all-to-all-start = ((f32[128,1,384]{2,1,0:T(1,128)}), f32[128,1,384]{2,1,0:T(1,128)S(1)}, u32[]{:S(2)}, u32[]{:S(2)}) async-start(f32[128,1,384]{2,1,0:T(1,128)} %broadcast_in_dim.27), calls=%async_computation | async-start | bytes 393216 | tf_op jit(solution)/shard_map/all_to_all | solution.py:558
  30.5 7.4 %all-to-all-done = f32[128,1,384]{2,1,0:T(1,128)S(1)} async-done(((f32[128,1,384]{2,1,0:T(1,128)}), f32[128,1,384]{2,1,0:T(1,128)S(1)}, u32[]{:S(2)}, u32[]{:S(2)}) %all-to-all-start) | async-done | bytes 196640 | tf_op jit(solution)/shard_map/all_to_all | solution.py:558
  37.8 3.6 %all-to-all-start.1 = ((f32[8,288,128]{2,1,0:T(8,128)}), f32[8,288,128]{2,1,0:T(8,128)S(1)}, u32[]{:S(2)}, u32[]{:S(2)}) async-start(f32[8,288,128]{2,1,0:T(8,128)} %reshape.122), calls=%async_computation.1 | async-start | bytes 2359296 | tf_op jit(solution)/shard_map/all_to_all | solution.py:622
  46.9 12.2 %all-to-all-done.1 = f32[8,288,128]{2,1,0:T(8,128)S(1)} async-done(((f32[8,288,128]{2,1,0:T(8,128)}), f32[8,288,128]{2,1,0:T(8,128)S(1)}, u32[]{:S(2)}, u32[]{:S(2)}) %all-to-all-start.1) | async-done | bytes 1179680 | tf_op jit(solution)/shard_map/all_to_all | solution.py:622
  59.1 1.4 reshape.123.data_ref
  60.4 16.7 %first_model.1 = (f32[8,32,2048]{2,1,0:T(8,128)}, f32[8,32,2048]{2,1,0:T(8,128)}, f32[8,8,2048]{2,1,0:T(8,128)}, f32[8,2,2,2,8,2048]{5,4,3,2,1,0:T(8,128)}) custom-call(f32[8,18,2048]{2,1,0:T(8,128)} %reshape.123.data_ref, f32[32,512]{1,0:T(8,128)} %bitcast.72, f32[8,8]{1,0:T(8,128)} %concatenate.11.geo_ref), custom_call_target="tpu_custom_call" | custom-call | tf_op jit(solution)/shard_map/first_model/pallas_call | solution.py:462
  77.2 37.3 %normal_and_model.2 = (f32[32,512]{1,0:T(8,128)}, f32[8,32,2048]{2,1,0:T(8,128)}, f32[8,32,2048]{2,1,0:T(8,128)}, f32[8,8,2048]{2,1,0:T(8,128)}, f32[1,128]{1,0:T(1,128)}) custom-call(f32[1,1]{1,0:T(1,128)} %bitcast.4.sigma_ref, f32[8,18,2048]{2,1,0:T(8,128)} %reshape.123.data_ref, f32[8,32,2048]{2,1,0:T(8,128)} %get-tuple-element.18.left_ref, ...), custom_call_target="tpu_custom_call" | custom-call | tf_op jit(solution)/shard_map/normal_and_model/pallas_call | solution.py:492
  115.2 14.0 %all_to_all.35 = f32[128,1,128]{2,1,0:T(1,128)S(1)} all-to-all(f32[128,1,128]{2,1,0:T(1,128)S(1)} %broadcast_in_dim.33), channel_id=1, replica_groups=mesh['bl_0'=4,'bl_1'=2,'freq_0'=4,'freq_1'=2,'freq_2'=2] {'bl_0','bl_1',..., dimensions={0} | all-to-all | bytes 131072 | tf_op jit(solution)/shard_map/all_to_all | solution.py:558
  130.4 37.3 %normal_and_model.3 = (f32[32,512]{1,0:T(8,128)}, f32[8,32,2048]{2,1,0:T(8,128)}, f32[8,32,2048]{2,1,0:T(8,128)}, f32[8,8,2048]{2,1,0:T(8,128)}, f32[1,128]{1,0:T(1,128)}) custom-call(f32[1,1]{1,0:T(1,128)} %bitcast.21.sigma_ref, f32[8,18,2048]{2,1,0:T(8,128)} %reshape.123.data_ref, f32[8,32,2048]{2,1,0:T(8,128)} %get-tuple-element.23.left_ref, ...), custom_call_target="tpu_custom_call" | custom-call | tf_op jit(solution)/shard_map/normal_and_model/pallas_call | solution.py:492
  167.8 1.3 broadcast_in_dim.69
  169.1 4.3 %all-to-all-start.3 = ((f32[128,1,128]{2,1,0:T(1,128)}), f32[128,1,128]{2,1,0:T(1,128)S(1)}, u32[]{:S(2)}, u32[]{:S(2)}) async-start(f32[128,1,128]{2,1,0:T(1,128)} %broadcast_in_dim.69), calls=%async_computation.3 | async-start | bytes 131072 | tf_op jit(solution)/shard_map/all_to_all | solution.py:558
  173.5 9.6 %all-to-all-done.3 = f32[128,1,128]{2,1,0:T(1,128)S(1)} async-done(((f32[128,1,128]{2,1,0:T(1,128)}), f32[128,1,128]{2,1,0:T(1,128)S(1)}, u32[]{:S(2)}, u32[]{:S(2)}) %all-to-all-start.3) | async-done | bytes 65568 | tf_op jit(solution)/shard_map/all_to_all | solution.py:558
  184.4 21.1 %normal_last.1 = f32[32,512]{1,0:T(8,128)} custom-call(f32[1,1]{1,0:T(1,128)} %bitcast.24.sigma_ref, f32[8,18,2048]{2,1,0:T(8,128)} %reshape.123.data_ref, f32[8,32,2048]{2,1,0:T(8,128)} %get-tuple-element.28.left_ref, f32[8,32,2048]{2,1,0:T(8,128)} %get-tuple-element.29.right_ref, f32[8,8,2048]{2,1,0:T(8,128)} %get-tuple-element.30.error_ref, ...), custom_call_target="tpu_custom_call" | custom-call | tf_op jit(solution)/shard_map/normal_last/pallas_call | solution.py:528
  207.9 4.5 %all-to-all-start.5 = ((f32[128,1,192]{2,1,0:T(1,128)}), f32[128,1,192]{2,1,0:T(1,128)S(1)}, u32[]{:S(2)}, u32[]{:S(2)}) async-start(f32[128,1,192]{2,1,0:T(1,128)} %reshape.144), calls=%async_computation.5 | async-start | bytes 262144 | tf_op jit(solution)/shard_map/all_to_all | solution.py:687
  217.0 5.6 %all-to-all-done.5 = f32[128,1,192]{2,1,0:T(1,128)S(1)} async-done(((f32[128,1,192]{2,1,0:T(1,128)}), f32[128,1,192]{2,1,0:T(1,128)S(1)}, u32[]{:S(2)}, u32[]{:S(2)}) %all-to-all-start.5) | async-done | bytes 98336 | tf_op jit(solution)/shard_map/all_to_all | solution.py:687
  225.4 4.3 %all-to-all-start.6 = ((f32[128,1,192]{2,1,0:T(1,128)}), f32[128,1,192]{2,1,0:T(1,128)S(1)}, u32[]{:S(2)}, u32[]{:S(2)}) async-start(f32[128,1,192]{2,1,0:T(1,128)} %reshape.146), calls=%async_computation.6 | async-start | bytes 262144 | tf_op jit(solution)/shard_map/all_to_all | solution.py:558
  229.7 10.0 %all-to-all-done.6 = f32[128,1,192]{2,1,0:T(1,128)S(1)} async-done(((f32[128,1,192]{2,1,0:T(1,128)}), f32[128,1,192]{2,1,0:T(1,128)S(1)}, u32[]{:S(2)}, u32[]{:S(2)}) %all-to-all-start.6) | async-done | bytes 98336 | tf_op jit(solution)/shard_map/all_to_all | solution.py:558
  240.6 3.7 %all-to-all-start.4 = ((f32[8,128,128]{2,1,0:T(8,128)}), f32[8,128,128]{2,1,0:T(8,128)S(1)}, u32[]{:S(2)}, u32[]{:S(2)}) async-start(f32[8,128,128]{2,1,0:T(8,128)} %broadcast_in_dim.71), calls=%async_computation.4 | async-start | bytes 1048576 | tf_op jit(solution)/shard_map/all_to_all | solution.py:558
  246.2 7.1 %all-to-all-done.4 = f32[8,128,128]{2,1,0:T(8,128)S(1)} async-done(((f32[8,128,128]{2,1,0:T(8,128)}), f32[8,128,128]{2,1,0:T(8,128)S(1)}, u32[]{:S(2)}, u32[]{:S(2)}) %all-to-all-start.4) | async-done | bytes 524320 | tf_op jit(solution)/shard_map/all_to_all | solution.py:558
  256.0 8.4 %wide_residual.1 = f32[2,2,16,2048]{3,2,1,0:T(8,128)} custom-call(f32[256,512]{1,0:T(8,128)} %bitcast.58, f32[2,2,16,2048]{3,2,1,0:T(8,128)} %vis_ref.3, s32[2,16,2048]{2,1,0:T(8,128)} %flag_ref.3, s32[2,2048]{1,0:T(2,128)} %pair_ref.3, f32[4,2048]{1,0:T(4,128)} %reshape.113.coord_ref, f32[2,8]{1,0:T(2,128)} %dirs_ref.3, f32[128,1]{1,0:T(8,128)} %reshape.134.flux_ref, ...), custom_call_target="tpu_custom_call" | custom-call | tf_op jit(solution)/shard_map/wide_residual/pallas_call | solution.py:166
  (90 shorter events, 23.1 us)
Async XLA Ops:
  0.6 26.6 %copy-start = (f32[2,2,16,2048]{3,2,1,0:T(8,128)S(1)}, f32[2,2,16,2048]{3,2,1,0:T(8,128)}, u32[]{:S(2)}) copy-start(f32[2,2,16,2048]{3,2,1,0:T(8,128)} %vis_ref.3) | copy-start | bytes 1572868
  14.2 13.4 %copy-start.1 = (s32[2,16,2048]{2,1,0:T(8,128)S(1)}, s32[2,16,2048]{2,1,0:T(8,128)}, u32[]{:S(2)}) copy-start(s32[2,16,2048]{2,1,0:T(8,128)} %flag_ref.3) | copy-start | bytes 786436
  14.2 13.4 %copy-start.5 = (s32[2,2048]{1,0:T(2,128)S(1)}, s32[2,2048]{1,0:T(2,128)}, u32[]{:S(2)}) copy-start(s32[2,2048]{1,0:T(2,128)} %pair_ref.3) | copy-start | bytes 49156
  15.8 22.1 %all-to-all-start = ((f32[128,1,384]{2,1,0:T(1,128)}), f32[128,1,384]{2,1,0:T(1,128)S(1)}, u32[]{:S(2)}, u32[]{:S(2)}) async-start(f32[128,1,384]{2,1,0:T(1,128)} %broadcast_in_dim.27), calls=%async_computation | async-start | bytes 393216 | tf_op jit(solution)/shard_map/all_to_all | solution.py:558
  27.6 0.8 copy-start.4
  30.5 11.0 %copy-start.8 = (f32[2,8]{1,0:T(2,128)S(1)}, f32[2,8]{1,0:T(2,128)}, u32[]{:S(2)}) copy-start(f32[2,8]{1,0:T(2,128)} %dirs_ref.3) | copy-start | bytes 196
  30.5 11.0 %copy-start.10 = (f32[8]{0:T(128)S(1)}, f32[8]{0:T(128)}, u32[]{:S(2)}) copy-start(f32[8]{0:T(128)} %param.21) | copy-start | bytes 100
  30.5 12.8 %copy-start.6 = (f32[2,3,8,512]{3,2,1,0:T(8,128)S(1)}, f32[2,3,8,512]{3,2,1,0:T(8,128)}, u32[]{:S(2)}) copy-start(f32[2,3,8,512]{3,2,1,0:T(8,128)} %param.20) | copy-start | bytes 294916
  30.5 12.8 %copy-start.2 = (f32[2,8,16,512]{3,2,1,0:T(8,128)S(1)}, f32[2,8,16,512]{3,2,1,0:T(8,128)}, u32[]{:S(2)}) copy-start(f32[2,8,16,512]{3,2,1,0:T(8,128)} %param.19) | copy-start | bytes 1572868
  30.5 13.5 %copy-start.7 = (f32[8,16]{1,0:T(8,128)S(1)}, f32[8,16]{1,0:T(8,128)}, u32[]{:S(2)}) copy-start(f32[8,16]{1,0:T(8,128)} %param.16) | copy-start | bytes 1540
  37.8 21.2 %all-to-all-start.1 = ((f32[8,288,128]{2,1,0:T(8,128)}), f32[8,288,128]{2,1,0:T(8,128)S(1)}, u32[]{:S(2)}, u32[]{:S(2)}) async-start(f32[8,288,128]{2,1,0:T(8,128)} %reshape.122), calls=%async_computation.1 | async-start | bytes 2359296 | tf_op jit(solution)/shard_map/all_to_all | solution.py:622
  169.1 14.0 %all-to-all-start.3 = ((f32[128,1,128]{2,1,0:T(1,128)}), f32[128,1,128]{2,1,0:T(1,128)S(1)}, u32[]{:S(2)}, u32[]{:S(2)}) async-start(f32[128,1,128]{2,1,0:T(1,128)} %broadcast_in_dim.69), calls=%async_computation.3 | async-start | bytes 131072 | tf_op jit(solution)/shard_map/all_to_all | solution.py:558
  207.9 21.8 %copy-start.3 = (f32[32,512]{1,0:T(8,128)S(1)}, f32[32,512]{1,0:T(8,128)}, u32[]{:S(2)}) copy-start(f32[32,512]{1,0:T(8,128)} %normal_last.1) | copy-start | bytes 196612
  207.9 14.7 %all-to-all-start.5 = ((f32[128,1,192]{2,1,0:T(1,128)}), f32[128,1,192]{2,1,0:T(1,128)S(1)}, u32[]{:S(2)}, u32[]{:S(2)}) async-start(f32[128,1,192]{2,1,0:T(1,128)} %reshape.144), calls=%async_computation.5 | async-start | bytes 262144 | tf_op jit(solution)/shard_map/all_to_all | solution.py:687
  224.5 19.8 %copy-start.9 = (f32[16]{0:T(128)S(1)}, f32[16]{0:T(128)}, u32[]{:S(2)}) copy-start(f32[16]{0:T(128)} %param.17) | copy-start | bytes 196
  225.4 14.4 %all-to-all-start.6 = ((f32[128,1,192]{2,1,0:T(1,128)}), f32[128,1,192]{2,1,0:T(1,128)S(1)}, u32[]{:S(2)}, u32[]{:S(2)}) async-start(f32[128,1,192]{2,1,0:T(1,128)} %reshape.146), calls=%async_computation.6 | async-start | bytes 262144 | tf_op jit(solution)/shard_map/all_to_all | solution.py:558
  240.6 12.7 %all-to-all-start.4 = ((f32[8,128,128]{2,1,0:T(8,128)}), f32[8,128,128]{2,1,0:T(8,128)S(1)}, u32[]{:S(2)}, u32[]{:S(2)}) async-start(f32[8,128,128]{2,1,0:T(8,128)} %broadcast_in_dim.71), calls=%async_computation.4 | async-start | bytes 1048576 | tf_op jit(solution)/shard_map/all_to_all | solution.py:558

commit v2 on v1

--- a/solution.py
+++ b/solution.py
@@ -22,6 +22,8 @@
 FEW = 2
 LOCAL = BASELINES // PARTS
 SUB = 256
+MODEL_RUNS = 4
+NORMAL_RUNS = 4
 
 robust_dof = 2.0
 small_term = 1e-06
@@ -43,6 +45,15 @@
 )
 
 F32 = jnp.float32
+PER_US = 4.0e6
+
+
+def lasts(microseconds):
+    return pl.CostEstimate(
+        flops=int(microseconds * PER_US), transcendentals=0, bytes_accessed=1 << 20
+    )
+
+
 BF16 = jnp.bfloat16
 
 
@@ -82,11 +93,19 @@
     channels,
     block,
 ):
-    outs, (high_ref, low_ref, left_ref, right_ref) = rest[:-4], rest[-4:]
+    outs, (high_ref, low_ref, left_ref, right_ref, column_ref) = rest[:-5], rest[-5:]
     step = pl.program_id(0)
 
     @pl.when(step == 0)
     def _():
+        own = lax.broadcasted_iota(jnp.int32, (channels, channels), 0)
+        own = own == lax.broadcasted_iota(jnp.int32, (channels, channels), 1)
+        for k in range(DIRS + 1):
+            row = flux_ref[k : k + 1, :] if k < DIRS else ratio_ref[...]
+            column = jnp.where(own, jnp.broadcast_to(row, (channels, channels)), 0.0)
+            column_ref[k * channels : (k + 1) * channels, :] = jnp.broadcast_to(
+                jnp.sum(column, axis=1, keepdims=True), (channels, 128)
+            )
         high, low = two_parts(gains_ref[...])
         high_ref[...] = high
         low_ref[...] = low
@@ -97,20 +116,20 @@
         target[...] = jnp.dot(high_ref[...], hot, preferred_element_type=F32) + jnp.dot(
             low_ref[...], hot, preferred_element_type=F32
         )
-    ratio = ratio_ref[:, :1]
+    ratio = column_ref[DIRS * channels :, :1]
     total = [[None, None] for _ in range(TIMES)]
     for k in range(DIRS):
         re = pl.ds(k * channels, channels)
         im = pl.ds((DIRS + k) * channels, channels)
         left_re, left_im = left_ref[re, :], left_ref[im, :]
         right_re, right_im = right_ref[re, :], right_ref[im, :]
-        flux = flux_ref[re, :1]
+        flux = column_ref[re, :1]
         pair_re = (left_re * right_re + left_im * right_im) * flux
         pair_im = (left_im * right_re - left_re * right_im) * flux
         for t in range(TIMES):
             project = (
-                dirs_ref[0, k] * coord_ref[t : t + 1, :]
-                + dirs_ref[1, k] * coord_ref[TIMES + t : TIMES + t + 1, :]
+                dirs_ref[0, k] * coord_ref[0, t : t + 1, :]
+                + dirs_ref[1, k] * coord_ref[1, t : t + 1, :]
             )
             sky_re, sky_im = turn_parts(project * ratio)
             model_re = pair_re * sky_re - pair_im * sky_im
@@ -173,10 +192,10 @@
             vis_spec,
             pl.BlockSpec((TIMES, channels, block), lambda i: (0, 0, i)),
             pl.BlockSpec((2, block), lambda i: (0, i)),
-            pl.BlockSpec((2 * TIMES, block), lambda i: (0, i)),
+            pl.BlockSpec((2, TIMES, block), lambda i: (0, 0, i)),
             pl.BlockSpec(memory_space=pltpu.SMEM),
-            whole((DIRS * channels, 1)),
-            whole((channels, 1)),
+            whole((DIRS, channels)),
+            whole((1, channels)),
         ],
         out_specs=out_spec,
         out_shape=out_shape,
@@ -185,9 +204,11 @@
             pltpu.VMEM((rows, STATIONS), BF16),
             pltpu.VMEM((rows, block), F32),
             pltpu.VMEM((rows, block), F32),
-        ],
+            pltpu.VMEM(((DIRS + 1) * channels, 128), F32),
+        ],
+        cost_estimate=lasts(8),
         name="wide_residual" if residual_out else "wide_misfit",
-    )(gains, vis, flags, pairs, coords, directions, flux.reshape(-1, 1), ratio.reshape(-1, 1))
+    )(gains, vis, flags, pairs, coords, directions, flux, ratio.reshape(1, -1))
 
 
 def swap_sum(rows):
@@ -204,23 +225,41 @@
     return rows[0]
 
 
+def one_hot(places, count):
+    row = jnp.concatenate([places, places], axis=0).astype(BF16)
+    lanes = places.shape[1]
+    base = lax.broadcasted_iota(jnp.int32, (16, lanes), 0).astype(F32)
+    one = jnp.ones((16, lanes), BF16)
+    none = jnp.zeros((16, lanes), BF16)
+    return jnp.concatenate(
+        [jnp.where(row == (base + float(i)).astype(BF16), one, none) for i in range(0, count, 16)],
+        axis=0,
+    )
+
+
 def model_block(data_ref, table_ref, sky_in, geo, outs, at, misfit):
     left_out, right_out, error_out, sky_out = outs
     lanes = pl.ds(at, SUB)
-    place = lax.broadcasted_iota(jnp.int32, (128, SUB), 0)
     picked = []
     for row in (16, 17):
-        station = data_ref[0, row : row + 1, lanes].astype(jnp.int32)
-        hot = (place == (station & 127)).astype(F32).astype(BF16)
+        station = jnp.broadcast_to(data_ref[0, row : row + 1, lanes], (8, SUB))
+        quarter = jnp.floor(station * (1.0 / 128.0))
+        hot = one_hot(station - 128.0 * quarter, 128)
         got = jnp.dot(
             table_ref[...], jnp.concatenate([hot, hot], axis=0), preferred_element_type=F32
         )
-        quarter = jnp.broadcast_to(station >> 7, (32, SUB))
+        first, second, upper = quarter == 0.0, quarter == 2.0, quarter < 2.0
         picked.append(
-            jnp.where(
-                quarter < 2,
-                jnp.where(quarter == 0, got[0:32], got[32:64]),
-                jnp.where(quarter == 2, got[64:96], got[96:128]),
+            jnp.concatenate(
+                [
+                    jnp.where(
+                        upper,
+                        jnp.where(first, got[i : i + 8], got[32 + i : 40 + i]),
+                        jnp.where(second, got[64 + i : 72 + i], got[96 + i : 104 + i]),
+                    )
+                    for i in range(0, 32, 8)
+                ],
+                axis=0,
             )
         )
     left, right = picked
@@ -255,6 +294,16 @@
     return misfit + part
 
 
+def model_runs(data_ref, table_ref, sky_in, geo, outs):
+    def run(i, misfit):
+        for j in range(MODEL_RUNS):
+            at = pl.multiple_of((i * MODEL_RUNS + j) * SUB, SUB)
+            misfit = model_block(data_ref, table_ref, sky_in, geo, outs, at, misfit)
+        return misfit
+
+    return lax.fori_loop(0, LOCAL // SUB // MODEL_RUNS, run, jnp.zeros((8, SUB), F32))
+
+
 def build_table(table_ref, gains):
     high, low = two_parts(gains)
     for q in range(4):
@@ -272,18 +321,10 @@
     col = lambda i: geo_ref[:, i : i + 1]
     geo = ((col(0), col(1)), (col(2), col(3)), (col(4), col(5)))
 
-    def run(i, carry):
-        at = pl.multiple_of(i * SUB, SUB)
-        model_block(
-            data_ref, table_ref, None, geo, (left_out, right_out, error_out, sky_out), at,
-            jnp.zeros((8, SUB), F32),
-        )
-        return carry
-
-    lax.fori_loop(0, LOCAL // SUB, run, 0)
-
-
-def normal_block(data_ref, left_ref, right_ref, error_ref, sky_ref, total_ref, at, inverse):
+    model_runs(data_ref, table_ref, None, geo, (left_out, right_out, error_out, sky_out))
+
+
+def normal_block(data_ref, left_ref, right_ref, error_ref, sky_ref, at, inverse):
     lanes = pl.ds(at, SUB)
     error = error_ref[0, :, lanes]
     square = error * error
@@ -311,29 +352,39 @@
         rr, ri = right[16 * f : 16 * f + 8], right[16 * f + 8 : 16 * f + 16]
         first += [rr * z_re - ri * z_im, rr * z_im + ri * z_re, (rr * rr + ri * ri) * power]
         second += [lr * z_re + li * z_im, li * z_re - lr * z_im, (lr * lr + li * li) * power]
-    place = lax.broadcasted_iota(jnp.int32, (256, SUB), 0)
-    total = None
+    made = []
     for row, pieces in ((16, first), (17, second)):
-        station = data_ref[0, row : row + 1, lanes].astype(jnp.int32)
-        hot = (place == (station & 255)).astype(F32).astype(BF16)
+        station = jnp.broadcast_to(data_ref[0, row : row + 1, lanes], (8, SUB))
+        half = jnp.where(station >= 256.0, 1.0, 0.0)
+        hot = one_hot(station - 256.0 * half, 256)
+        high = jnp.concatenate([half, half], axis=0).astype(BF16)
         values = jnp.concatenate(pieces, axis=0)
-        upper = jnp.broadcast_to(station, (48, SUB)) >= 256
-        parts = []
-        for half in (jnp.where(upper, 0.0, values), jnp.where(upper, values, 0.0)):
-            parts += list(two_parts(half))
-        got = lax.dot_general(
-            jnp.concatenate(parts, axis=0),
-            hot,
+        parts = two_parts(values)
+        upper = [part[i : i + 16] * high for part in parts for i in (0, 16, 32)]
+        made.append((jnp.concatenate(list(parts) + upper, axis=0), hot))
+    return made
+
+
+def normal_runs(data_ref, left_ref, right_ref, error_ref, sky_ref, total_ref, inverse):
+    def run(i, carry):
+        made = []
+        for j in range(NORMAL_RUNS):
+            at = pl.multiple_of((i * NORMAL_RUNS + j) * SUB, SUB)
+            made += normal_block(data_ref, left_ref, right_ref, error_ref, sky_ref, at, inverse)
+        total_ref[...] += lax.dot_general(
+            jnp.concatenate([m[0] for m in made], axis=1),
+            jnp.concatenate([m[1] for m in made], axis=1),
             (((1,), (1,)), ((), ())),
             preferred_element_type=F32,
         )
-        total = got if total is None else total + got
-    total_ref[...] += total
+        return carry
+
+    lax.fori_loop(0, LOCAL // SUB // NORMAL_RUNS, run, 0)
 
 
 def renew_gains(gains, anchor, total, columns):
-    halves = [total[0:48] + total[48:96], total[96:144] + total[144:192]]
-    sums = jnp.concatenate(halves, axis=1)
+    both, upper = total[0:48] + total[48:96], total[96:144] + total[144:192]
+    sums = jnp.concatenate([both - upper, upper], axis=1)
     rows = []
     for f in range(FEW):
         flux = columns[:, 2 + f : 3 + f]
@@ -348,8 +399,15 @@
     return jnp.concatenate(rows, axis=0)
 
 
+def inverse_of(squares_ref, count_ref):
+    squares = jnp.sum(jnp.sum(squares_ref[...], axis=0, keepdims=True), axis=1, keepdims=True)
+    count = jnp.sum(count_ref[...], axis=1, keepdims=True)
+    return 1.0 / (squares / (count + 1.0) + small_term)
+
+
 def middle_kernel(
-    sigma_ref,
+    squares_ref,
+    count_ref,
     data_ref,
     left_ref,
     right_ref,
@@ -365,6 +423,7 @@
     misfit_out,
     table_ref,
     total_ref,
+    misfit_ref,
 ):
     phase, step = pl.program_id(0), pl.program_id(1)
     last = pl.num_programs(1) - 1
@@ -375,16 +434,10 @@
 
     @pl.when(phase == 0)
     def _():
-        inverse = sigma_ref[0, 0]
-
-        def run(i, carry):
-            at = pl.multiple_of(i * SUB, SUB)
-            normal_block(
-                data_ref, left_ref, right_ref, error_ref, sky_ref, total_ref, at, inverse
-            )
-            return carry
-
-        lax.fori_loop(0, LOCAL // SUB, run, 0)
+        normal_runs(
+            data_ref, left_ref, right_ref, error_ref, sky_ref, total_ref,
+            inverse_of(squares_ref, count_ref),
+        )
 
     @pl.when((phase == 0) & (step == last))
     def _():
@@ -394,27 +447,27 @@
 
     @pl.when(phase == 1)
     def _():
-        def run(i, misfit):
-            at = pl.multiple_of(i * SUB, SUB)
-            return model_block(
-                data_ref, table_ref, sky_ref, None, (left_out, right_out, error_out, None), at,
-                misfit,
-            )
-
-        misfit = lax.fori_loop(0, LOCAL // SUB, run, jnp.zeros((8, SUB), F32))
+        misfit = model_runs(
+            data_ref, table_ref, sky_ref, None, (left_out, right_out, error_out, None)
+        )
         misfit = jnp.sum(misfit[:, :128] + misfit[:, 128:], axis=0, keepdims=True)
 
         @pl.when(step == 0)
         def _():
-            misfit_out[...] = misfit
+            misfit_ref[...] = misfit
 
         @pl.when(step > 0)
         def _():
-            misfit_out[...] += misfit
+            misfit_ref[...] += misfit
+
+        @pl.when(step == last)
+        def _():
+            misfit_out[...] = jnp.broadcast_to(misfit_ref[...], misfit_out.shape)
 
 
 def last_kernel(
-    sigma_ref,
+    squares_ref,
+    count_ref,
     data_ref,
     left_ref,
     right_ref,
@@ -432,14 +485,10 @@
     def _():
         total_ref[...] = jnp.zeros_like(total_ref)
 
-    inverse = sigma_ref[0, 0]
-
-    def run(i, carry):
-        at = pl.multiple_of(i * SUB, SUB)
-        normal_block(data_ref, left_ref, right_ref, error_ref, sky_ref, total_ref, at, inverse)
-        return carry
-
-    lax.fori_loop(0, LOCAL // SUB, run, 0)
+    normal_runs(
+        data_ref, left_ref, right_ref, error_ref, sky_ref, total_ref,
+        inverse_of(squares_ref, count_ref),
+    )
 
     @pl.when(step == pl.num_programs(0) - 1)
     def _():
@@ -480,11 +529,12 @@
             jax.ShapeDtypeStruct((PARTS,) + SKY + (LOCAL,), F32),
         ],
         scratch_shapes=[pltpu.VMEM((128, 256), BF16)],
+        cost_estimate=lasts(10),
         name="first_model",
     )(data, gains, geo)
 
 
-def middle_call(sigma, data, left, right, error, sky, gains, anchor, geo):
+def middle_call(squares, count, data, left, right, error, sky, gains, anchor, geo, devices):
     at = lambda p, i: (i, 0, 0)
     held = lambda p, i: ((1 - p) * i + p * (PARTS - 1), 0, 0)
     made = lambda p, i: (p * i, 0, 0)
@@ -493,7 +543,8 @@
         middle_kernel,
         grid=(2, PARTS),
         in_specs=[
-            pl.BlockSpec(memory_space=pltpu.SMEM),
+            pl.BlockSpec(squares.shape, small),
+            pl.BlockSpec((1, 128), small),
             pl.BlockSpec((1, ROWS, LOCAL), at),
             pl.BlockSpec((1, GAIN_ROWS, LOCAL), held),
             pl.BlockSpec((1, GAIN_ROWS, LOCAL), held),
@@ -508,28 +559,34 @@
             pl.BlockSpec((1, GAIN_ROWS, LOCAL), made),
             pl.BlockSpec((1, GAIN_ROWS, LOCAL), made),
             pl.BlockSpec((1, 8, LOCAL), made),
-            pl.BlockSpec((1, 128), small),
+            pl.BlockSpec((devices, 128), small),
         ],
         out_shape=[
             jax.ShapeDtypeStruct((GAIN_ROWS, STATIONS), F32),
             shapes_of(GAIN_ROWS),
             shapes_of(GAIN_ROWS),
             shapes_of(8),
-            jax.ShapeDtypeStruct((1, 128), F32),
-        ],
-        scratch_shapes=[pltpu.VMEM((128, 256), BF16), pltpu.VMEM((192, 256), F32)],
+            jax.ShapeDtypeStruct((devices, 128), F32),
+        ],
+        scratch_shapes=[
+            pltpu.VMEM((128, 256), BF16),
+            pltpu.VMEM((192, 256), F32),
+            pltpu.VMEM((1, 128), F32),
+        ],
+        cost_estimate=lasts(20),
         name="normal_and_model",
-    )(sigma, data, left, right, error, sky, gains, anchor, geo)
-
-
-def last_call(sigma, data, left, right, error, sky, gains, anchor, geo):
+    )(squares, count, data, left, right, error, sky, gains, anchor, geo)
+
+
+def last_call(squares, count, data, left, right, error, sky, gains, anchor, geo):
     at = lambda i: (i, 0, 0)
     small = lambda i: (0, 0)
     return pl.pallas_call(
         last_kernel,
         grid=(PARTS,),
         in_specs=[
-            pl.BlockSpec(memory_space=pltpu.SMEM),
+            pl.BlockSpec(squares.shape, small),
+            pl.BlockSpec((1, 128), small),
             pl.BlockSpec((1, ROWS, LOCAL), at),
             pl.BlockSpec((1, GAIN_ROWS, LOCAL), at),
             pl.BlockSpec((1, GAIN_ROWS, LOCAL), at),
@@ -542,8 +599,9 @@
         out_specs=pl.BlockSpec((GAIN_ROWS, STATIONS), small),
         out_shape=jax.ShapeDtypeStruct((GAIN_ROWS, STATIONS), F32),
         scratch_shapes=[pltpu.VMEM((192, 256), F32)],
+        cost_estimate=lasts(11),
         name="normal_last",
-    )(sigma, data, left, right, error, sky, gains, anchor, geo)
+    )(squares, count, data, left, right, error, sky, gains, anchor, geo)
 
 
 def legendre(ratios):
@@ -621,13 +679,12 @@
     send = send.reshape(PARTS, ROWS * LOCAL // 128, 128)
     data = lax.all_to_all(send, BL, 0, 0, tiled=True).reshape(PARTS, ROWS, LOCAL)
 
-    coords = baseline_spatial_coords.reshape(2 * TIMES, LOCAL)
     wide = functools.partial(
         wide_model,
         vis=visibilities,
         flags=sample_flag_weight,
         pairs=baseline_station_pair,
-        coords=coords,
+        coords=baseline_spatial_coords,
         directions=directions,
         flux=source_flux,
         ratio=channel_ratio,
@@ -638,14 +695,12 @@
     flux = own_channels(source_flux, 1, own)
     basis = legendre(ratio)
     gram_own = (basis[:, None, :] * basis[None, :, :]).sum(-1)
+    sums, data = lax.optimization_barrier((sums, data))
     payload = jnp.concatenate([sums, jnp.pad(gram_own.reshape(1, 9), ((0, 0), (0, 119)))], axis=1)
     arrived = sent_to_all(payload, ALL)
-    arrived = arrived.sum(axis=0)[0]
-    squares, weight_count = arrived[:128].sum(), arrived[128:256].sum()
-    gram = arrived[256:265].reshape(3, 3)
-
-    def inverse_sigma(squares):
-        return (1.0 / (squares / (weight_count + 1.0) + small_term)).reshape(1, 1)
+    arrived = arrived.sum(axis=0)
+    squares, count = arrived[:, :128], arrived[:, 128:256]
+    gram = arrived[0, 256:265].reshape(3, 3)
 
     def rows_of(array):
         part = own_channels(array, 2, own)
@@ -671,38 +726,39 @@
     )
 
     left, right, error, sky = first_call(data, gains, geo)
-    sigma = inverse_sigma(squares)
     for iteration in range(ITERS - 1):
         gains, left, right, error, misfit = middle_call(
-            sigma, data, left, right, error, sky, gains, anchor, geo
-        )
-        sigma = inverse_sigma(sent_to_all(misfit, ALL).sum())
-    gains = last_call(sigma, data, left, right, error, sky, gains, anchor, geo)
-
-    new_rows = gains.reshape(FEW, 2, DIRS, STATIONS)
-    lifted = new_rows + dual
-    part = 2 * DIRS * STATIONS // devices
-    rhs = (basis[:, :, None] * lifted.reshape(1, FEW, -1)).sum(axis=1)
-    rhs = rhs.reshape(NPOLY, devices, part).transpose(1, 0, 2)
-    rhs = lax.all_to_all(rhs, ALL, 0, 0, tiled=True).sum(axis=0)
-    solved = jnp.stack(cholesky_solve(gram, [rhs[j] for j in range(NPOLY)]))
-    everyone = sent_to_all(solved, ALL)
-    new_consensus = (
-        everyone.transpose(1, 0, 2).reshape(NPOLY, 2, DIRS, STATIONS).transpose(1, 0, 2, 3)
-    )
+            squares, count, data, left, right, error, sky, gains, anchor, geo, devices
+        )
+        squares = lax.all_to_all(misfit[:, None], ALL, 0, 0, tiled=True)[:, 0]
+    gains = last_call(squares, count, data, left, right, error, sky, gains, anchor, geo)
 
     gathered = sent_to_all(gains.reshape(GAIN_ROWS * STATIONS // 128, 128), BL)
     new_gains = (
         gathered.reshape(PARTS * FEW, 2, DIRS, STATIONS).transpose(1, 2, 0, 3)
     )
+    new_gains = lax.optimization_barrier(new_gains)
     residuals = wide(new_gains.reshape(-1, STATIONS), residual_out=True)
 
     all_basis = legendre(channel_ratio)
+    lifted = new_gains + scaled_dual
+    rhs = jnp.stack(
+        [
+            (all_basis[j][None, None, :, None] * lifted).sum(axis=2).reshape(-1, STATIONS)
+            for j in range(NPOLY)
+        ],
+        axis=1,
+    )
+    rhs = lax.all_to_all(rhs, FREQ, 0, 0, tiled=True)
+    rhs = rhs.sum(axis=0)
+    solved = jnp.stack(cholesky_solve(gram, [rhs[j] for j in range(NPOLY)]))
+    everyone = sent_to_all(solved, FREQ)
+    new_consensus = everyone.reshape(2, DIRS, NPOLY, STATIONS).transpose(0, 2, 1, 3)
     fitted = sum(
         all_basis[j][None, None, :, None] * new_consensus[:, j][:, :, None, :]
         for j in range(NPOLY)
     )
-    new_dual = scaled_dual + new_gains - fitted
+    new_dual = lifted - fitted
     return (new_gains, new_consensus, new_dual, residuals)
 
 

time: 266 us -> 189 us (0.71)
  Pallas kernels: 129 us -> 79.6 us
  waiting for transfers between devices: 51.8 us -> 19.6 us
  blocking collectives: 14 us -> 35.1 us
  local copies, waits for them, and re-layouts: 22.1 us -> 16.1 us
  starting transfers between devices: 31.9 us -> 27.7 us
  other arithmetic: 7.74 us -> 3.77 us
  between operations: 7.7 us -> 4.99 us
    pallas_call x3, Pallas kernels: 95.7 us -> 53.1 us  [the longest x2 41.1 us: middle_call(): pl.pallas_call(middle_kernel, grid=(2, PARTS), in_specs=[pl.BlockSpec(squ...]
    all_to_all x4 -> x3, waiting for transfers between devices: 34.1 us -> 8.45 us  [sent_to_all(): lax.all_to_all(jnp.broadcast_to(array[None], (count, *array.shape)), axes...]
    all_to_all x1 -> x2, blocking collectives: 14 us -> 35.1 us  [body(): squares = lax.all_to_all(misfit[:, None], ALL, 0, 0, tiled=True)[:, 0]]
    all_to_all x4 -> x3, starting transfers between devices: 23.8 us -> 16.6 us  [sent_to_all(): lax.all_to_all(jnp.broadcast_to(array[None], (count, *array.shape)), axes...]
    pallas_call x1, Pallas kernels: 16.7 us -> 9.73 us  [first_call(): pl.pallas_call(first_kernel, grid=(PARTS,), in_specs=[pl.BlockSpec((1, RO...]
    reshape x6 -> x0, local copies, waits for them, and re-layouts: 4.44 us -> none  [the longest x1 1.39 us: body(): coords = baseline_spatial_coords.reshape(2 * TIMES, LOCAL)]
    all_to_all x1, waiting for transfers between devices: 12.2 us -> 8.2 us  [body(): lax.all_to_all(send, BL, 0, 0, tiled=True).reshape(PARTS, ROWS, LOCAL)]
  transfers between devices with their start and end apart: 6 -> 5, of which waited for: 6 -> 3; matrix products, arithmetic and copies ran while one was open for 4% -> 3% of each run, Pallas kernels for 0% -> 14%
where the time goes in v2:
time: 189 us; the launch traced here: 187 us
  Pallas kernels  79.6 us (42%)
  blocking collectives  35.1 us (19%)
  starting transfers between devices  27.7 us (15%)
  waiting for transfers between devices  19.6 us (10%)
  local copies, waits for them, and re-layouts  16.1 us (9%)
  between operations  4.99 us (3%)
  other arithmetic  3.77 us (2%)
    pallas_call x2, Pallas kernels, middle_call(): pl.pallas_call(middle_kernel, grid=(2, PARTS), in_specs=[pl.BlockSpec(squ...  41.1 us
    all_to_all x2, blocking collectives, body(): squares = lax.all_to_all(misfit[:, None], ALL, 0, 0, tiled=True)[:, 0]  35.1 us
    pallas_call x2, Pallas kernels, wide_model(): pl.pallas_call(functools.partial(wide_kernel, residual_out=residual_out,...  16.8 us
    all_to_all x3, starting transfers between devices, sent_to_all(): lax.all_to_all(jnp.broadcast_to(array[None], (count, *array.shape)), axes...  16.6 us
    pallas_call x1, Pallas kernels, last_call(): pl.pallas_call(last_kernel, grid=(PARTS,), in_specs=[pl.BlockSpec(squares...  12 us
    pallas_call x1, Pallas kernels, first_call(): pl.pallas_call(first_kernel, grid=(PARTS,), in_specs=[pl.BlockSpec((1, RO...  9.73 us
    all_to_all x3, waiting for transfers between devices, sent_to_all(): lax.all_to_all(jnp.broadcast_to(array[None], (count, *array.shape)), axes...  8.45 us
    all_to_all x1, waiting for transfers between devices, body(): lax.all_to_all(send, BL, 0, 0, tiled=True).reshape(PARTS, ROWS, LOCAL)  8.2 us
  transfers between devices with their start and end apart: 5, of which 3 were waited for; matrix products, arithmetic and copies ran while one was open for 3% of the time, Pallas kernels for 14%

profile of v2, /device:TPU:1, one launch (start us, length us, event | category | flops | bytes accessed | tf_op | source)
XLA Modules:
  0.0 186.9 jit_solution(17848655551302100407)
XLA Ops:
  2.2 1.0 convert_element_type.8
  5.1 1.2 reshape.80
  6.3 6.0 %all-to-all-start = ((f32[8,288,128]{2,1,0:T(8,128)}), f32[8,288,128]{2,1,0:T(8,128)S(1)}, u32[]{:S(2)}, u32[]{:S(2)}) async-start(f32[8,288,128]{2,1,0:T(8,128)} %reshape.80), calls=%async_computation | async-start | bytes 2359296 | tf_op jit(solution)/shard_map/all_to_all | solution.py:680
  12.9 8.4 %wide_misfit.1 = f32[1,256]{1,0:T(1,128)} custom-call(f32[256,512]{1,0:T(8,128)} %bitcast.68, f32[2,2,16,2048]{3,2,1,0:T(8,128)} %vis_ref.3, s32[2,16,2048]{2,1,0:T(8,128)} %flag_ref.3, s32[2,2048]{1,0:T(2,128)} %pair_ref.3, f32[2,2,2048]{2,1,0:T(2,128)} %coord_ref.3, f32[2,8]{1,0:T(2,128)} %dirs_ref.3, f32[8,16]{1,0:T(8,128)} %flux_ref.3, f32[1,16]{1,0:T(1,128)} %bitcast.76), custom_call_target="tpu_custom_call" | custom-call | flops 32000000 | bytes 1048576 | tf_op jit(solution)/shard_map/wide_misfit/pallas_call | solution.py:185
  21.5 8.2 %all-to-all-done = f32[8,288,128]{2,1,0:T(8,128)S(1)} async-done(((f32[8,288,128]{2,1,0:T(8,128)}), f32[8,288,128]{2,1,0:T(8,128)S(1)}, u32[]{:S(2)}, u32[]{:S(2)}) %all-to-all-start) | async-done | bytes 1179680 | tf_op jit(solution)/shard_map/all_to_all | solution.py:680
  29.7 1.4 reshape.81.data_ref
  31.8 8.8 %all-to-all-start.1 = ((f32[128,1,384]{2,1,0:T(1,128)}), f32[128,1,384]{2,1,0:T(1,128)S(1)}, u32[]{:S(2)}, u32[]{:S(2)}) async-start(f32[128,1,384]{2,1,0:T(1,128)} %broadcast_in_dim.55), calls=%async_computation.1 | async-start | bytes 393216 | tf_op jit(solution)/shard_map/all_to_all | solution.py:616
  40.6 1.0 dynamic-slice_bitcast_fusion
  43.7 9.7 %first_model.1 = (f32[8,32,2048]{2,1,0:T(8,128)}, f32[8,32,2048]{2,1,0:T(8,128)}, f32[8,8,2048]{2,1,0:T(8,128)}, f32[8,2,2,2,8,2048]{5,4,3,2,1,0:T(8,128)}) custom-call(f32[8,18,2048]{2,1,0:T(8,128)} %reshape.81.data_ref, f32[32,512]{1,0:T(8,128)} %bitcast.69, f32[8,8]{1,0:T(8,128)} %concatenate.11.geo_ref), custom_call_target="tpu_custom_call" | custom-call | flops 40000000 | bytes 1048576 | tf_op jit(solution)/shard_map/first_model/pallas_call | solution.py:511
  54.2 20.5 %normal_and_model.2 = (f32[32,512]{1,0:T(8,128)}, f32[8,32,2048]{2,1,0:T(8,128)}, f32[8,32,2048]{2,1,0:T(8,128)}, f32[8,8,2048]{2,1,0:T(8,128)}, f32[128,128]{1,0:T(8,128)}) custom-call(f32[1,128]{1,0:T(1,128)} %get-tuple-element.80.squares_ref, f32[1,128]{1,0:T(1,128)} %get-tuple-element.79.count_ref, f32[8,18,2048]{2,1,0:T(8,128)} %reshape.81.data_ref, ...), custom_call_target="tpu_custom_call" | custom-call | flops 80000000 | bytes 1048576 | tf_op jit(solution)/shard_map/normal_and_model/pallas_call | solution.py:542
  74.8 19.7 %all_to_all.35 = f32[128,1,128]{2,1,0:T(1,128)} all-to-all(f32[128,1,128]{2,1,0:T(1,128)} %bitcast.73), channel_id=1, replica_groups=mesh['bl_0'=4,'bl_1'=2,'freq_0'=4,'freq_1'=2,'freq_2'=2] {'bl_0','bl_1',..., dimensions={0} | all-to-all | bytes 131072 | tf_op jit(solution)/shard_map/all_to_all | solution.py:733
  94.4 20.6 %normal_and_model.3 = (f32[32,512]{1,0:T(8,128)}, f32[8,32,2048]{2,1,0:T(8,128)}, f32[8,32,2048]{2,1,0:T(8,128)}, f32[8,8,2048]{2,1,0:T(8,128)}, f32[128,128]{1,0:T(8,128)}) custom-call(f32[128,128]{1,0:T(8,128)} %bitcast.71, f32[1,128]{1,0:T(1,128)} %get-tuple-element.79.count_ref, f32[8,18,2048]{2,1,0:T(8,128)} %reshape.81.data_ref, ...), custom_call_target="tpu_custom_call" | custom-call | flops 80000000 | bytes 1048576 | tf_op jit(solution)/shard_map/normal_and_model/pallas_call | solution.py:542
  115.0 15.4 %all_to_all.36 = f32[128,1,128]{2,1,0:T(1,128)} all-to-all(f32[128,1,128]{2,1,0:T(1,128)} %bitcast.74), channel_id=1, replica_groups=mesh['bl_0'=4,'bl_1'=2,'freq_0'=4,'freq_1'=2,'freq_2'=2] {'bl_0','bl_1',..., dimensions={0} | all-to-all | bytes 131072 | tf_op jit(solution)/shard_map/all_to_all | solution.py:733
  130.5 12.0 %normal_last.1 = f32[32,512]{1,0:T(8,128)} custom-call(f32[128,128]{1,0:T(8,128)} %bitcast.72, f32[1,128]{1,0:T(1,128)} %get-tuple-element.79.count_ref, f32[8,18,2048]{2,1,0:T(8,128)} %reshape.81.data_ref, f32[8,32,2048]{2,1,0:T(8,128)} %get-tuple-element.32.left_ref, f32[8,32,2048]{2,1,0:T(8,128)} %get-tuple-element.33.right_ref, ...), custom_call_target="tpu_custom_call" | custom-call | flops 44000000 | bytes 1048576 | tf_op jit(solution)/shard_map/normal_last/pallas_call | solution.py:584
  142.4 0.9 broadcast_in_dim.60
  143.3 0.8 broadcast_in_dim.61
  144.1 3.5 %all-to-all-start.4 = ((f32[8,128,128]{2,1,0:T(8,128)}), f32[8,128,128]{2,1,0:T(8,128)S(1)}, u32[]{:S(2)}, u32[]{:S(2)}) async-start(f32[8,128,128]{2,1,0:T(8,128)} %broadcast_in_dim.61), calls=%async_computation.4 | async-start | bytes 1048576 | tf_op jit(solution)/shard_map/all_to_all | solution.py:616
  147.8 8.4 %all-to-all-done.4 = f32[8,128,128]{2,1,0:T(8,128)S(1)} async-done(((f32[8,128,128]{2,1,0:T(8,128)}), f32[8,128,128]{2,1,0:T(8,128)S(1)}, u32[]{:S(2)}, u32[]{:S(2)}) %all-to-all-start.4) | async-done | bytes 524320 | tf_op jit(solution)/shard_map/all_to_all | solution.py:616
  157.5 5.1 %all-to-all-start.5 = ((f32[16,3,512]{2,1,0:T(4,128)}), f32[16,3,512]{2,1,0:T(4,128)S(1)}, u32[]{:S(2)}, u32[]{:S(2)}) async-start(f32[16,3,512]{2,1,0:T(4,128)} %pad_maximum_fusion.1), calls=%async_computation.5 | async-start | bytes 262144 | tf_op jit(solution)/shard_map/all_to_all | solution.py:752
  167.3 3.0 %all-to-all-done.5 = f32[16,3,512]{2,1,0:T(4,128)S(1)} async-done(((f32[16,3,512]{2,1,0:T(4,128)}), f32[16,3,512]{2,1,0:T(4,128)S(1)}, u32[]{:S(2)}, u32[]{:S(2)}) %all-to-all-start.5) | async-done | bytes 98336 | tf_op jit(solution)/shard_map/all_to_all | solution.py:752
  171.1 4.3 %all-to-all-start.6 = ((f32[16,3,512]{2,1,0:T(4,128)}), f32[16,3,512]{2,1,0:T(4,128)S(1)}, u32[]{:S(2)}, u32[]{:S(2)}) async-start(f32[16,3,512]{2,1,0:T(4,128)} %broadcast_in_dim.62), calls=%async_computation.6 | async-start | bytes 262144 | tf_op jit(solution)/shard_map/all_to_all | solution.py:616
  175.4 1.1 copy.90
  176.5 8.4 %wide_residual.1 = f32[2,2,16,2048]{3,2,1,0:T(8,128)} custom-call(f32[256,512]{1,0:T(8,128)} %bitcast.59, f32[2,2,16,2048]{3,2,1,0:T(8,128)} %vis_ref.3, s32[2,16,2048]{2,1,0:T(8,128)} %flag_ref.3, s32[2,2048]{1,0:T(2,128)} %pair_ref.3, f32[2,2,2048]{2,1,0:T(2,128)} %coord_ref.3, f32[2,8]{1,0:T(2,128)} %dirs_ref.3, f32[8,16]{1,0:T(8,128)} %flux_ref.3, ...), custom_call_target="tpu_custom_call" | custom-call | flops 32000000 | bytes 1048576 | tf_op jit(solution)/shard_map/wide_residual/pallas_call | solution.py:185
  185.8 1.1 copy.92
  (72 shorter events, 11.4 us)
Async XLA Ops:
  0.6 2.9 %copy-start = (f32[2,2,16,2048]{3,2,1,0:T(8,128)S(1)}, f32[2,2,16,2048]{3,2,1,0:T(8,128)}, u32[]{:S(2)}) copy-start(f32[2,2,16,2048]{3,2,1,0:T(8,128)} %vis_ref.3) | copy-start | bytes 1572868
  6.3 6.0 %copy-start.5 = (f32[16]{0:T(128)S(1)}, f32[16]{0:T(128)}, u32[]{:S(2)}) copy-start(f32[16]{0:T(128)} %param.17) | copy-start | bytes 196
  6.3 6.5 %copy-start.4 = (f32[2,8]{1,0:T(2,128)S(1)}, f32[2,8]{1,0:T(2,128)}, u32[]{:S(2)}) copy-start(f32[2,8]{1,0:T(2,128)} %dirs_ref.3) | copy-start | bytes 196
  6.3 23.3 %all-to-all-start = ((f32[8,288,128]{2,1,0:T(8,128)}), f32[8,288,128]{2,1,0:T(8,128)S(1)}, u32[]{:S(2)}, u32[]{:S(2)}) async-start(f32[8,288,128]{2,1,0:T(8,128)} %reshape.80), calls=%async_computation | async-start | bytes 2359296 | tf_op jit(solution)/shard_map/all_to_all | solution.py:680
  12.3 9.0 %copy-start.8 = (f32[8]{0:T(128)S(1)}, f32[8]{0:T(128)}, u32[]{:S(2)}) copy-start(f32[8]{0:T(128)} %param.21) | copy-start | bytes 100
  12.3 9.0 %copy-start.2 = (f32[2,3,8,512]{3,2,1,0:T(8,128)S(1)}, f32[2,3,8,512]{3,2,1,0:T(8,128)}, u32[]{:S(2)}) copy-start(f32[2,3,8,512]{3,2,1,0:T(8,128)} %param.20) | copy-start | bytes 294916
  12.3 9.0 %copy-start.1 = (f32[2,8,16,512]{3,2,1,0:T(8,128)S(1)}, f32[2,8,16,512]{3,2,1,0:T(8,128)}, u32[]{:S(2)}) copy-start(f32[2,8,16,512]{3,2,1,0:T(8,128)} %param.19) | copy-start | bytes 1572868
  21.4 9.6 %copy-start.7 = (f32[1,256]{1,0:T(1,128)S(1)}, f32[1,256]{1,0:T(1,128)}, u32[]{:S(2)}) copy-start(f32[1,256]{1,0:T(1,128)} %wide_misfit.1) | copy-start | bytes 3076
  21.4 21.5 %copy-start.3 = (f32[8,16]{1,0:T(8,128)S(1)}, f32[8,16]{1,0:T(8,128)}, u32[]{:S(2)}) copy-start(f32[8,16]{1,0:T(8,128)} %flux_ref.3) | copy-start | bytes 1540
  31.8 21.6 %all-to-all-start.1 = ((f32[128,1,384]{2,1,0:T(1,128)}), f32[128,1,384]{2,1,0:T(1,128)S(1)}, u32[]{:S(2)}, u32[]{:S(2)}) async-start(f32[128,1,384]{2,1,0:T(1,128)} %broadcast_in_dim.55), calls=%async_computation.1 | async-start | bytes 393216 | tf_op jit(solution)/shard_map/all_to_all | solution.py:616
  142.4 5.2 %copy-start.6 = (f32[16]{0:T(128)S(1)}, f32[16]{0:T(128)}, u32[]{:S(2)}) copy-start(f32[16]{0:T(128)} %param.17) | copy-start | bytes 196
  144.1 12.1 %all-to-all-start.4 = ((f32[8,128,128]{2,1,0:T(8,128)}), f32[8,128,128]{2,1,0:T(8,128)S(1)}, u32[]{:S(2)}, u32[]{:S(2)}) async-start(f32[8,128,128]{2,1,0:T(8,128)} %broadcast_in_dim.61), calls=%async_computation.4 | async-start | bytes 1048576 | tf_op jit(solution)/shard_map/all_to_all | solution.py:616
  157.5 12.8 %all-to-all-start.5 = ((f32[16,3,512]{2,1,0:T(4,128)}), f32[16,3,512]{2,1,0:T(4,128)S(1)}, u32[]{:S(2)}, u32[]{:S(2)}) async-start(f32[16,3,512]{2,1,0:T(4,128)} %pad_maximum_fusion.1), calls=%async_computation.5 | async-start | bytes 262144 | tf_op jit(solution)/shard_map/all_to_all | solution.py:752
  171.1 13.9 %all-to-all-start.6 = ((f32[16,3,512]{2,1,0:T(4,128)}), f32[16,3,512]{2,1,0:T(4,128)S(1)}, u32[]{:S(2)}, u32[]{:S(2)}) async-start(f32[16,3,512]{2,1,0:T(4,128)} %broadcast_in_dim.62), calls=%async_computation.6 | async-start | bytes 262144 | tf_op jit(solution)/shard_map/all_to_all | solution.py:616

commit v3 on v2

--- a/solution.py
+++ b/solution.py
@@ -22,7 +22,7 @@
 FEW = 2
 LOCAL = BASELINES // PARTS
 SUB = 256
-MODEL_RUNS = 4
+MODEL_RUNS = 8
 NORMAL_RUNS = 4
 
 robust_dof = 2.0
@@ -207,6 +207,7 @@
             pltpu.VMEM(((DIRS + 1) * channels, 128), F32),
         ],
         cost_estimate=lasts(8),
+        compiler_params=pltpu.CompilerParams(vmem_limit_bytes=16 * 1024 * 1024),
         name="wide_residual" if residual_out else "wide_misfit",
     )(gains, vis, flags, pairs, coords, directions, flux, ratio.reshape(1, -1))
 
@@ -237,23 +238,23 @@
     )
 
 
-def model_block(data_ref, table_ref, sky_in, geo, outs, at, misfit):
-    left_out, right_out, error_out, sky_out = outs
+def model_block(part, at, data_ref, table_ref, sky_ref, outs, misfit, geo):
+    left_out, right_out, error_out = outs
     lanes = pl.ds(at, SUB)
     picked = []
-    for row in (16, 17):
-        station = jnp.broadcast_to(data_ref[0, row : row + 1, lanes], (8, SUB))
+    for side in range(2):
+        station = jnp.broadcast_to(data_ref[part, 16 + side : 17 + side, lanes], (8, SUB))
         quarter = jnp.floor(station * (1.0 / 128.0))
         hot = one_hot(station - 128.0 * quarter, 128)
         got = jnp.dot(
             table_ref[...], jnp.concatenate([hot, hot], axis=0), preferred_element_type=F32
         )
-        first, second, upper = quarter == 0.0, quarter == 2.0, quarter < 2.0
+        first, second, lower = quarter == 0.0, quarter == 2.0, quarter < 2.0
         picked.append(
             jnp.concatenate(
                 [
                     jnp.where(
-                        upper,
+                        lower,
                         jnp.where(first, got[i : i + 8], got[32 + i : 40 + i]),
                         jnp.where(second, got[64 + i : 72 + i], got[96 + i : 104 + i]),
                     )
@@ -263,8 +264,8 @@
             )
         )
     left, right = picked
-    left_out[0, :, lanes] = left
-    right_out[0, :, lanes] = right
+    left_out[part, :, lanes] = left
+    right_out[part, :, lanes] = right
     pieces = [None] * 8
     for f in range(FEW):
         lr, li = left[16 * f : 16 * f + 8], left[16 * f + 8 : 16 * f + 16]
@@ -272,69 +273,61 @@
         pair_re = lr * rr + li * ri
         pair_im = li * rr - lr * ri
         for t in range(TIMES):
-            if sky_in is None:
+            if geo is not None:
                 dirs, flux, ratio = geo
-                project = dirs[0] * data_ref[0, 12 + t : 13 + t, lanes] + dirs[1] * data_ref[
-                    0, 14 + t : 15 + t, lanes
-                ]
+                project = dirs[0] * data_ref[part, 12 + t : 13 + t, lanes] + dirs[
+                    1
+                ] * data_ref[part, 14 + t : 15 + t, lanes]
                 sky_re, sky_im = turn_parts(project * ratio[f])
                 sky_re = sky_re * flux[f]
                 sky_im = sky_im * flux[f]
-                sky_out[0, t, f, 0, :, lanes] = sky_re
-                sky_out[0, t, f, 1, :, lanes] = sky_im
+                sky_ref[part, t, f, 0, :, lanes] = sky_re
+                sky_ref[part, t, f, 1, :, lanes] = sky_im
             else:
-                sky_re = sky_in[0, t, f, 0, :, lanes]
-                sky_im = sky_in[0, t, f, 1, :, lanes]
+                sky_re = sky_ref[part, t, f, 0, :, lanes]
+                sky_im = sky_ref[part, t, f, 1, :, lanes]
             pieces[2 * t + f] = pair_re * sky_re - pair_im * sky_im
             pieces[4 + 2 * t + f] = pair_re * sky_im + pair_im * sky_re
-    error = data_ref[0, 0:8, lanes] - swap_sum(pieces)
-    error_out[0, :, lanes] = error
-    flagged = data_ref[0, 8:12, lanes]
-    part = jnp.concatenate([flagged, flagged], axis=0) * (error * error)
-    return misfit + part
-
-
-def model_runs(data_ref, table_ref, sky_in, geo, outs):
+    error = data_ref[part, 0:8, lanes] - swap_sum(pieces)
+    error_out[part, :, lanes] = error
+    flagged = data_ref[part, 8:12, lanes]
+    return misfit + jnp.concatenate([flagged, flagged], axis=0) * (error * error)
+
+
+def model_runs(data_ref, table_ref, sky_ref, outs, geo):
+    steps = LOCAL // SUB // MODEL_RUNS
+
     def run(i, misfit):
+        part, first = i // steps, (i % steps) * MODEL_RUNS
         for j in range(MODEL_RUNS):
-            at = pl.multiple_of((i * MODEL_RUNS + j) * SUB, SUB)
-            misfit = model_block(data_ref, table_ref, sky_in, geo, outs, at, misfit)
+            at = pl.multiple_of((first + j) * SUB, SUB)
+            misfit = model_block(
+                part, at, data_ref, table_ref, sky_ref, outs, misfit, geo
+            )
         return misfit
 
-    return lax.fori_loop(0, LOCAL // SUB // MODEL_RUNS, run, jnp.zeros((8, SUB), F32))
+    return lax.fori_loop(0, PARTS * steps, run, jnp.zeros((8, SUB), F32))
 
 
 def build_table(table_ref, gains):
-    high, low = two_parts(gains)
-    for q in range(4):
-        table_ref[32 * q : 32 * q + 32, 0:128] = high[:, 128 * q : 128 * q + 128]
-        table_ref[32 * q : 32 * q + 32, 128:256] = low[:, 128 * q : 128 * q + 128]
-
-
-def first_kernel(
-    data_ref, gains_ref, geo_ref, left_out, right_out, error_out, sky_out, table_ref
-):
-    @pl.when(pl.program_id(0) == 0)
-    def _():
-        build_table(table_ref, gains_ref[...])
-
-    col = lambda i: geo_ref[:, i : i + 1]
-    geo = ((col(0), col(1)), (col(2), col(3)), (col(4), col(5)))
-
-    model_runs(data_ref, table_ref, None, geo, (left_out, right_out, error_out, sky_out))
-
-
-def normal_block(data_ref, left_ref, right_ref, error_ref, sky_ref, at, inverse):
+    for p, part in enumerate(two_parts(gains)):
+        for q in range(4):
+            table_ref[32 * q : 32 * q + 32, 128 * p : 128 * p + 128] = part[
+                :, 128 * q : 128 * q + 128
+            ]
+
+
+def normal_block(part, at, data_ref, left_ref, right_ref, error_ref, sky_ref, inverse):
     lanes = pl.ds(at, SUB)
-    error = error_ref[0, :, lanes]
+    error = error_ref[part, :, lanes]
     square = error * error
     square = square + pltpu.roll(square, 4, axis=0)
-    flagged = data_ref[0, 8:12, lanes]
+    flagged = data_ref[part, 8:12, lanes]
     flagged = jnp.concatenate([flagged, flagged], axis=0)
     weight = flagged * (robust_dof + 1.0) / (robust_dof + square * inverse)
     scaled = weight * error
-    left = left_ref[0, :, lanes]
-    right = right_ref[0, :, lanes]
+    left = left_ref[part, :, lanes]
+    right = right_ref[part, :, lanes]
     first, second = [], []
     wide = lambda row: jnp.broadcast_to(row, (DIRS, SUB))
     for f in range(FEW):
@@ -342,8 +335,8 @@
         for t in range(TIMES):
             i = 2 * t + f
             y_re, y_im = wide(scaled[i : i + 1]), wide(scaled[4 + i : 5 + i])
-            sky_re = sky_ref[0, t, f, 0, :, lanes]
-            sky_im = sky_ref[0, t, f, 1, :, lanes]
+            sky_re = sky_ref[part, t, f, 0, :, lanes]
+            sky_im = sky_ref[part, t, f, 1, :, lanes]
             a = sky_re * y_re + sky_im * y_im
             b = sky_re * y_im - sky_im * y_re
             z_re, z_im = (a, b) if t == 0 else (z_re + a, z_im + b)
@@ -353,24 +346,29 @@
         first += [rr * z_re - ri * z_im, rr * z_im + ri * z_re, (rr * rr + ri * ri) * power]
         second += [lr * z_re + li * z_im, li * z_re - lr * z_im, (lr * lr + li * li) * power]
     made = []
-    for row, pieces in ((16, first), (17, second)):
-        station = jnp.broadcast_to(data_ref[0, row : row + 1, lanes], (8, SUB))
+    for side, pieces in ((0, first), (1, second)):
+        station = jnp.broadcast_to(data_ref[part, 16 + side : 17 + side, lanes], (8, SUB))
         half = jnp.where(station >= 256.0, 1.0, 0.0)
+        high = jnp.concatenate([half, half], axis=0).astype(BF16)
+        parts = two_parts(jnp.concatenate(pieces, axis=0))
+        upper = [p[i : i + 16] * high for p in parts for i in (0, 16, 32)]
         hot = one_hot(station - 256.0 * half, 256)
-        high = jnp.concatenate([half, half], axis=0).astype(BF16)
-        values = jnp.concatenate(pieces, axis=0)
-        parts = two_parts(values)
-        upper = [part[i : i + 16] * high for part in parts for i in (0, 16, 32)]
         made.append((jnp.concatenate(list(parts) + upper, axis=0), hot))
     return made
 
 
 def normal_runs(data_ref, left_ref, right_ref, error_ref, sky_ref, total_ref, inverse):
+    steps = LOCAL // SUB // NORMAL_RUNS
+    total_ref[...] = jnp.zeros_like(total_ref)
+
     def run(i, carry):
+        part, first = i // steps, (i % steps) * NORMAL_RUNS
         made = []
         for j in range(NORMAL_RUNS):
-            at = pl.multiple_of((i * NORMAL_RUNS + j) * SUB, SUB)
-            made += normal_block(data_ref, left_ref, right_ref, error_ref, sky_ref, at, inverse)
+            at = pl.multiple_of((first + j) * SUB, SUB)
+            made += normal_block(
+                part, at, data_ref, left_ref, right_ref, error_ref, sky_ref, inverse
+            )
         total_ref[...] += lax.dot_general(
             jnp.concatenate([m[0] for m in made], axis=1),
             jnp.concatenate([m[1] for m in made], axis=1),
@@ -379,7 +377,7 @@
         )
         return carry
 
-    lax.fori_loop(0, LOCAL // SUB // NORMAL_RUNS, run, 0)
+    lax.fori_loop(0, PARTS * steps, run, 0)
 
 
 def renew_gains(gains, anchor, total, columns):
@@ -403,6 +401,46 @@
     squares = jnp.sum(jnp.sum(squares_ref[...], axis=0, keepdims=True), axis=1, keepdims=True)
     count = jnp.sum(count_ref[...], axis=1, keepdims=True)
     return 1.0 / (squares / (count + 1.0) + small_term)
+
+
+def renewed(squares_ref, count_ref, data_ref, held, gains_ref, anchor_ref, geo_ref, total_ref):
+    normal_runs(data_ref, *held, total_ref, inverse_of(squares_ref, count_ref))
+    return renew_gains(gains_ref[...], anchor_ref[...], total_ref[...], geo_ref[...])
+
+
+def next_model(gains, data_ref, sky_ref, outs, misfit_out, table_ref):
+    build_table(table_ref, gains)
+    misfit = model_runs(data_ref, table_ref, sky_ref, outs, None)
+    misfit = jnp.sum(misfit[:, :128] + misfit[:, 128:], axis=0, keepdims=True)
+    misfit_out[...] = jnp.broadcast_to(misfit, misfit_out.shape)
+
+
+def first_kernel(
+    squares_ref,
+    count_ref,
+    data_ref,
+    gains_ref,
+    anchor_ref,
+    geo_ref,
+    gains_out,
+    left_out,
+    right_out,
+    error_out,
+    sky_out,
+    misfit_out,
+    table_ref,
+    total_ref,
+):
+    build_table(table_ref, gains_ref[...])
+    col = lambda i: geo_ref[:, i : i + 1]
+    geo = ((col(0), col(1)), (col(2), col(3)), (col(4), col(5)))
+    outs = (left_out, right_out, error_out)
+    model_runs(data_ref, table_ref, sky_out, outs, geo)
+    gains = renewed(
+        squares_ref, count_ref, data_ref, (*outs, sky_out), gains_ref, anchor_ref, geo_ref, total_ref
+    )
+    gains_out[...] = gains
+    next_model(gains, data_ref, sky_out, outs, misfit_out, table_ref)
 
 
 def middle_kernel(
@@ -423,46 +461,15 @@
     misfit_out,
     table_ref,
     total_ref,
-    misfit_ref,
 ):
-    phase, step = pl.program_id(0), pl.program_id(1)
-    last = pl.num_programs(1) - 1
-
-    @pl.when((phase == 0) & (step == 0))
-    def _():
-        total_ref[...] = jnp.zeros_like(total_ref)
-
-    @pl.when(phase == 0)
-    def _():
-        normal_runs(
-            data_ref, left_ref, right_ref, error_ref, sky_ref, total_ref,
-            inverse_of(squares_ref, count_ref),
-        )
-
-    @pl.when((phase == 0) & (step == last))
-    def _():
-        gains = renew_gains(gains_ref[...], anchor_ref[...], total_ref[...], geo_ref[...])
-        gains_out[...] = gains
-        build_table(table_ref, gains)
-
-    @pl.when(phase == 1)
-    def _():
-        misfit = model_runs(
-            data_ref, table_ref, sky_ref, None, (left_out, right_out, error_out, None)
-        )
-        misfit = jnp.sum(misfit[:, :128] + misfit[:, 128:], axis=0, keepdims=True)
-
-        @pl.when(step == 0)
-        def _():
-            misfit_ref[...] = misfit
-
-        @pl.when(step > 0)
-        def _():
-            misfit_ref[...] += misfit
-
-        @pl.when(step == last)
-        def _():
-            misfit_out[...] = jnp.broadcast_to(misfit_ref[...], misfit_out.shape)
+    held = (left_ref, right_ref, error_ref, sky_ref)
+    gains = renewed(
+        squares_ref, count_ref, data_ref, held, gains_ref, anchor_ref, geo_ref, total_ref
+    )
+    gains_out[...] = gains
+    next_model(
+        gains, data_ref, sky_ref, (left_out, right_out, error_out), misfit_out, table_ref
+    )
 
 
 def last_kernel(
@@ -479,88 +486,48 @@
     gains_out,
     total_ref,
 ):
-    step = pl.program_id(0)
-
-    @pl.when(step == 0)
-    def _():
-        total_ref[...] = jnp.zeros_like(total_ref)
-
-    normal_runs(
-        data_ref, left_ref, right_ref, error_ref, sky_ref, total_ref,
-        inverse_of(squares_ref, count_ref),
-    )
-
-    @pl.when(step == pl.num_programs(0) - 1)
-    def _():
-        gains_out[...] = renew_gains(
-            gains_ref[...], anchor_ref[...], total_ref[...], geo_ref[...]
-        )
+    held = (left_ref, right_ref, error_ref, sky_ref)
+    gains_out[...] = renewed(
+        squares_ref, count_ref, data_ref, held, gains_ref, anchor_ref, geo_ref, total_ref
+    )
 
 
 ROWS = 18
 GAIN_ROWS = 2 * FEW * DIRS
 SKY = (TIMES, FEW, 2, DIRS)
+GRANT = pltpu.CompilerParams(vmem_limit_bytes=8 * 1024 * 1024)
+ON_CHIP = pl.BlockSpec(memory_space=pltpu.VMEM)
 
 
 def shapes_of(rows):
     return jax.ShapeDtypeStruct((PARTS, rows, LOCAL), F32)
 
 
-def first_call(data, gains, geo):
-    at = lambda i: (i, 0, 0)
+def first_call(squares, count, data, gains, anchor, geo, devices):
     return pl.pallas_call(
         first_kernel,
-        grid=(PARTS,),
-        in_specs=[
-            pl.BlockSpec((1, ROWS, LOCAL), at),
-            pl.BlockSpec((GAIN_ROWS, STATIONS), lambda i: (0, 0)),
-            pl.BlockSpec((DIRS, 8), lambda i: (0, 0)),
-        ],
-        out_specs=[
-            pl.BlockSpec((1, GAIN_ROWS, LOCAL), at),
-            pl.BlockSpec((1, GAIN_ROWS, LOCAL), at),
-            pl.BlockSpec((1, 8, LOCAL), at),
-            pl.BlockSpec((1,) + SKY + (LOCAL,), lambda i: (i, 0, 0, 0, 0, 0)),
-        ],
+        in_specs=[ON_CHIP] * 6,
+        out_specs=[ON_CHIP] * 6,
         out_shape=[
+            jax.ShapeDtypeStruct((GAIN_ROWS, STATIONS), F32),
             shapes_of(GAIN_ROWS),
             shapes_of(GAIN_ROWS),
             shapes_of(8),
             jax.ShapeDtypeStruct((PARTS,) + SKY + (LOCAL,), F32),
+            jax.ShapeDtypeStruct((devices, 128), F32),
         ],
-        scratch_shapes=[pltpu.VMEM((128, 256), BF16)],
-        cost_estimate=lasts(10),
-        name="first_model",
-    )(data, gains, geo)
-
-
-def middle_call(squares, count, data, left, right, error, sky, gains, anchor, geo, devices):
-    at = lambda p, i: (i, 0, 0)
-    held = lambda p, i: ((1 - p) * i + p * (PARTS - 1), 0, 0)
-    made = lambda p, i: (p * i, 0, 0)
-    small = lambda p, i: (0, 0)
+        scratch_shapes=[pltpu.VMEM((128, 256), BF16), pltpu.VMEM((192, 256), F32)],
+        compiler_params=GRANT,
+        cost_estimate=lasts(18),
+        name="first_step",
+    )(squares, count, data, gains, anchor, geo)
+
+
+def middle_call(squares, count, data, held, gains, anchor, geo, devices):
     return pl.pallas_call(
         middle_kernel,
-        grid=(2, PARTS),
-        in_specs=[
-            pl.BlockSpec(squares.shape, small),
-            pl.BlockSpec((1, 128), small),
-            pl.BlockSpec((1, ROWS, LOCAL), at),
-            pl.BlockSpec((1, GAIN_ROWS, LOCAL), held),
-            pl.BlockSpec((1, GAIN_ROWS, LOCAL), held),
-            pl.BlockSpec((1, 8, LOCAL), held),
-            pl.BlockSpec((1,) + SKY + (LOCAL,), lambda p, i: (i, 0, 0, 0, 0, 0)),
-            pl.BlockSpec((GAIN_ROWS, STATIONS), small),
-            pl.BlockSpec((GAIN_ROWS, STATIONS), small),
-            pl.BlockSpec((DIRS, 8), small),
-        ],
-        out_specs=[
-            pl.BlockSpec((GAIN_ROWS, STATIONS), small),
-            pl.BlockSpec((1, GAIN_ROWS, LOCAL), made),
-            pl.BlockSpec((1, GAIN_ROWS, LOCAL), made),
-            pl.BlockSpec((1, 8, LOCAL), made),
-            pl.BlockSpec((devices, 128), small),
-        ],
+        in_specs=[ON_CHIP] * 10,
+        out_specs=[ON_CHIP] * 5,
         out_shape=[
             jax.ShapeDtypeStruct((GAIN_ROWS, STATIONS), F32),
             shapes_of(GAIN_ROWS),
@@ -568,40 +535,24 @@
             shapes_of(8),
             jax.ShapeDtypeStruct((devices, 128), F32),
         ],
-        scratch_shapes=[
-            pltpu.VMEM((128, 256), BF16),
-            pltpu.VMEM((192, 256), F32),
-            pltpu.VMEM((1, 128), F32),
-        ],
-        cost_estimate=lasts(20),
+        scratch_shapes=[pltpu.VMEM((128, 256), BF16), pltpu.VMEM((192, 256), F32)],
+        compiler_params=GRANT,
+        cost_estimate=lasts(14),
         name="normal_and_model",
-    )(squares, count, data, left, right, error, sky, gains, anchor, geo)
-
-
-def last_call(squares, count, data, left, right, error, sky, gains, anchor, geo):
-    at = lambda i: (i, 0, 0)
-    small = lambda i: (0, 0)
+    )(squares, count, data, *held, gains, anchor, geo)
+
+
+def last_call(squares, count, data, held, gains, anchor, geo):
     return pl.pallas_call(
         last_kernel,
-        grid=(PARTS,),
-        in_specs=[
-            pl.BlockSpec(squares.shape, small),
-            pl.BlockSpec((1, 128), small),
-            pl.BlockSpec((1, ROWS, LOCAL), at),
-            pl.BlockSpec((1, GAIN_ROWS, LOCAL), at),
-            pl.BlockSpec((1, GAIN_ROWS, LOCAL), at),
-            pl.BlockSpec((1, 8, LOCAL), at),
-            pl.BlockSpec((1,) + SKY + (LOCAL,), lambda i: (i, 0, 0, 0, 0, 0)),
-            pl.BlockSpec((GAIN_ROWS, STATIONS), small),
-            pl.BlockSpec((GAIN_ROWS, STATIONS), small),
-            pl.BlockSpec((DIRS, 8), small),
-        ],
-        out_specs=pl.BlockSpec((GAIN_ROWS, STATIONS), small),
+        in_specs=[ON_CHIP] * 10,
+        out_specs=ON_CHIP,
         out_shape=jax.ShapeDtypeStruct((GAIN_ROWS, STATIONS), F32),
         scratch_shapes=[pltpu.VMEM((192, 256), F32)],
-        cost_estimate=lasts(11),
+        compiler_params=GRANT,
+        cost_estimate=lasts(8),
         name="normal_last",
-    )(squares, count, data, left, right, error, sky, gains, anchor, geo)
+    )(squares, count, data, *held, gains, anchor, geo)
 
 
 def legendre(ratios):
@@ -673,12 +624,6 @@
     channels = channel_ratio.shape[0]
     rho = penalty * (2.0 * BASELINES * TIMES / STATIONS)
 
-    send = packed(
-        visibilities, sample_flag_weight, baseline_station_pair, baseline_spatial_coords
-    )
-    send = send.reshape(PARTS, ROWS * LOCAL // 128, 128)
-    data = lax.all_to_all(send, BL, 0, 0, tiled=True).reshape(PARTS, ROWS, LOCAL)
-
     wide = functools.partial(
         wide_model,
         vis=visibilities,
@@ -695,9 +640,15 @@
     flux = own_channels(source_flux, 1, own)
     basis = legendre(ratio)
     gram_own = (basis[:, None, :] * basis[None, :, :]).sum(-1)
-    sums, data = lax.optimization_barrier((sums, data))
     payload = jnp.concatenate([sums, jnp.pad(gram_own.reshape(1, 9), ((0, 0), (0, 119)))], axis=1)
     arrived = sent_to_all(payload, ALL)
+    send = packed(
+        visibilities, sample_flag_weight, baseline_station_pair, baseline_spatial_coords
+    )
+    arrived, send = lax.optimization_barrier(
+        (arrived, send.reshape(PARTS, ROWS * LOCAL // 128, 128))
+    )
+    data = lax.all_to_all(send, BL, 0, 0, tiled=True).reshape(PARTS, ROWS, LOCAL)
     arrived = arrived.sum(axis=0)
     squares, count = arrived[:, :128], arrived[:, 128:256]
     gram = arrived[0, 256:265].reshape(3, 3)
@@ -725,13 +676,18 @@
         axis=1,
     )
 
-    left, right, error, sky = first_call(data, gains, geo)
-    for iteration in range(ITERS - 1):
-        gains, left, right, error, misfit = middle_call(
-            squares, count, data, left, right, error, sky, gains, anchor, geo, devices
-        )
+    gains, left, right, error, sky, misfit = first_call(
+        squares, count, data, gains, anchor, geo, devices
+    )
+    for iteration in range(1, ITERS):
         squares = lax.all_to_all(misfit[:, None], ALL, 0, 0, tiled=True)[:, 0]
-    gains = last_call(squares, count, data, left, right, error, sky, gains, anchor, geo)
+        held = (left, right, error, sky)
+        if iteration + 1 < ITERS:
+            gains, left, right, error, misfit = middle_call(
+                squares, count, data, held, gains, anchor, geo, devices
+            )
+        else:
+            gains = last_call(squares, count, data, held, gains, anchor, geo)
 
     gathered = sent_to_all(gains.reshape(GAIN_ROWS * STATIONS // 128, 128), BL)
     new_gains = (

time: 189 us -> 171 us (0.905)
  Pallas kernels: 79.6 us -> 53.7 us
  waiting for transfers between devices: 19.6 us -> 34.9 us
  blocking collectives: 35.1 us -> 27.7 us
    pallas_call x4 -> x3, Pallas kernels: 62.8 us -> 39.3 us  [the longest x1 18.4 us: first_call(): pl.pallas_call(first_kernel, in_specs=[ON_CHIP] * 6, out_specs=[ON_CHIP]...]
    all_to_all x1, waiting for transfers between devices: 8.2 us -> 16 us  [body(): lax.all_to_all(send, BL, 0, 0, tiled=True).reshape(PARTS, ROWS, LOCAL)]
    all_to_all x3, waiting for transfers between devices: 8.45 us -> 15.9 us  [sent_to_all(): lax.all_to_all(jnp.broadcast_to(array[None], (count, *array.shape)), axes...]
    all_to_all x2, blocking collectives: 35.1 us -> 27.7 us  [body(): squares = lax.all_to_all(misfit[:, None], ALL, 0, 0, tiled=True)[:, 0]]
    unnamed x22 -> x42, local copies, waits for them, and re-layouts: 2.98 us -> 8.72 us
    all_to_all x3, starting transfers between devices: 16.6 us -> 19.3 us  [sent_to_all(): lax.all_to_all(jnp.broadcast_to(array[None], (count, *array.shape)), axes...]
    pallas_call x2, Pallas kernels: 16.8 us -> 14.4 us  [wide_model(): pl.pallas_call(functools.partial(wide_kernel, residual_out=residual_out,...]
  transfers between devices with their start and end apart: 5 -> 5, of which waited for: 3 -> 4; matrix products, arithmetic and copies ran while one was open for 3% -> 3% of each run, Pallas kernels for 14% -> 4%
where the time goes in v3:
time: 171 us
  Pallas kernels  53.7 us (31%)
  waiting for transfers between devices  34.9 us (20%)
  starting transfers between devices  28.6 us (17%)
  blocking collectives  27.7 us (16%)
  local copies, waits for them, and re-layouts  17.9 us (10%)
  between operations  5.07 us (3%)
  other arithmetic  2.72 us (2%)
    all_to_all x2, blocking collectives, body(): squares = lax.all_to_all(misfit[:, None], ALL, 0, 0, tiled=True)[:, 0]  27.7 us
    all_to_all x3, starting transfers between devices, sent_to_all(): lax.all_to_all(jnp.broadcast_to(array[None], (count, *array.shape)), axes...  19.3 us
    pallas_call x1, Pallas kernels, first_call(): pl.pallas_call(first_kernel, in_specs=[ON_CHIP] * 6, out_specs=[ON_CHIP]...  18.4 us
    all_to_all x1, waiting for transfers between devices, body(): lax.all_to_all(send, BL, 0, 0, tiled=True).reshape(PARTS, ROWS, LOCAL)  16 us
    all_to_all x3, waiting for transfers between devices, sent_to_all(): lax.all_to_all(jnp.broadcast_to(array[None], (count, *array.shape)), axes...  15.9 us
    pallas_call x2, Pallas kernels, wide_model(): pl.pallas_call(functools.partial(wide_kernel, residual_out=residual_out,...  14.4 us
    pallas_call x1, Pallas kernels, middle_call(): pl.pallas_call(middle_kernel, in_specs=[ON_CHIP] * 10, out_specs=[ON_CHIP...  12.5 us
    unnamed x42, local copies, waits for them, and re-layouts  8.72 us
  transfers between devices with their start and end apart: 5, of which 4 were waited for; matrix products, arithmetic and copies ran while one was open for 3% of the time, Pallas kernels for 4%

profile of v3, /device:TPU:1, one launch (start us, length us, event | category | flops | bytes accessed | tf_op | source)
XLA Modules:
  0.0 170.5 jit_solution(8618064285424903557)
XLA Ops:
  1.8 1.0 copy-done
  2.8 0.9 copy-done.2
  3.8 1.0 copy-done.5
  8.3 7.0 %wide_misfit.1 = f32[1,256]{1,0:T(1,128)S(1)} custom-call(f32[256,512]{1,0:T(8,128)S(1)} %bitcast.60, f32[2,2,16,2048]{3,2,1,0:T(8,128)S(1)} %copy-done, s32[2,16,2048]{2,1,0:T(8,128)S(1)} %copy-done.2, s32[2,2048]{1,0:T(2,128)S(1)} %copy-done.8, f32[2,2,2048]{2,1,0:T(2,128)S(1)} %copy-done.6, f32[2,8]{1,0:T(2,128)S(1)} %copy-done.12, ...), custom_call_target="tpu_custom_call" | custom-call | flops 32000000 | bytes 1048576 | tf_op jit(solution)/shard_map/wide_misfit/pallas_call | solution.py:185
  16.1 11.5 %all-to-all-start = ((f32[128,1,384]{2,1,0:T(1,128)}), f32[128,1,384]{2,1,0:T(1,128)S(1)}, u32[]{:S(2)}, u32[]{:S(2)}) async-start(f32[128,1,384]{2,1,0:T(1,128)} %broadcast_in_dim.25), calls=%async_computation | async-start | bytes 393216 | tf_op jit(solution)/shard_map/all_to_all | solution.py:567
  29.6 1.2 reshape.81
  30.8 7.3 %all-to-all-done = f32[128,1,384]{2,1,0:T(1,128)S(1)} async-done(((f32[128,1,384]{2,1,0:T(1,128)}), f32[128,1,384]{2,1,0:T(1,128)S(1)}, u32[]{:S(2)}, u32[]{:S(2)}) %all-to-all-start) | async-done | bytes 196640 | tf_op jit(solution)/shard_map/all_to_all | solution.py:567
  38.1 4.3 %all-to-all-start.1 = ((f32[8,288,128]{2,1,0:T(8,128)}), f32[8,288,128]{2,1,0:T(8,128)}, u32[]{:S(2)}, u32[]{:S(2)}) async-start(f32[8,288,128]{2,1,0:T(8,128)} %reshape.81), calls=%async_computation.1 | async-start | bytes 2359296 | tf_op jit(solution)/shard_map/all_to_all | solution.py:651
  42.4 1.0 dynamic-slice_bitcast_fusion
  44.1 16.0 %all-to-all-done.1 = f32[8,288,128]{2,1,0:T(8,128)} async-done(((f32[8,288,128]{2,1,0:T(8,128)}), f32[8,288,128]{2,1,0:T(8,128)}, u32[]{:S(2)}, u32[]{:S(2)}) %all-to-all-start.1) | async-done | bytes 1179680 | tf_op jit(solution)/shard_map/all_to_all | solution.py:651
  60.2 1.4 reshape.82.data_ref
  61.6 18.4 %first_step.1 = (f32[32,512]{1,0:T(8,128)S(1)}, f32[8,32,2048]{2,1,0:T(8,128)S(1)}, f32[8,32,2048]{2,1,0:T(8,128)S(1)}, f32[8,8,2048]{2,1,0:T(8,128)S(1)}, f32[8...) custom-call(f32[1,128]{1,0:T(1,128)S(1)} %get-tuple-element.70.squares_ref, ...), custom_call_target="tpu_custom_call" | custom-call | flops 72000000 | bytes 1048576 | tf_op jit(solution)/shard_map/first_step/pallas_call | solution.py:507
  80.0 14.0 %all_to_all.35 = f32[128,1,128]{2,1,0:T(1,128)S(1)} all-to-all(f32[128,1,128]{2,1,0:T(1,128)S(1)} %bitcast.65), channel_id=1, replica_groups=mesh['bl_0'=4,'bl_1'=2,'freq_0'=4,'freq_1'=2,'freq_2'=2] {'bl_0','bl_1',..., dimensions={0} | all-to-all | bytes 131072 | tf_op jit(solution)/shard_map/all_to_all | solution.py:683
  94.0 12.5 %normal_and_model.1 = (f32[32,512]{1,0:T(8,128)S(1)}, f32[8,32,2048]{2,1,0:T(8,128)S(1)}, f32[8,32,2048]{2,1,0:T(8,128)S(1)}, f32[8,8,2048]{2,1,0:T(8,128)S(1)}, f32[128,128]{1,0:T(8,128)S(1)}) custom-call(f32[128,128]{1,0:T(8,128)S(1)} %bitcast.61, f32[1,128]{1,0:T(1,128)S(1)} %get-tuple-element.69.count_ref, f32[8,18,2048]{2,1,0:T(8,128)S(1)} %reshape.82.data_ref, ...), custom_call_target="tpu_custom_call" | custom-call | flops 56000000 | bytes 1048576 | tf_op jit(solution)/shard_map/normal_and_model/pallas_call | solution.py:527
  106.5 13.7 %all_to_all.36 = f32[128,1,128]{2,1,0:T(1,128)S(1)} all-to-all(f32[128,1,128]{2,1,0:T(1,128)S(1)} %bitcast.64), channel_id=1, replica_groups=mesh['bl_0'=4,'bl_1'=2,'freq_0'=4,'freq_1'=2,'freq_2'=2] {'bl_0','bl_1',..., dimensions={0} | all-to-all | bytes 131072 | tf_op jit(solution)/shard_map/all_to_all | solution.py:683
  120.2 8.4 %normal_last.1 = f32[32,512]{1,0:T(8,128)S(1)} custom-call(f32[128,128]{1,0:T(8,128)S(1)} %bitcast.62, f32[1,128]{1,0:T(1,128)S(1)} %get-tuple-element.69.count_ref, f32[8,18,2048]{2,1,0:T(8,128)S(1)} %reshape.82.data_ref, f32[8,32,2048]{2,1,0:T(8,128)S(1)} %get-tuple-element.26.left_ref, f32[8,32,2048]{2,1,0:T(8,128)S(1)} %get-tuple-element.27.right_ref, ...), custom_call_target="tpu_custom_call" | custom-call | flops 32000000 | bytes 1048576 | tf_op jit(solution)/shard_map/normal_last/pallas_call | solution.py:546
  128.7 0.8 broadcast_in_dim.61
  129.5 3.5 %all-to-all-start.4 = ((f32[8,128,128]{2,1,0:T(8,128)}), f32[8,128,128]{2,1,0:T(8,128)S(1)}, u32[]{:S(2)}, u32[]{:S(2)}) async-start(f32[8,128,128]{2,1,0:T(8,128)} %broadcast_in_dim.61), calls=%async_computation.4 | async-start | bytes 1048576 | tf_op jit(solution)/shard_map/all_to_all | solution.py:567
  133.1 8.5 %all-to-all-done.4 = f32[8,128,128]{2,1,0:T(8,128)S(1)} async-done(((f32[8,128,128]{2,1,0:T(8,128)}), f32[8,128,128]{2,1,0:T(8,128)S(1)}, u32[]{:S(2)}, u32[]{:S(2)}) %all-to-all-start.4) | async-done | bytes 524320 | tf_op jit(solution)/shard_map/all_to_all | solution.py:567
  142.9 5.0 %all-to-all-start.5 = ((f32[16,3,512]{2,1,0:T(4,128)}), f32[16,3,512]{2,1,0:T(4,128)S(1)}, u32[]{:S(2)}, u32[]{:S(2)}) async-start(f32[16,3,512]{2,1,0:T(4,128)} %pad_maximum_fusion.1), calls=%async_computation.5 | async-start | bytes 262144 | tf_op jit(solution)/shard_map/all_to_all | solution.py:708
  152.7 3.0 %all-to-all-done.5 = f32[16,3,512]{2,1,0:T(4,128)S(1)} async-done(((f32[16,3,512]{2,1,0:T(4,128)}), f32[16,3,512]{2,1,0:T(4,128)S(1)}, u32[]{:S(2)}, u32[]{:S(2)}) %all-to-all-start.5) | async-done | bytes 98336 | tf_op jit(solution)/shard_map/all_to_all | solution.py:708
  156.4 4.3 %all-to-all-start.6 = ((f32[16,3,512]{2,1,0:T(4,128)}), f32[16,3,512]{2,1,0:T(4,128)S(1)}, u32[]{:S(2)}, u32[]{:S(2)}) async-start(f32[16,3,512]{2,1,0:T(4,128)} %broadcast_in_dim.62), calls=%async_computation.6 | async-start | bytes 262144 | tf_op jit(solution)/shard_map/all_to_all | solution.py:567
  161.1 7.5 %wide_residual.1 = f32[2,2,16,2048]{3,2,1,0:T(8,128)} custom-call(f32[256,512]{1,0:T(8,128)S(1)} %bitcast.56, f32[2,2,16,2048]{3,2,1,0:T(8,128)S(1)} %copy-done.1, s32[2,16,2048]{2,1,0:T(8,128)S(1)} %copy-done.3, s32[2,2048]{1,0:T(2,128)S(1)} %copy-done.9, f32[2,2,2048]{2,1,0:T(2,128)S(1)} %copy-done.7, f32[2,8]{1,0:T(2,128)S(1)} %copy-done.13, ...), custom_call_target="tpu_custom_call" | custom-call | flops 32000000 | bytes 1048576 | tf_op jit(solution)/shard_map/wide_residual/pallas_call | solution.py:185
  169.4 1.1 copy.74
  (91 shorter events, 12.0 us)
Async XLA Ops:
  0.6 26.9 %copy-start.9 = (s32[2,2048]{1,0:T(2,128)S(1)}, s32[2,2048]{1,0:T(2,128)}, u32[]{:S(2)}) copy-start(s32[2,2048]{1,0:T(2,128)} %pair_ref.3) | copy-start | bytes 49156
  0.6 26.9 %copy-start.7 = (f32[2,2,2048]{2,1,0:T(2,128)S(1)}, f32[2,2,2048]{2,1,0:T(2,128)}, u32[]{:S(2)}) copy-start(f32[2,2,2048]{2,1,0:T(2,128)} %coord_ref.3) | copy-start | bytes 98308
  1.8 1.0 copy-start
  2.8 0.9 copy-start.2
  3.7 1.0 copy-start.5
  4.8 0.8 copy-start.6
  5.5 0.7 copy-start.8
  6.3 0.7 copy-start.10
  7.0 0.7 copy-start.12
  7.6 0.7 copy-start.14
  8.3 19.3 %copy-start.3 = (s32[2,16,2048]{2,1,0:T(8,128)S(1)}, s32[2,16,2048]{2,1,0:T(8,128)}, u32[]{:S(2)}) copy-start(s32[2,16,2048]{2,1,0:T(8,128)} %flag_ref.3) | copy-start | bytes 786436
  8.3 19.4 %copy-start.1 = (f32[2,2,16,2048]{3,2,1,0:T(8,128)S(1)}, f32[2,2,16,2048]{3,2,1,0:T(8,128)}, u32[]{:S(2)}) copy-start(f32[2,2,16,2048]{3,2,1,0:T(8,128)} %vis_ref.3) | copy-start | bytes 1572868
  16.1 22.1 %all-to-all-start = ((f32[128,1,384]{2,1,0:T(1,128)}), f32[128,1,384]{2,1,0:T(1,128)S(1)}, u32[]{:S(2)}, u32[]{:S(2)}) async-start(f32[128,1,384]{2,1,0:T(1,128)} %broadcast_in_dim.25), calls=%async_computation | async-start | bytes 393216 | tf_op jit(solution)/shard_map/all_to_all | solution.py:567
  30.8 12.6 %copy-start.13 = (f32[2,8]{1,0:T(2,128)S(1)}, f32[2,8]{1,0:T(2,128)}, u32[]{:S(2)}) copy-start(f32[2,8]{1,0:T(2,128)} %dirs_ref.3) | copy-start | bytes 196
  30.8 12.7 %copy-start.17 = (f32[2,3,8,512]{3,2,1,0:T(8,128)S(1)}, f32[2,3,8,512]{3,2,1,0:T(8,128)}, u32[]{:S(2)}) copy-start(f32[2,3,8,512]{3,2,1,0:T(8,128)} %param.20) | copy-start | bytes 294916
  30.8 12.8 %copy-start.16 = (f32[2,8,16,512]{3,2,1,0:T(8,128)S(1)}, f32[2,8,16,512]{3,2,1,0:T(8,128)}, u32[]{:S(2)}) copy-start(f32[2,8,16,512]{3,2,1,0:T(8,128)} %param.19) | copy-start | bytes 1572868
  30.8 12.9 %copy-start.18 = (f32[8]{0:T(128)S(1)}, f32[8]{0:T(128)}, u32[]{:S(2)}) copy-start(f32[8]{0:T(128)} %param.21) | copy-start | bytes 100
  30.8 13.0 %copy-start.11 = (f32[8,16]{1,0:T(8,128)S(1)}, f32[8,16]{1,0:T(8,128)}, u32[]{:S(2)}) copy-start(f32[8,16]{1,0:T(8,128)} %flux_ref.3) | copy-start | bytes 1540
  38.1 22.0 %all-to-all-start.1 = ((f32[8,288,128]{2,1,0:T(8,128)}), f32[8,288,128]{2,1,0:T(8,128)}, u32[]{:S(2)}, u32[]{:S(2)}) async-start(f32[8,288,128]{2,1,0:T(8,128)} %reshape.81), calls=%async_computation.1 | async-start | bytes 2359296 | tf_op jit(solution)/shard_map/all_to_all | solution.py:651
  128.6 4.4 %copy-start.15 = (f32[16]{0:T(128)S(1)}, f32[16]{0:T(128)}, u32[]{:S(2)}) copy-start(f32[16]{0:T(128)} %param.17) | copy-start | bytes 196
  129.5 12.1 %all-to-all-start.4 = ((f32[8,128,128]{2,1,0:T(8,128)}), f32[8,128,128]{2,1,0:T(8,128)S(1)}, u32[]{:S(2)}, u32[]{:S(2)}) async-start(f32[8,128,128]{2,1,0:T(8,128)} %broadcast_in_dim.61), calls=%async_computation.4 | async-start | bytes 1048576 | tf_op jit(solution)/shard_map/all_to_all | solution.py:567
  142.9 12.7 %all-to-all-start.5 = ((f32[16,3,512]{2,1,0:T(4,128)}), f32[16,3,512]{2,1,0:T(4,128)S(1)}, u32[]{:S(2)}, u32[]{:S(2)}) async-start(f32[16,3,512]{2,1,0:T(4,128)} %pad_maximum_fusion.1), calls=%async_computation.5 | async-start | bytes 262144 | tf_op jit(solution)/shard_map/all_to_all | solution.py:708
  156.4 12.1 %all-to-all-start.6 = ((f32[16,3,512]{2,1,0:T(4,128)}), f32[16,3,512]{2,1,0:T(4,128)S(1)}, u32[]{:S(2)}, u32[]{:S(2)}) async-start(f32[16,3,512]{2,1,0:T(4,128)} %broadcast_in_dim.62), calls=%async_computation.6 | async-start | bytes 262144 | tf_op jit(solution)/shard_map/all_to_all | solution.py:567
  161.1 8.2 %copy-start.4 = (f32[2,8,16,512]{3,2,1,0:T(8,128)}, f32[2,8,16,512]{3,2,1,0:T(8,128)S(1)}, u32[]{:S(2)}) copy-start(f32[2,8,16,512]{3,2,1,0:T(8,128)S(1)} %copy.72) | copy-start | bytes 1572868

commit v4 on v3

--- a/solution.py
+++ b/solution.py
@@ -57,6 +57,13 @@
 BF16 = jnp.bfloat16
 
 
+def legendre(ratios):
+    scaled = (ratios - 1.05) / 0.35
+    values = [jnp.ones_like(scaled), scaled]
+    values.append((3 * scaled * values[1] - 1 * values[0]) / 2)
+    return values[:NPOLY]
+
+
 def horner(terms, w):
     value = jnp.full_like(w, terms[-1])
     for term in terms[-2::-1]:
@@ -93,7 +100,8 @@
     channels,
     block,
 ):
-    outs, (high_ref, low_ref, left_ref, right_ref, column_ref) = rest[:-5], rest[-5:]
+    outs, rest = rest[:1], rest[1:]
+    high_ref, low_ref, left_ref, right_ref, column_ref, held_ref = rest
     step = pl.program_id(0)
 
     @pl.when(step == 0)
@@ -156,20 +164,30 @@
                 for c in range(0, block, 128):
                     misfit += part[r : r + 8, c : c + 128]
                     count += flagged[r : r + 8, c : c + 128]
-        sums = jnp.concatenate(
-            [jnp.sum(misfit, axis=0, keepdims=True), jnp.sum(count, axis=0, keepdims=True)], axis=1
-        )
+        step_sums = jnp.concatenate([misfit, count], axis=0)
 
         @pl.when(step == 0)
         def _():
-            sums_ref[...] = sums
+            held_ref[...] = step_sums
 
         @pl.when(step > 0)
         def _():
-            sums_ref[...] += sums
-
-
-def wide_model(gains, vis, flags, pairs, coords, directions, flux, ratio, residual_out):
+            held_ref[...] += step_sums
+
+        @pl.when(step == pl.num_programs(0) - 1)
+        def _():
+            full = lambda x: jnp.sum(jnp.sum(x, axis=0, keepdims=True), axis=1, keepdims=True)
+            basis = legendre(ratio_ref[...])
+            entries = [full(held_ref[0:8, :]), full(held_ref[8:16, :])]
+            entries += [full(basis[i] * basis[j]) for i in range(NPOLY) for j in range(i + 1)]
+            lane = lax.broadcasted_iota(jnp.int32, (8, 128), 1)
+            row = jnp.zeros((8, 128), F32)
+            for i, entry in enumerate(entries):
+                row = jnp.where(lane == i, jnp.broadcast_to(entry, (8, 128)), row)
+            sums_ref[...] = jnp.broadcast_to(row[0:1], sums_ref.shape)
+
+
+def wide_model(gains, vis, flags, pairs, coords, directions, flux, ratio, residual_out, devices=None):
     channels = vis.shape[2]
     count = vis.shape[3]
     block = SUB
@@ -180,8 +198,8 @@
         out_shape = jax.ShapeDtypeStruct(vis.shape, F32)
         out_spec = vis_spec
     else:
-        out_shape = jax.ShapeDtypeStruct((1, 256), F32)
-        out_spec = whole((1, 256))
+        out_shape = jax.ShapeDtypeStruct((devices, 128), F32)
+        out_spec = whole((devices, 128))
     return pl.pallas_call(
         functools.partial(
             wide_kernel, residual_out=residual_out, channels=channels, block=block
@@ -205,9 +223,9 @@
             pltpu.VMEM((rows, block), F32),
             pltpu.VMEM((rows, block), F32),
             pltpu.VMEM(((DIRS + 1) * channels, 128), F32),
+            pltpu.VMEM((16, 128), F32),
         ],
         cost_estimate=lasts(8),
-        compiler_params=pltpu.CompilerParams(vmem_limit_bytes=16 * 1024 * 1024),
         name="wide_residual" if residual_out else "wide_misfit",
     )(gains, vis, flags, pairs, coords, directions, flux, ratio.reshape(1, -1))
 
@@ -398,12 +416,16 @@
 
 
 def inverse_of(squares_ref, count_ref):
-    squares = jnp.sum(jnp.sum(squares_ref[...], axis=0, keepdims=True), axis=1, keepdims=True)
-    count = jnp.sum(count_ref[...], axis=1, keepdims=True)
-    return 1.0 / (squares / (count + 1.0) + small_term)
-
-
-def renewed(squares_ref, count_ref, data_ref, held, gains_ref, anchor_ref, geo_ref, total_ref):
+    squares = jnp.sum(squares_ref[...], axis=0, keepdims=True)
+    count = jnp.sum(count_ref[...], axis=0, keepdims=True)
+    lane = lax.broadcasted_iota(jnp.int32, (1, 128), 1)
+    pick = lambda row, i: jnp.sum(jnp.where(lane == i, row, 0.0), axis=1, keepdims=True)
+    return 1.0 / (pick(squares, 0) / (pick(count, 1) + 1.0) + small_term)
+
+
+def renewed(
+    squares_ref, count_ref, data_ref, held, gains_ref, anchor_ref, geo_ref, total_ref
+):
     normal_runs(data_ref, *held, total_ref, inverse_of(squares_ref, count_ref))
     return renew_gains(gains_ref[...], anchor_ref[...], total_ref[...], geo_ref[...])
 
@@ -412,35 +434,17 @@
     build_table(table_ref, gains)
     misfit = model_runs(data_ref, table_ref, sky_ref, outs, None)
     misfit = jnp.sum(misfit[:, :128] + misfit[:, 128:], axis=0, keepdims=True)
+    misfit = jnp.sum(misfit, axis=1, keepdims=True)
     misfit_out[...] = jnp.broadcast_to(misfit, misfit_out.shape)
 
 
 def first_kernel(
-    squares_ref,
-    count_ref,
-    data_ref,
-    gains_ref,
-    anchor_ref,
-    geo_ref,
-    gains_out,
-    left_out,
-    right_out,
-    error_out,
-    sky_out,
-    misfit_out,
-    table_ref,
-    total_ref,
+    data_ref, gains_ref, geo_ref, left_out, right_out, error_out, sky_out, table_ref
 ):
     build_table(table_ref, gains_ref[...])
     col = lambda i: geo_ref[:, i : i + 1]
     geo = ((col(0), col(1)), (col(2), col(3)), (col(4), col(5)))
-    outs = (left_out, right_out, error_out)
-    model_runs(data_ref, table_ref, sky_out, outs, geo)
-    gains = renewed(
-        squares_ref, count_ref, data_ref, (*outs, sky_out), gains_ref, anchor_ref, geo_ref, total_ref
-    )
-    gains_out[...] = gains
-    next_model(gains, data_ref, sky_out, outs, misfit_out, table_ref)
+    model_runs(data_ref, table_ref, sky_out, (left_out, right_out, error_out), geo)
 
 
 def middle_kernel(
@@ -503,24 +507,26 @@
     return jax.ShapeDtypeStruct((PARTS, rows, LOCAL), F32)
 
 
-def first_call(squares, count, data, gains, anchor, geo, devices):
+def held_shapes():
+    return [
+        shapes_of(GAIN_ROWS),
+        shapes_of(GAIN_ROWS),
+        shapes_of(8),
+        jax.ShapeDtypeStruct((PARTS,) + SKY + (LOCAL,), F32),
+    ]
+
+
+def first_call(data, gains, geo):
     return pl.pallas_call(
         first_kernel,
-        in_specs=[ON_CHIP] * 6,
-        out_specs=[ON_CHIP] * 6,
-        out_shape=[
-            jax.ShapeDtypeStruct((GAIN_ROWS, STATIONS), F32),
-            shapes_of(GAIN_ROWS),
-            shapes_of(GAIN_ROWS),
-            shapes_of(8),
-            jax.ShapeDtypeStruct((PARTS,) + SKY + (LOCAL,), F32),
-            jax.ShapeDtypeStruct((devices, 128), F32),
-        ],
-        scratch_shapes=[pltpu.VMEM((128, 256), BF16), pltpu.VMEM((192, 256), F32)],
+        in_specs=[ON_CHIP] * 3,
+        out_specs=[ON_CHIP] * 4,
+        out_shape=held_shapes(),
+        scratch_shapes=[pltpu.VMEM((128, 256), BF16)],
         compiler_params=GRANT,
-        cost_estimate=lasts(18),
-        name="first_step",
-    )(squares, count, data, gains, anchor, geo)
+        cost_estimate=lasts(6),
+        name="first_model",
+    )(data, gains, geo)
 
 
 def middle_call(squares, count, data, held, gains, anchor, geo, devices):
@@ -555,13 +561,6 @@
     )(squares, count, data, *held, gains, anchor, geo)
 
 
-def legendre(ratios):
-    scaled = (ratios - 1.05) / 0.35
-    values = [jnp.ones_like(scaled), scaled]
-    values.append((3 * scaled * values[1] - 1 * values[0]) / 2)
-    return jnp.stack(values[:NPOLY])
-
-
 def sent_to_all(array, axes):
     count = lax.axis_size(axes)
     return lax.all_to_all(
@@ -574,7 +573,7 @@
     factor = [[None] * order for _ in range(order)]
     for i in range(order):
         for j in range(i + 1):
-            value = gram[i, j]
+            value = gram[i][j]
             for m in range(j):
                 value = value - factor[i][m] * factor[j][m]
             factor[i][j] = jnp.sqrt(value) if i == j else value / factor[j][j]
@@ -634,24 +633,20 @@
         flux=source_flux,
         ratio=channel_ratio,
     )
-    sums = wide(jones_gains.reshape(-1, STATIONS), residual_out=False)
+    payload = wide(jones_gains.reshape(-1, STATIONS), residual_out=False, devices=devices)
+    send = packed(
+        visibilities, sample_flag_weight, baseline_station_pair, baseline_spatial_coords
+    )
+    send = send.reshape(PARTS, ROWS * LOCAL // 128, 128)
+    data = lax.all_to_all(send, BL, 0, 0, tiled=True).reshape(PARTS, ROWS, LOCAL)
+    payload, data = lax.optimization_barrier((payload, data))
+    arrived = lax.all_to_all(payload[:, None], ALL, 0, 0, tiled=True)[:, 0]
 
     ratio = own_channels(channel_ratio, 0, own)
     flux = own_channels(source_flux, 1, own)
     basis = legendre(ratio)
-    gram_own = (basis[:, None, :] * basis[None, :, :]).sum(-1)
-    payload = jnp.concatenate([sums, jnp.pad(gram_own.reshape(1, 9), ((0, 0), (0, 119)))], axis=1)
-    arrived = sent_to_all(payload, ALL)
-    send = packed(
-        visibilities, sample_flag_weight, baseline_station_pair, baseline_spatial_coords
-    )
-    arrived, send = lax.optimization_barrier(
-        (arrived, send.reshape(PARTS, ROWS * LOCAL // 128, 128))
-    )
-    data = lax.all_to_all(send, BL, 0, 0, tiled=True).reshape(PARTS, ROWS, LOCAL)
-    arrived = arrived.sum(axis=0)
-    squares, count = arrived[:, :128], arrived[:, 128:256]
-    gram = arrived[0, 256:265].reshape(3, 3)
+    sums = arrived.sum(axis=0) / lax.axis_size(BL)
+    gram = [[sums[2 + i * (i + 1) // 2 + j] for j in range(i + 1)] for i in range(NPOLY)]
 
     def rows_of(array):
         part = own_channels(array, 2, own)
@@ -676,18 +671,14 @@
         axis=1,
     )
 
-    gains, left, right, error, sky, misfit = first_call(
-        squares, count, data, gains, anchor, geo, devices
-    )
-    for iteration in range(1, ITERS):
+    left, right, error, sky = first_call(data, gains, geo)
+    squares = arrived
+    for iteration in range(ITERS - 1):
+        gains, left, right, error, misfit = middle_call(
+            squares, arrived, data, (left, right, error, sky), gains, anchor, geo, devices
+        )
         squares = lax.all_to_all(misfit[:, None], ALL, 0, 0, tiled=True)[:, 0]
-        held = (left, right, error, sky)
-        if iteration + 1 < ITERS:
-            gains, left, right, error, misfit = middle_call(
-                squares, count, data, held, gains, anchor, geo, devices
-            )
-        else:
-            gains = last_call(squares, count, data, held, gains, anchor, geo)
+    gains = last_call(squares, arrived, data, (left, right, error, sky), gains, anchor, geo)
 
     gathered = sent_to_all(gains.reshape(GAIN_ROWS * STATIONS // 128, 128), BL)
     new_gains = (

time: 171 us -> 165 us (0.965)
  waiting for transfers between devices: 34.9 us -> 18.8 us
  blocking collectives: 27.7 us -> 32.9 us
  local copies, waits for them, and re-layouts: 17.9 us -> 20.9 us
  Pallas kernels: 53.7 us -> 56.5 us
    pallas_call x1 -> x2, Pallas kernels: 12.5 us -> 25.2 us  [middle_call(): pl.pallas_call(middle_kernel, in_specs=[ON_CHIP] * 10, out_specs=[ON_CHIP...]
    pallas_call x1, Pallas kernels: 18.4 us -> 5.87 us  [first_call(): pl.pallas_call(first_kernel, in_specs=[ON_CHIP] * 3, out_specs=[ON_CHIP]...]
    all_to_all x3 -> x2, starting transfers between devices: 19.3 us -> 7.84 us  [sent_to_all(): lax.all_to_all(jnp.broadcast_to(array[None], (count, *array.shape)), axes...]
    all_to_all x0 -> x1, starting transfers between devices: none -> 8.81 us  [body(): arrived = lax.all_to_all(payload[:, None], ALL, 0, 0, tiled=True)[:, 0]]
    all_to_all x1, waiting for transfers between devices: 16 us -> 7.35 us  [body(): lax.all_to_all(send, BL, 0, 0, tiled=True).reshape(PARTS, ROWS, LOCAL)]
    all_to_all x3 -> x2, waiting for transfers between devices: 15.9 us -> 8.46 us  [sent_to_all(): lax.all_to_all(jnp.broadcast_to(array[None], (count, *array.shape)), axes...]
    all_to_all x2, blocking collectives: 27.7 us -> 32.9 us  [body(): squares = lax.all_to_all(misfit[:, None], ALL, 0, 0, tiled=True)[:, 0]]
    unnamed x42 -> x38, local copies, waits for them, and re-layouts: 8.72 us -> 13 us
  transfers between devices with their start and end apart: 5 -> 5, of which waited for: 4 -> 3; matrix products, arithmetic and copies ran while one was open for 3% -> 2% of each run, Pallas kernels for 4% -> 14%
where the time goes in v4:
time: 165 us; the launch traced here: 164 us
  Pallas kernels  56.5 us (34%)
  blocking collectives  32.9 us (20%)
  starting transfers between devices  27.7 us (17%)
  local copies, waits for them, and re-layouts  20.9 us (13%)
  waiting for transfers between devices  18.8 us (11%)
  between operations  5.06 us (3%)
  other arithmetic  1.84 us (1%)
    all_to_all x2, blocking collectives, body(): squares = lax.all_to_all(misfit[:, None], ALL, 0, 0, tiled=True)[:, 0]  32.9 us
    pallas_call x2, Pallas kernels, middle_call(): pl.pallas_call(middle_kernel, in_specs=[ON_CHIP] * 10, out_specs=[ON_CHIP...  25.2 us
    pallas_call x2, Pallas kernels, wide_model(): pl.pallas_call(functools.partial(wide_kernel, residual_out=residual_out,...  17 us
    unnamed x38, local copies, waits for them, and re-layouts  13 us
    all_to_all x1, starting transfers between devices, body(): arrived = lax.all_to_all(payload[:, None], ALL, 0, 0, tiled=True)[:, 0]  8.81 us
    all_to_all x2, waiting for transfers between devices, sent_to_all(): lax.all_to_all(jnp.broadcast_to(array[None], (count, *array.shape)), axes...  8.46 us
    pallas_call x1, Pallas kernels, last_call(): pl.pallas_call(last_kernel, in_specs=[ON_CHIP] * 10, out_specs=ON_CHIP, o...  8.45 us
    all_to_all x2, starting transfers between devices, sent_to_all(): lax.all_to_all(jnp.broadcast_to(array[None], (count, *array.shape)), axes...  7.84 us
  transfers between devices with their start and end apart: 5, of which 3 were waited for; matrix products, arithmetic and copies ran while one was open for 2% of the time, Pallas kernels for 14%

profile of v4, /device:TPU:1, one launch (start us, length us, event | category | flops | bytes accessed | tf_op | source)
XLA Modules:
  0.0 163.7 jit_solution(15655795243471319121)
XLA Ops:
  0.6 1.4 reshape.67
  3.7 1.2 reshape.71
  5.0 6.0 %all-to-all-start = ((f32[8,288,128]{2,1,0:T(8,128)}), f32[8,288,128]{2,1,0:T(8,128)S(1)}, u32[]{:S(2)}, u32[]{:S(2)}) async-start(f32[8,288,128]{2,1,0:T(8,128)} %reshape.71), calls=%async_computation | async-start | bytes 2359296 | tf_op jit(solution)/shard_map/all_to_all | solution.py:641
  12.4 8.6 %wide_misfit.1 = f32[128,128]{1,0:T(8,128)} custom-call(f32[256,512]{1,0:T(8,128)} %bitcast.78, f32[2,2,16,2048]{3,2,1,0:T(8,128)} %vis_ref.3, s32[2,16,2048]{2,1,0:T(8,128)} %flag_ref.3, s32[2,2048]{1,0:T(2,128)} %pair_ref.3, f32[2,2,2048]{2,1,0:T(2,128)} %coord_ref.3, f32[2,8]{1,0:T(2,128)} %dirs_ref.3, f32[8,16]{1,0:T(8,128)} %flux_ref.3, f32[1,16]{1,0:T(1,128)} %bitcast.80), custom_call_target="tpu_custom_call" | custom-call | flops 32000000 | bytes 1048576 | tf_op jit(solution)/shard_map/wide_misfit/pallas_call | solution.py:203
  21.0 7.3 %all-to-all-done = f32[8,288,128]{2,1,0:T(8,128)S(1)} async-done(((f32[8,288,128]{2,1,0:T(8,128)}), f32[8,288,128]{2,1,0:T(8,128)S(1)}, u32[]{:S(2)}, u32[]{:S(2)}) %all-to-all-start) | async-done | bytes 1179680 | tf_op jit(solution)/shard_map/all_to_all | solution.py:641
  28.5 8.8 %all-to-all-start.1 = ((f32[128,1,128]{2,1,0:T(1,128)}), f32[128,1,128]{2,1,0:T(1,128)S(1)}, u32[]{:S(2)}, u32[]{:S(2)}) async-start(f32[128,1,128]{2,1,0:T(1,128)} %bitcast.8), calls=%async_computation.1 | async-start | bytes 131072 | tf_op jit(solution)/shard_map/all_to_all | solution.py:643
  37.5 5.9 %first_model.1 = (f32[8,32,2048]{2,1,0:T(8,128)S(1)}, f32[8,32,2048]{2,1,0:T(8,128)S(1)}, f32[8,8,2048]{2,1,0:T(8,128)S(1)}, f32[8,2,2,2,8,2048]{5,4,3,2,1,0:T(8,128)S(1)}) custom-call(f32[8,18,2048]{2,1,0:T(8,128)S(1)} %reshape.72.data_ref, f32[32,512]{1,0:T(8,128)S(1)} %bitcast.63, f32[8,8]{1,0:T(8,128)S(1)} %concatenate.7.geo_ref), custom_call_target="tpu_custom_call" | custom-call | flops 24000000 | bytes 1048576 | tf_op jit(solution)/shard_map/first_model/pallas_call | solution.py:520
  43.4 1.9 %copy-done = f32[8,2,2,2,8,2048]{5,4,3,2,1,0:T(8,128)} copy-done((f32[8,2,2,2,8,2048]{5,4,3,2,1,0:T(8,128)}, f32[8,2,2,2,8,2048]{5,4,3,2,1,0:T(8,128)S(1)}, u32[]{:S(2)}) %copy-start) | copy-done | bytes 4194328
  45.3 1.3 copy-done.3
  46.7 1.4 copy-done.5
  48.0 2.2 %copy-done.1 = f32[8,2,2,2,8,2048]{5,4,3,2,1,0:T(8,128)S(1)} copy-done((f32[8,2,2,2,8,2048]{5,4,3,2,1,0:T(8,128)S(1)}, f32[8,2,2,2,8,2048]{5,4,3,2,1,0:T(8,128)}, u32[]{:S(2)}) %copy-start.1) | copy-done | bytes 4194328
  50.2 1.6 copy-done.4
  51.8 1.6 copy-done.6
  53.4 12.6 %normal_and_model.2 = (f32[32,512]{1,0:T(8,128)S(1)}, f32[8,32,2048]{2,1,0:T(8,128)S(1)}, f32[8,32,2048]{2,1,0:T(8,128)S(1)}, f32[8,8,2048]{2,1,0:T(8,128)S(1)}, f32[128,128]{1,0:T(8,128)S(1)}) custom-call(f32[128,128]{1,0:T(8,128)S(1)} %bitcast.56, f32[128,128]{1,0:T(8,128)S(1)} %bitcast.57, f32[8,18,2048]{2,1,0:T(8,128)S(1)} %reshape.72.data_ref, ...), custom_call_target="tpu_custom_call" | custom-call | flops 56000000 | bytes 1048576 | tf_op jit(solution)/shard_map/normal_and_model/pallas_call | solution.py:533
  66.0 19.2 %all_to_all.35 = f32[128,1,128]{2,1,0:T(1,128)S(1)} all-to-all(f32[128,1,128]{2,1,0:T(1,128)S(1)} %bitcast.68), channel_id=1, replica_groups=mesh['bl_0'=4,'bl_1'=2,'freq_0'=4,'freq_1'=2,'freq_2'=2] {'bl_0','bl_1',..., dimensions={0} | all-to-all | bytes 131072 | tf_op jit(solution)/shard_map/all_to_all | solution.py:680
  85.2 12.6 %normal_and_model.3 = (f32[32,512]{1,0:T(8,128)S(1)}, f32[8,32,2048]{2,1,0:T(8,128)S(1)}, f32[8,32,2048]{2,1,0:T(8,128)S(1)}, f32[8,8,2048]{2,1,0:T(8,128)S(1)}, f32[128,128]{1,0:T(8,128)S(1)}) custom-call(f32[128,128]{1,0:T(8,128)S(1)} %bitcast.65, f32[128,128]{1,0:T(8,128)S(1)} %bitcast.58, f32[8,18,2048]{2,1,0:T(8,128)S(1)} %reshape.72.data_ref, ...), custom_call_target="tpu_custom_call" | custom-call | flops 56000000 | bytes 1048576 | tf_op jit(solution)/shard_map/normal_and_model/pallas_call | solution.py:533
  97.8 13.7 %all_to_all.36 = f32[128,1,128]{2,1,0:T(1,128)S(1)} all-to-all(f32[128,1,128]{2,1,0:T(1,128)S(1)} %bitcast.67), channel_id=1, replica_groups=mesh['bl_0'=4,'bl_1'=2,'freq_0'=4,'freq_1'=2,'freq_2'=2] {'bl_0','bl_1',..., dimensions={0} | all-to-all | bytes 131072 | tf_op jit(solution)/shard_map/all_to_all | solution.py:680
  111.5 8.4 %normal_last.1 = f32[32,512]{1,0:T(8,128)S(1)} custom-call(f32[128,128]{1,0:T(8,128)S(1)} %bitcast.66, f32[128,128]{1,0:T(8,128)S(1)} %bitcast.59, f32[8,18,2048]{2,1,0:T(8,128)S(1)} %reshape.72.data_ref, f32[8,32,2048]{2,1,0:T(8,128)S(1)} %get-tuple-element.32.left_ref, f32[8,32,2048]{2,1,0:T(8,128)S(1)} %get-tuple-element.33.right_ref, ...), custom_call_target="tpu_custom_call" | custom-call | flops 32000000 | bytes 1048576 | tf_op jit(solution)/shard_map/normal_last/pallas_call | solution.py:552
  120.9 3.5 %all-to-all-start.4 = ((f32[8,128,128]{2,1,0:T(8,128)}), f32[8,128,128]{2,1,0:T(8,128)S(1)}, u32[]{:S(2)}, u32[]{:S(2)}) async-start(f32[8,128,128]{2,1,0:T(8,128)} %broadcast_in_dim.59), calls=%async_computation.4 | async-start | bytes 1048576 | tf_op jit(solution)/shard_map/all_to_all | solution.py:566
  124.5 8.5 %all-to-all-done.4 = f32[8,128,128]{2,1,0:T(8,128)S(1)} async-done(((f32[8,128,128]{2,1,0:T(8,128)}), f32[8,128,128]{2,1,0:T(8,128)S(1)}, u32[]{:S(2)}, u32[]{:S(2)}) %all-to-all-start.4) | async-done | bytes 524320 | tf_op jit(solution)/shard_map/all_to_all | solution.py:566
  134.3 5.0 %all-to-all-start.5 = ((f32[16,3,512]{2,1,0:T(4,128)}), f32[16,3,512]{2,1,0:T(4,128)S(1)}, u32[]{:S(2)}, u32[]{:S(2)}) async-start(f32[16,3,512]{2,1,0:T(4,128)} %pad_maximum_fusion.1), calls=%async_computation.5 | async-start | bytes 262144 | tf_op jit(solution)/shard_map/all_to_all | solution.py:699
  144.1 3.0 %all-to-all-done.5 = f32[16,3,512]{2,1,0:T(4,128)S(1)} async-done(((f32[16,3,512]{2,1,0:T(4,128)}), f32[16,3,512]{2,1,0:T(4,128)S(1)}, u32[]{:S(2)}, u32[]{:S(2)}) %all-to-all-start.5) | async-done | bytes 98336 | tf_op jit(solution)/shard_map/all_to_all | solution.py:699
  147.8 4.3 %all-to-all-start.6 = ((f32[16,3,512]{2,1,0:T(4,128)}), f32[16,3,512]{2,1,0:T(4,128)S(1)}, u32[]{:S(2)}, u32[]{:S(2)}) async-start(f32[16,3,512]{2,1,0:T(4,128)} %broadcast_in_dim.60), calls=%async_computation.6 | async-start | bytes 262144 | tf_op jit(solution)/shard_map/all_to_all | solution.py:566
  153.2 8.4 %wide_residual.1 = f32[2,2,16,2048]{3,2,1,0:T(8,128)} custom-call(f32[256,512]{1,0:T(8,128)} %bitcast.72, f32[2,2,16,2048]{3,2,1,0:T(8,128)} %vis_ref.3, s32[2,16,2048]{2,1,0:T(8,128)} %flag_ref.3, s32[2,2048]{1,0:T(2,128)} %pair_ref.3, f32[2,2,2048]{2,1,0:T(2,128)} %coord_ref.3, f32[2,8]{1,0:T(2,128)} %dirs_ref.3, f32[8,16]{1,0:T(8,128)} %flux_ref.3, ...), custom_call_target="tpu_custom_call" | custom-call | flops 32000000 | bytes 1048576 | tf_op jit(solution)/shard_map/wide_residual/pallas_call | solution.py:203
  (78 shorter events, 10.2 us)
Async XLA Ops:
  0.6 1.7 %copy-start.7 = (s32[2,16,2048]{2,1,0:T(8,128)S(1)}, s32[2,16,2048]{2,1,0:T(8,128)}, u32[]{:S(2)}) copy-start(s32[2,16,2048]{2,1,0:T(8,128)} %flag_ref.3) | copy-start | bytes 786436
  2.0 0.8 copy-start.9
  2.0 0.8 copy-start.10
  5.0 6.0 %copy-start.16 = (f32[8]{0:T(128)S(1)}, f32[8]{0:T(128)}, u32[]{:S(2)}) copy-start(f32[8]{0:T(128)} %param.21) | copy-start | bytes 100
  5.0 6.1 %copy-start.13 = (f32[2,8]{1,0:T(2,128)S(1)}, f32[2,8]{1,0:T(2,128)}, u32[]{:S(2)}) copy-start(f32[2,8]{1,0:T(2,128)} %dirs_ref.3) | copy-start | bytes 196
  5.0 7.2 %copy-start.14 = (f32[16]{0:T(128)S(1)}, f32[16]{0:T(128)}, u32[]{:S(2)}) copy-start(f32[16]{0:T(128)} %param.17) | copy-start | bytes 196
  5.0 7.3 %copy-start.11 = (f32[2,3,8,512]{3,2,1,0:T(8,128)S(1)}, f32[2,3,8,512]{3,2,1,0:T(8,128)}, u32[]{:S(2)}) copy-start(f32[2,3,8,512]{3,2,1,0:T(8,128)} %param.20) | copy-start | bytes 294916
  5.0 7.3 %copy-start.8 = (f32[2,8,16,512]{3,2,1,0:T(8,128)S(1)}, f32[2,8,16,512]{3,2,1,0:T(8,128)}, u32[]{:S(2)}) copy-start(f32[2,8,16,512]{3,2,1,0:T(8,128)} %param.19) | copy-start | bytes 1572868
  5.0 23.4 %all-to-all-start = ((f32[8,288,128]{2,1,0:T(8,128)}), f32[8,288,128]{2,1,0:T(8,128)S(1)}, u32[]{:S(2)}, u32[]{:S(2)}) async-start(f32[8,288,128]{2,1,0:T(8,128)} %reshape.71), calls=%async_computation | async-start | bytes 2359296 | tf_op jit(solution)/shard_map/all_to_all | solution.py:641
  21.0 16.4 %copy-start.12 = (f32[8,16]{1,0:T(8,128)S(1)}, f32[8,16]{1,0:T(8,128)}, u32[]{:S(2)}) copy-start(f32[8,16]{1,0:T(8,128)} %flux_ref.3) | copy-start | bytes 1540
  28.5 19.5 %all-to-all-start.1 = ((f32[128,1,128]{2,1,0:T(1,128)}), f32[128,1,128]{2,1,0:T(1,128)S(1)}, u32[]{:S(2)}, u32[]{:S(2)}) async-start(f32[128,1,128]{2,1,0:T(1,128)} %bitcast.8), calls=%async_computation.1 | async-start | bytes 131072 | tf_op jit(solution)/shard_map/all_to_all | solution.py:643
  43.4 1.9 %copy-start = (f32[8,2,2,2,8,2048]{5,4,3,2,1,0:T(8,128)}, f32[8,2,2,2,8,2048]{5,4,3,2,1,0:T(8,128)S(1)}, u32[]{:S(2)}) copy-start(f32[8,2,2,2,8,2048]{5,4,3,2,1,0:T(8,128)S(1)} %get-tuple-element.25.sky_ref) | copy-start | bytes 12582916
  45.3 1.3 copy-start.3
  46.7 1.4 copy-start.5
  48.0 2.2 %copy-start.1 = (f32[8,2,2,2,8,2048]{5,4,3,2,1,0:T(8,128)S(1)}, f32[8,2,2,2,8,2048]{5,4,3,2,1,0:T(8,128)}, u32[]{:S(2)}) copy-start(f32[8,2,2,2,8,2048]{5,4,3,2,1,0:T(8,128)} %copy-done) | copy-start | bytes 12582916
  50.2 1.6 copy-start.4
  51.8 1.6 copy-start.6
  53.4 31.8 %copy-start.2 = (f32[8,2,2,2,8,2048]{5,4,3,2,1,0:T(8,128)S(1)}, f32[8,2,2,2,8,2048]{5,4,3,2,1,0:T(8,128)}, u32[]{:S(2)}) copy-start(f32[8,2,2,2,8,2048]{5,4,3,2,1,0:T(8,128)} %copy-done) | copy-start | bytes 12582916
  120.0 4.4 %copy-start.15 = (f32[16]{0:T(128)S(1)}, f32[16]{0:T(128)}, u32[]{:S(2)}) copy-start(f32[16]{0:T(128)} %param.17) | copy-start | bytes 196
  120.9 12.1 %all-to-all-start.4 = ((f32[8,128,128]{2,1,0:T(8,128)}), f32[8,128,128]{2,1,0:T(8,128)S(1)}, u32[]{:S(2)}, u32[]{:S(2)}) async-start(f32[8,128,128]{2,1,0:T(8,128)} %broadcast_in_dim.59), calls=%async_computation.4 | async-start | bytes 1048576 | tf_op jit(solution)/shard_map/all_to_all | solution.py:566
  134.3 12.7 %all-to-all-start.5 = ((f32[16,3,512]{2,1,0:T(4,128)}), f32[16,3,512]{2,1,0:T(4,128)S(1)}, u32[]{:S(2)}, u32[]{:S(2)}) async-start(f32[16,3,512]{2,1,0:T(4,128)} %pad_maximum_fusion.1), calls=%async_computation.5 | async-start | bytes 262144 | tf_op jit(solution)/shard_map/all_to_all | solution.py:699
  147.8 13.9 %all-to-all-start.6 = ((f32[16,3,512]{2,1,0:T(4,128)}), f32[16,3,512]{2,1,0:T(4,128)S(1)}, u32[]{:S(2)}, u32[]{:S(2)}) async-start(f32[16,3,512]{2,1,0:T(4,128)} %broadcast_in_dim.60), calls=%async_computation.6 | async-start | bytes 262144 | tf_op jit(solution)/shard_map/all_to_all | solution.py:566

commit v5 on v4

--- a/solution.py
+++ b/solution.py
@@ -375,27 +375,44 @@
     return made
 
 
-def normal_runs(data_ref, left_ref, right_ref, error_ref, sky_ref, total_ref, inverse):
+def normal_runs(data_ref, left_ref, right_ref, error_ref, sky_ref, total_ref, buffers, inverse):
     steps = LOCAL // SUB // NORMAL_RUNS
-    total_ref[...] = jnp.zeros_like(total_ref)
-
-    def run(i, carry):
+    width = 2 * SUB * NORMAL_RUNS
+
+    def fill(i, into):
         part, first = i // steps, (i % steps) * NORMAL_RUNS
-        made = []
+        values_ref, hots_ref = into
         for j in range(NORMAL_RUNS):
             at = pl.multiple_of((first + j) * SUB, SUB)
-            made += normal_block(
+            made = normal_block(
                 part, at, data_ref, left_ref, right_ref, error_ref, sky_ref, inverse
             )
-        total_ref[...] += lax.dot_general(
-            jnp.concatenate([m[0] for m in made], axis=1),
-            jnp.concatenate([m[1] for m in made], axis=1),
+            for side in range(2):
+                where = slice((2 * j + side) * SUB, (2 * j + side + 1) * SUB)
+                values_ref[:, where] = made[side][0]
+                hots_ref[:, where] = made[side][1]
+
+    def add(into):
+        values_ref, hots_ref = into
+        return lax.dot_general(
+            values_ref[...],
+            hots_ref[...],
             (((1,), (1,)), ((), ())),
             preferred_element_type=F32,
         )
+
+    fill(0, buffers[0])
+    total_ref[...] = jnp.zeros_like(total_ref)
+
+    def run(i, carry):
+        one = add(buffers[0])
+        fill(2 * i + 1, buffers[1])
+        two = add(buffers[1])
+        fill(jnp.minimum(2 * i + 2, PARTS * steps - 1), buffers[0])
+        total_ref[...] += one + two
         return carry
 
-    lax.fori_loop(0, PARTS * steps, run, 0)
+    lax.fori_loop(0, PARTS * steps // 2, run, 0)
 
 
 def renew_gains(gains, anchor, total, columns):
@@ -424,9 +441,11 @@
 
 
 def renewed(
-    squares_ref, count_ref, data_ref, held, gains_ref, anchor_ref, geo_ref, total_ref
+    squares_ref, count_ref, data_ref, held, gains_ref, anchor_ref, geo_ref, total_ref, buffers
 ):
-    normal_runs(data_ref, *held, total_ref, inverse_of(squares_ref, count_ref))
+    normal_runs(
+        data_ref, *held, total_ref, buffers, inverse_of(squares_ref, count_ref)
+    )
     return renew_gains(gains_ref[...], anchor_ref[...], total_ref[...], geo_ref[...])
 
 
@@ -465,10 +484,12 @@
     misfit_out,
     table_ref,
     total_ref,
+    *flat,
 ):
+    buffers = (flat[0:2], flat[2:4])
     held = (left_ref, right_ref, error_ref, sky_ref)
     gains = renewed(
-        squares_ref, count_ref, data_ref, held, gains_ref, anchor_ref, geo_ref, total_ref
+        squares_ref, count_ref, data_ref, held, gains_ref, anchor_ref, geo_ref, total_ref, buffers
     )
     gains_out[...] = gains
     next_model(
@@ -489,11 +510,14 @@
     geo_ref,
     gains_out,
     total_ref,
+    *flat,
 ):
+    buffers = (flat[0:2], flat[2:4])
     held = (left_ref, right_ref, error_ref, sky_ref)
-    gains_out[...] = renewed(
-        squares_ref, count_ref, data_ref, held, gains_ref, anchor_ref, geo_ref, total_ref
-    )
+    gains = renewed(
+        squares_ref, count_ref, data_ref, held, gains_ref, anchor_ref, geo_ref, total_ref, buffers
+    )
+    gains_out[...] = jnp.broadcast_to(gains[None], gains_out.shape)
 
 
 ROWS = 18
@@ -527,6 +551,11 @@
         cost_estimate=lasts(6),
         name="first_model",
     )(data, gains, geo)
+
+
+def run_buffers():
+    width = 2 * SUB * NORMAL_RUNS
+    return [pltpu.VMEM((192, width), BF16), pltpu.VMEM((256, width), BF16)] * 2
 
 
 def middle_call(squares, count, data, held, gains, anchor, geo, devices):
@@ -541,7 +570,7 @@
             shapes_of(8),
             jax.ShapeDtypeStruct((devices, 128), F32),
         ],
-        scratch_shapes=[pltpu.VMEM((128, 256), BF16), pltpu.VMEM((192, 256), F32)],
+        scratch_shapes=[pltpu.VMEM((128, 256), BF16), pltpu.VMEM((192, 256), F32), *run_buffers()],
         compiler_params=GRANT,
         cost_estimate=lasts(14),
         name="normal_and_model",
@@ -553,12 +582,49 @@
         last_kernel,
         in_specs=[ON_CHIP] * 10,
         out_specs=ON_CHIP,
-        out_shape=jax.ShapeDtypeStruct((GAIN_ROWS, STATIONS), F32),
-        scratch_shapes=[pltpu.VMEM((192, 256), F32)],
+        out_shape=jax.ShapeDtypeStruct((PARTS, GAIN_ROWS, STATIONS), F32),
+        scratch_shapes=[pltpu.VMEM((192, 256), F32), *run_buffers()],
         compiler_params=GRANT,
         cost_estimate=lasts(8),
         name="normal_last",
     )(squares, count, data, *held, gains, anchor, geo)
+
+
+def finish_kernel(solved_ref, gains_ref, dual_ref, ratio_ref, consensus_out, dual_out):
+    channels = ratio_ref.shape[1]
+    own = lax.broadcasted_iota(jnp.int32, (channels, channels), 0)
+    own = own == lax.broadcasted_iota(jnp.int32, (channels, channels), 1)
+    columns = [
+        jnp.sum(
+            jnp.where(own, jnp.broadcast_to(row, (channels, channels)), 0.0),
+            axis=1,
+            keepdims=True,
+        )
+        for row in legendre(ratio_ref[...])
+    ]
+    for c in range(2):
+        for k in range(DIRS):
+            g = DIRS * c + k
+            rows = [solved_ref[g, j : j + 1, :] for j in range(NPOLY)]
+            for j in range(NPOLY):
+                consensus_out[c, j, k : k + 1, :] = rows[j]
+            fitted = sum(columns[j] * rows[j] for j in range(NPOLY))
+            dual_out[c, k] = dual_ref[c, k] + gains_ref[c, k] - fitted
+
+
+def finish_call(solved, gains, dual, ratio):
+    return pl.pallas_call(
+        finish_kernel,
+        in_specs=[ON_CHIP] * 4,
+        out_specs=[ON_CHIP] * 2,
+        out_shape=[
+            jax.ShapeDtypeStruct((2, NPOLY, DIRS, STATIONS), F32),
+            jax.ShapeDtypeStruct(dual.shape, F32),
+        ],
+        compiler_params=GRANT,
+        cost_estimate=lasts(1),
+        name="finish",
+    )(solved, gains, dual, ratio.reshape(1, -1))
 
 
 def sent_to_all(array, axes):
@@ -639,15 +705,10 @@
     )
     send = send.reshape(PARTS, ROWS * LOCAL // 128, 128)
     data = lax.all_to_all(send, BL, 0, 0, tiled=True).reshape(PARTS, ROWS, LOCAL)
-    payload, data = lax.optimization_barrier((payload, data))
-    arrived = lax.all_to_all(payload[:, None], ALL, 0, 0, tiled=True)[:, 0]
 
     ratio = own_channels(channel_ratio, 0, own)
     flux = own_channels(source_flux, 1, own)
     basis = legendre(ratio)
-    sums = arrived.sum(axis=0) / lax.axis_size(BL)
-    gram = [[sums[2 + i * (i + 1) // 2 + j] for j in range(i + 1)] for i in range(NPOLY)]
-
     def rows_of(array):
         part = own_channels(array, 2, own)
         return part.transpose(2, 0, 1, 3)
@@ -672,6 +733,8 @@
     )
 
     left, right, error, sky = first_call(data, gains, geo)
+    payload, error, anchor = lax.optimization_barrier((payload, error, anchor))
+    arrived = lax.all_to_all(payload[:, None], ALL, 0, 0, tiled=True)[:, 0]
     squares = arrived
     for iteration in range(ITERS - 1):
         gains, left, right, error, misfit = middle_call(
@@ -680,7 +743,7 @@
         squares = lax.all_to_all(misfit[:, None], ALL, 0, 0, tiled=True)[:, 0]
     gains = last_call(squares, arrived, data, (left, right, error, sky), gains, anchor, geo)
 
-    gathered = sent_to_all(gains.reshape(GAIN_ROWS * STATIONS // 128, 128), BL)
+    gathered = lax.all_to_all(gains, BL, 0, 0, tiled=True)
     new_gains = (
         gathered.reshape(PARTS * FEW, 2, DIRS, STATIONS).transpose(1, 2, 0, 3)
     )
@@ -697,15 +760,13 @@
         axis=1,
     )
     rhs = lax.all_to_all(rhs, FREQ, 0, 0, tiled=True)
+    rhs, residuals = lax.optimization_barrier((rhs, residuals))
     rhs = rhs.sum(axis=0)
+    sums = arrived.sum(axis=0) / lax.axis_size(BL)
+    gram = [[sums[2 + i * (i + 1) // 2 + j] for j in range(i + 1)] for i in range(NPOLY)]
     solved = jnp.stack(cholesky_solve(gram, [rhs[j] for j in range(NPOLY)]))
     everyone = sent_to_all(solved, FREQ)
-    new_consensus = everyone.reshape(2, DIRS, NPOLY, STATIONS).transpose(0, 2, 1, 3)
-    fitted = sum(
-        all_basis[j][None, None, :, None] * new_consensus[:, j][:, :, None, :]
-        for j in range(NPOLY)
-    )
-    new_dual = lifted - fitted
+    new_consensus, new_dual = finish_call(everyone, new_gains, scaled_dual, channel_ratio)
     return (new_gains, new_consensus, new_dual, residuals)
 
 

time: 165 us -> 162 us (0.982)
  blocking collectives: 32.9 us -> 60.3 us
  local copies, waits for them, and re-layouts: 20.9 us -> 7.45 us
  starting transfers between devices: 27.7 us -> 14.7 us
  waiting for transfers between devices: 18.8 us -> 15.5 us
  Pallas kernels: 56.5 us -> 54.7 us
    all_to_all x0 -> x2, blocking collectives: none -> 32.9 us  [the longest x1 18.2 us: body(): arrived = lax.all_to_all(payload[:, None], ALL, 0, 0, tiled=True)[:, 0]]
    all_to_all x3 -> x1, starting transfers between devices: 16.7 us -> 3.67 us  [body(): gathered = lax.all_to_all(gains, BL, 0, 0, tiled=True)]
    unnamed x38 -> x25, local copies, waits for them, and re-layouts: 13 us -> 1.18 us
    all_to_all x2, blocking collectives: 32.9 us -> 27.4 us  [body(): squares = lax.all_to_all(misfit[:, None], ALL, 0, 0, tiled=True)[:, 0]]
    all_to_all x1, waiting for transfers between devices: 2.95 us -> 0.01 us  [body(): rhs = lax.all_to_all(rhs, FREQ, 0, 0, tiled=True)]
    pallas_call x2, Pallas kernels: 25.2 us -> 22.7 us  [middle_call(): pl.pallas_call(middle_kernel, in_specs=[ON_CHIP] * 10, out_specs=[ON_CHIP...]
    all_to_all x3 -> x1, waiting for transfers between devices: 8.46 us -> 8.28 us  [body(): gathered = lax.all_to_all(gains, BL, 0, 0, tiled=True)]
  transfers between devices with their start and end apart: 5 -> 3, of which waited for: 3 -> 2; matrix products, arithmetic and copies ran while one was open for 2% -> 1% of each run, Pallas kernels for 14% -> 11%
where the time goes in v5:
time: 162 us; the launch traced here: 161 us
  blocking collectives  60.3 us (37%)
  Pallas kernels  54.7 us (34%)
  waiting for transfers between devices  15.5 us (10%)
  starting transfers between devices  14.7 us (9%)
  local copies, waits for them, and re-layouts  7.45 us (5%)
  between operations  4.84 us (3%)
  other arithmetic  3.43 us (2%)
    all_to_all x2, blocking collectives, body(): squares = lax.all_to_all(misfit[:, None], ALL, 0, 0, tiled=True)[:, 0]  27.4 us
    pallas_call x2, Pallas kernels, middle_call(): pl.pallas_call(middle_kernel, in_specs=[ON_CHIP] * 10, out_specs=[ON_CHIP...  22.7 us
    all_to_all x1, blocking collectives, body(): arrived = lax.all_to_all(payload[:, None], ALL, 0, 0, tiled=True)[:, 0]  18.2 us
    pallas_call x2, Pallas kernels, wide_model(): pl.pallas_call(functools.partial(wide_kernel, residual_out=residual_out,...  17 us
    all_to_all x1, blocking collectives, sent_to_all(): lax.all_to_all(jnp.broadcast_to(array[None], (count, *array.shape)), axes...  14.7 us
    all_to_all x1, waiting for transfers between devices, body(): gathered = lax.all_to_all(gains, BL, 0, 0, tiled=True)  8.28 us
    pallas_call x1, Pallas kernels, last_call(): pl.pallas_call(last_kernel, in_specs=[ON_CHIP] * 10, out_specs=ON_CHIP, o...  8.1 us
    all_to_all x1, waiting for transfers between devices, body(): lax.all_to_all(send, BL, 0, 0, tiled=True).reshape(PARTS, ROWS, LOCAL)  7.21 us
  transfers between devices with their start and end apart: 3, of which 2 were waited for; matrix products, arithmetic and copies ran while one was open for 1% of the time, Pallas kernels for 11%

profile of v5, /device:TPU:1, one launch (start us, length us, event | category | flops | bytes accessed | tf_op | source)
XLA Modules:
  0.0 160.9 jit_solution(6491044820168176190)
XLA Ops:
  0.6 0.8 convert_element_type.7
  1.4 0.8 broadcast_in_dim.18
  2.2 1.0 convert_element_type.6
  4.4 0.7 copy.37
  5.1 1.2 reshape.65
  6.3 6.0 %all-to-all-start = ((f32[8,288,128]{2,1,0:T(8,128)}), f32[8,288,128]{2,1,0:T(8,128)S(1)}, u32[]{:S(2)}, u32[]{:S(2)}) async-start(f32[8,288,128]{2,1,0:T(8,128)} %reshape.65), calls=%async_computation | async-start | bytes 2359296 | tf_op jit(solution)/shard_map/all_to_all | solution.py:707
  12.3 1.0 dynamic-slice_bitcast_fusion
  14.0 8.5 %wide_misfit.1 = f32[128,128]{1,0:T(8,128)} custom-call(f32[256,512]{1,0:T(8,128)} %bitcast.73, f32[2,2,16,2048]{3,2,1,0:T(8,128)} %vis_ref.3, s32[2,16,2048]{2,1,0:T(8,128)} %flag_ref.3, s32[2,2048]{1,0:T(2,128)} %pair_ref.3, f32[2,2,2048]{2,1,0:T(2,128)} %coord_ref.3, f32[2,8]{1,0:T(2,128)} %dirs_ref.3, f32[8,16]{1,0:T(8,128)} %flux_ref.3, f32[1,16]{1,0:T(1,128)} %bitcast.65), custom_call_target="tpu_custom_call" | custom-call | flops 32000000 | bytes 1048576 | tf_op jit(solution)/shard_map/wide_misfit/pallas_call | solution.py:203
  22.5 7.2 %all-to-all-done = f32[8,288,128]{2,1,0:T(8,128)S(1)} async-done(((f32[8,288,128]{2,1,0:T(8,128)}), f32[8,288,128]{2,1,0:T(8,128)S(1)}, u32[]{:S(2)}, u32[]{:S(2)}) %all-to-all-start) | async-done | bytes 1179680 | tf_op jit(solution)/shard_map/all_to_all | solution.py:707
  29.9 5.9 %first_model.1 = (f32[8,32,2048]{2,1,0:T(8,128)S(1)}, f32[8,32,2048]{2,1,0:T(8,128)S(1)}, f32[8,8,2048]{2,1,0:T(8,128)S(1)}, f32[8,2,2,2,8,2048]{5,4,3,2,1,0:T(8,128)S(1)}) custom-call(f32[8,18,2048]{2,1,0:T(8,128)S(1)} %reshape.66.data_ref, f32[32,512]{1,0:T(8,128)S(1)} %bitcast.59, f32[8,8]{1,0:T(8,128)S(1)} %concatenate.7.geo_ref), custom_call_target="tpu_custom_call" | custom-call | flops 24000000 | bytes 1048576 | tf_op jit(solution)/shard_map/first_model/pallas_call | solution.py:544
  35.8 18.2 %all_to_all.35 = f32[128,1,128]{2,1,0:T(1,128)S(1)} all-to-all(f32[128,1,128]{2,1,0:T(1,128)S(1)} %bitcast.74), channel_id=1, replica_groups=mesh['bl_0'=4,'bl_1'=2,'freq_0'=4,'freq_1'=2,'freq_2'=2] {'bl_0','bl_1',..., dimensions={0} | all-to-all | bytes 131072 | tf_op jit(solution)/shard_map/all_to_all | solution.py:737
  54.1 11.3 %normal_and_model.2 = (f32[32,512]{1,0:T(8,128)S(1)}, f32[8,32,2048]{2,1,0:T(8,128)S(1)}, f32[8,32,2048]{2,1,0:T(8,128)S(1)}, f32[8,8,2048]{2,1,0:T(8,128)S(1)}, f32[128,128]{1,0:T(8,128)S(1)}) custom-call(f32[128,128]{1,0:T(8,128)S(1)} %bitcast.52, f32[128,128]{1,0:T(8,128)S(1)} %bitcast.53, f32[8,18,2048]{2,1,0:T(8,128)S(1)} %reshape.66.data_ref, ...), custom_call_target="tpu_custom_call" | custom-call | flops 56000000 | bytes 1048576 | tf_op jit(solution)/shard_map/normal_and_model/pallas_call | solution.py:562
  65.4 13.7 %all_to_all.36 = f32[128,1,128]{2,1,0:T(1,128)S(1)} all-to-all(f32[128,1,128]{2,1,0:T(1,128)S(1)} %bitcast.64), channel_id=1, replica_groups=mesh['bl_0'=4,'bl_1'=2,'freq_0'=4,'freq_1'=2,'freq_2'=2] {'bl_0','bl_1',..., dimensions={0} | all-to-all | bytes 131072 | tf_op jit(solution)/shard_map/all_to_all | solution.py:743
  79.1 11.3 %normal_and_model.3 = (f32[32,512]{1,0:T(8,128)S(1)}, f32[8,32,2048]{2,1,0:T(8,128)S(1)}, f32[8,32,2048]{2,1,0:T(8,128)S(1)}, f32[8,8,2048]{2,1,0:T(8,128)S(1)}, f32[128,128]{1,0:T(8,128)S(1)}) custom-call(f32[128,128]{1,0:T(8,128)S(1)} %bitcast.61, f32[128,128]{1,0:T(8,128)S(1)} %bitcast.54, f32[8,18,2048]{2,1,0:T(8,128)S(1)} %reshape.66.data_ref, ...), custom_call_target="tpu_custom_call" | custom-call | flops 56000000 | bytes 1048576 | tf_op jit(solution)/shard_map/normal_and_model/pallas_call | solution.py:562
  90.5 13.7 %all_to_all.37 = f32[128,1,128]{2,1,0:T(1,128)S(1)} all-to-all(f32[128,1,128]{2,1,0:T(1,128)S(1)} %bitcast.63), channel_id=1, replica_groups=mesh['bl_0'=4,'bl_1'=2,'freq_0'=4,'freq_1'=2,'freq_2'=2] {'bl_0','bl_1',..., dimensions={0} | all-to-all | bytes 131072 | tf_op jit(solution)/shard_map/all_to_all | solution.py:743
  104.2 8.1 %normal_last.1 = f32[8,32,512]{2,1,0:T(8,128)} custom-call(f32[128,128]{1,0:T(8,128)S(1)} %bitcast.62, f32[128,128]{1,0:T(8,128)S(1)} %bitcast.55, f32[8,18,2048]{2,1,0:T(8,128)S(1)} %reshape.66.data_ref, f32[8,32,2048]{2,1,0:T(8,128)S(1)} %get-tuple-element.38.left_ref, f32[8,32,2048]{2,1,0:T(8,128)S(1)} %get-tuple-element.39.right_ref, ...), custom_call_target="tpu_custom_call" | custom-call | flops 32000000 | bytes 1048576 | tf_op jit(solution)/shard_map/normal_last/pallas_call | solution.py:581
  112.3 3.7 %all-to-all-start.4 = ((f32[8,32,512]{2,1,0:T(8,128)}), f32[8,32,512]{2,1,0:T(8,128)S(1)}, u32[]{:S(2)}, u32[]{:S(2)}) async-start(f32[8,32,512]{2,1,0:T(8,128)} %normal_last.1), calls=%async_computation.4 | async-start | bytes 1048576 | tf_op jit(solution)/shard_map/all_to_all | solution.py:746
  116.2 8.3 %all-to-all-done.4 = f32[8,32,512]{2,1,0:T(8,128)S(1)} async-done(((f32[8,32,512]{2,1,0:T(8,128)}), f32[8,32,512]{2,1,0:T(8,128)S(1)}, u32[]{:S(2)}, u32[]{:S(2)}) %all-to-all-start.4) | async-done | bytes 524320 | tf_op jit(solution)/shard_map/all_to_all | solution.py:746
  125.3 0.7 pad_maximum_fusion.1
  126.0 5.0 %all-to-all-start.5 = ((f32[16,3,512]{2,1,0:T(4,128)}), f32[16,3,512]{2,1,0:T(4,128)S(1)}, u32[]{:S(2)}, u32[]{:S(2)}) async-start(f32[16,3,512]{2,1,0:T(4,128)} %pad_maximum_fusion.1), calls=%async_computation.5 | async-start | bytes 262144 | tf_op jit(solution)/shard_map/all_to_all | solution.py:762
  135.6 8.5 %wide_residual.1 = f32[2,2,16,2048]{3,2,1,0:T(8,128)} custom-call(f32[256,512]{1,0:T(8,128)} %bitcast.49, f32[2,2,16,2048]{3,2,1,0:T(8,128)} %vis_ref.3, s32[2,16,2048]{2,1,0:T(8,128)} %flag_ref.3, s32[2,2048]{1,0:T(2,128)} %pair_ref.3, f32[2,2,2048]{2,1,0:T(2,128)} %coord_ref.3, f32[2,8]{1,0:T(2,128)} %dirs_ref.3, f32[8,16]{1,0:T(8,128)} %flux_ref.3, ...), custom_call_target="tpu_custom_call" | custom-call | flops 32000000 | bytes 1048576 | tf_op jit(solution)/shard_map/wide_residual/pallas_call | solution.py:203
  144.2 14.7 %all_to_all.38.solved_ref = f32[16,3,512]{2,1,0:T(4,128)S(1)} all-to-all(f32[16,3,512]{2,1,0:T(4,128)S(1)} %broadcast_in_dim.49), channel_id=1, replica_groups=mesh['bl_0'=4,'bl_1'=2,'freq_0'=4,'freq_1'=2,'freq_2'=2] {'freq_0','freq..., dimensions={0} | all-to-all | bytes 196608 | tf_op jit(solution)/shard_map/all_to_all | solution.py:632
  158.9 1.0 copy-done.1
  159.9 1.0 finish.1
  (59 shorter events, 3.6 us)
Async XLA Ops:
  0.6 2.9 %copy-start.6 = (f32[2,2,16,2048]{3,2,1,0:T(8,128)S(1)}, f32[2,2,16,2048]{3,2,1,0:T(8,128)}, u32[]{:S(2)}) copy-start(f32[2,2,16,2048]{3,2,1,0:T(8,128)} %vis_ref.3) | copy-start | bytes 1572868
  6.3 7.0 %copy-start.10 = (f32[2,8]{1,0:T(2,128)S(1)}, f32[2,8]{1,0:T(2,128)}, u32[]{:S(2)}) copy-start(f32[2,8]{1,0:T(2,128)} %dirs_ref.3) | copy-start | bytes 196
  6.3 7.1 %copy-start.11 = (f32[8]{0:T(128)S(1)}, f32[8]{0:T(128)}, u32[]{:S(2)}) copy-start(f32[8]{0:T(128)} %param.21) | copy-start | bytes 100
  6.3 7.2 %copy-start.3 = (f32[16]{0:T(128)S(1)}, f32[16]{0:T(128)}, u32[]{:S(2)}) copy-start(f32[16]{0:T(128)} %param.17) | copy-start | bytes 196
  6.3 7.3 %copy-start.8 = (f32[2,3,8,512]{3,2,1,0:T(8,128)S(1)}, f32[2,3,8,512]{3,2,1,0:T(8,128)}, u32[]{:S(2)}) copy-start(f32[2,3,8,512]{3,2,1,0:T(8,128)} %param.20) | copy-start | bytes 294916
  6.3 7.3 %copy-start.2 = (f32[2,8,16,512]{3,2,1,0:T(8,128)S(1)}, f32[2,8,16,512]{3,2,1,0:T(8,128)}, u32[]{:S(2)}) copy-start(f32[2,8,16,512]{3,2,1,0:T(8,128)} %dual_ref.1) | copy-start | bytes 1572868
  6.3 7.5 %copy-start.9 = (f32[8,16]{1,0:T(8,128)S(1)}, f32[8,16]{1,0:T(8,128)}, u32[]{:S(2)}) copy-start(f32[8,16]{1,0:T(8,128)} %flux_ref.3) | copy-start | bytes 1540
  6.3 23.4 %all-to-all-start = ((f32[8,288,128]{2,1,0:T(8,128)}), f32[8,288,128]{2,1,0:T(8,128)S(1)}, u32[]{:S(2)}, u32[]{:S(2)}) async-start(f32[8,288,128]{2,1,0:T(8,128)} %reshape.65), calls=%async_computation | async-start | bytes 2359296 | tf_op jit(solution)/shard_map/all_to_all | solution.py:707
  29.9 6.0 %copy-start.7 = (f32[128,128]{1,0:T(8,128)S(1)}, f32[128,128]{1,0:T(8,128)}, u32[]{:S(2)}) copy-start(f32[128,128]{1,0:T(8,128)} %wide_misfit.1) | copy-start | bytes 196612
  104.2 11.8 %copy-start.4 = (f32[16]{0:T(128)S(1)}, f32[16]{0:T(128)}, u32[]{:S(2)}) copy-start(f32[16]{0:T(128)} %param.17) | copy-start | bytes 196
  112.3 12.1 %all-to-all-start.4 = ((f32[8,32,512]{2,1,0:T(8,128)}), f32[8,32,512]{2,1,0:T(8,128)S(1)}, u32[]{:S(2)}, u32[]{:S(2)}) async-start(f32[8,32,512]{2,1,0:T(8,128)} %normal_last.1), calls=%async_computation.4 | async-start | bytes 1048576 | tf_op jit(solution)/shard_map/all_to_all | solution.py:746
  124.7 10.8 %copy-start = (f32[16,2,8,512]{3,0,2,1:T(8,128)}, f32[16,2,8,512]{3,0,2,1:T(8,128)S(1)}, u32[]{:S(2)}) copy-start(f32[16,2,8,512]{3,0,2,1:T(8,128)S(1)} %copy.47) | copy-start | bytes 1572868
  126.0 18.1 %all-to-all-start.5 = ((f32[16,3,512]{2,1,0:T(4,128)}), f32[16,3,512]{2,1,0:T(4,128)S(1)}, u32[]{:S(2)}, u32[]{:S(2)}) async-start(f32[16,3,512]{2,1,0:T(4,128)} %pad_maximum_fusion.1), calls=%async_computation.5 | async-start | bytes 262144 | tf_op jit(solution)/shard_map/all_to_all | solution.py:762
  135.6 23.3 %copy-start.5 = (f32[16]{0:T(128)S(1)}, f32[16]{0:T(128)}, u32[]{:S(2)}) copy-start(f32[16]{0:T(128)} %param.17) | copy-start | bytes 196
  158.9 1.0 copy-start.1

commit v6 on v5

--- a/solution.py
+++ b/solution.py
@@ -590,50 +590,6 @@
     )(squares, count, data, *held, gains, anchor, geo)
 
 
-def finish_kernel(solved_ref, gains_ref, dual_ref, ratio_ref, consensus_out, dual_out):
-    channels = ratio_ref.shape[1]
-    own = lax.broadcasted_iota(jnp.int32, (channels, channels), 0)
-    own = own == lax.broadcasted_iota(jnp.int32, (channels, channels), 1)
-    columns = [
-        jnp.sum(
-            jnp.where(own, jnp.broadcast_to(row, (channels, channels)), 0.0),
-            axis=1,
-            keepdims=True,
-        )
-        for row in legendre(ratio_ref[...])
-    ]
-    for c in range(2):
-        for k in range(DIRS):
-            g = DIRS * c + k
-            rows = [solved_ref[g, j : j + 1, :] for j in range(NPOLY)]
-            for j in range(NPOLY):
-                consensus_out[c, j, k : k + 1, :] = rows[j]
-            fitted = sum(columns[j] * rows[j] for j in range(NPOLY))
-            dual_out[c, k] = dual_ref[c, k] + gains_ref[c, k] - fitted
-
-
-def finish_call(solved, gains, dual, ratio):
-    return pl.pallas_call(
-        finish_kernel,
-        in_specs=[ON_CHIP] * 4,
-        out_specs=[ON_CHIP] * 2,
-        out_shape=[
-            jax.ShapeDtypeStruct((2, NPOLY, DIRS, STATIONS), F32),
-            jax.ShapeDtypeStruct(dual.shape, F32),
-        ],
-        compiler_params=GRANT,
-        cost_estimate=lasts(1),
-        name="finish",
-    )(solved, gains, dual, ratio.reshape(1, -1))
-
-
-def sent_to_all(array, axes):
-    count = lax.axis_size(axes)
-    return lax.all_to_all(
-        jnp.broadcast_to(array[None], (count, *array.shape)), axes, 0, 0, tiled=True
-    )
-
-
 def cholesky_solve(gram, rhs):
     order = len(rhs)
     factor = [[None] * order for _ in range(order)]
@@ -658,17 +614,118 @@
     return backward
 
 
+def consensus_kernel(rhs_ref, arrived_ref, out_ref, *, copies):
+    rhs = rhs_ref[0]
+    for i in range(1, rhs_ref.shape[0]):
+        rhs = rhs + rhs_ref[i]
+    sums = jnp.sum(arrived_ref[...], axis=0, keepdims=True) * (1.0 / copies)
+    lane = lax.broadcasted_iota(jnp.int32, (1, 128), 1)
+    pick = lambda i: jnp.sum(jnp.where(lane == i, sums, 0.0), axis=1, keepdims=True)
+    gram = [[pick(2 + i * (i + 1) // 2 + j) for j in range(i + 1)] for i in range(NPOLY)]
+    solved = cholesky_solve(gram, [rhs[j : j + 1] for j in range(NPOLY)])
+    out_ref[...] = jnp.broadcast_to(jnp.concatenate(solved, axis=0)[None], out_ref.shape)
+
+
+def consensus_call(rhs, arrived, copies):
+    return pl.pallas_call(
+        functools.partial(consensus_kernel, copies=copies),
+        in_specs=[ON_CHIP] * 2,
+        out_specs=ON_CHIP,
+        out_shape=jax.ShapeDtypeStruct(rhs.shape, F32),
+        compiler_params=GRANT,
+        cost_estimate=lasts(1),
+        name="consensus",
+    )(rhs, arrived)
+
+
+def finish_kernel(solved_ref, gains_ref, dual_ref, ratio_ref, consensus_out, dual_out):
+    channels = ratio_ref.shape[1]
+    own = lax.broadcasted_iota(jnp.int32, (channels, channels), 0)
+    own = own == lax.broadcasted_iota(jnp.int32, (channels, channels), 1)
+    columns = [
+        jnp.sum(
+            jnp.where(own, jnp.broadcast_to(row, (channels, channels)), 0.0),
+            axis=1,
+            keepdims=True,
+        )
+        for row in legendre(ratio_ref[...])
+    ]
+    for k in range(DIRS):
+        rows = [solved_ref[k, j : j + 1, :] for j in range(NPOLY)]
+        for j in range(NPOLY):
+            consensus_out[0, j, k : k + 1, :] = rows[j]
+        fitted = sum(columns[j] * rows[j] for j in range(NPOLY))
+        dual_out[0, k] = dual_ref[0, k] + gains_ref[0, k] - fitted
+
+
+def finish_call(solved, gains, dual, ratio):
+    channels = ratio.shape[0]
+    big = pl.BlockSpec((1, DIRS, channels, STATIONS), lambda c: (c, 0, 0, 0))
+    return pl.pallas_call(
+        finish_kernel,
+        grid=(2,),
+        in_specs=[
+            pl.BlockSpec((DIRS, NPOLY, STATIONS), lambda c: (c, 0, 0)),
+            big,
+            big,
+            pl.BlockSpec((1, channels), lambda c: (0, 0)),
+        ],
+        out_specs=[pl.BlockSpec((1, NPOLY, DIRS, STATIONS), lambda c: (c, 0, 0, 0)), big],
+        out_shape=[
+            jax.ShapeDtypeStruct((2, NPOLY, DIRS, STATIONS), F32),
+            jax.ShapeDtypeStruct(dual.shape, F32),
+        ],
+        cost_estimate=lasts(1),
+        name="finish",
+    )(solved, gains, dual, ratio.reshape(1, -1))
+
+
 def own_channels(array, axis, own):
     return lax.dynamic_slice_in_dim(array, own * FEW, FEW, axis)
 
 
+def pack_kernel(vis_ref, flag_ref, pair_ref, coord_ref, out_ref):
+    def run(j, carry):
+        lanes = pl.ds(pl.multiple_of(j * 128, 128), 128)
+        to = pl.ds(j, 1)
+        for c in range(2):
+            for t in range(TIMES):
+                rows = vis_ref[c, t, :, lanes]
+                for f in range(PARTS * FEW):
+                    out_ref[f // FEW, (2 * c + t) * FEW + f % FEW, to, :] = rows[f : f + 1]
+                rows = coord_ref[c, t : t + 1, lanes]
+                for d in range(PARTS):
+                    out_ref[d, 12 + 2 * c + t, to, :] = rows
+        for t in range(TIMES):
+            rows = flag_ref[t, :, lanes].astype(F32)
+            for f in range(PARTS * FEW):
+                out_ref[f // FEW, 8 + t * FEW + f % FEW, to, :] = rows[f : f + 1]
+        for side in range(2):
+            rows = pair_ref[side : side + 1, lanes].astype(F32)
+            for d in range(PARTS):
+                out_ref[d, 16 + side, to, :] = rows
+        return carry
+
+    lax.fori_loop(0, out_ref.shape[2], run, 0)
+
+
 def packed(vis, flags, pairs, coords):
-    vis = vis.reshape(4, PARTS, FEW, LOCAL).transpose(1, 0, 2, 3).reshape(PARTS, 8, LOCAL)
-    flags = flags.astype(F32).reshape(TIMES, PARTS, FEW, LOCAL).transpose(1, 0, 2, 3)
-    flags = flags.reshape(PARTS, 4, LOCAL)
-    coords = jnp.broadcast_to(coords.reshape(1, 4, LOCAL), (PARTS, 4, LOCAL))
-    pairs = jnp.broadcast_to(pairs.astype(F32)[None], (PARTS, 2, LOCAL))
-    return jnp.concatenate([vis, flags, coords, pairs], axis=1)
+    half = LOCAL // 2
+    channels = vis.shape[2]
+    return pl.pallas_call(
+        pack_kernel,
+        grid=(2,),
+        in_specs=[
+            pl.BlockSpec((2, TIMES, channels, half), lambda i: (0, 0, 0, i)),
+            pl.BlockSpec((TIMES, channels, half), lambda i: (0, 0, i)),
+            pl.BlockSpec((2, half), lambda i: (0, i)),
+            pl.BlockSpec((2, TIMES, half), lambda i: (0, 0, i)),
+        ],
+        out_specs=pl.BlockSpec((PARTS, ROWS, half // 128, 128), lambda i: (0, 0, i, 0)),
+        out_shape=jax.ShapeDtypeStruct((PARTS, ROWS, LOCAL // 128, 128), F32),
+        cost_estimate=lasts(2),
+        name="pack",
+    )(vis, flags, pairs, coords)
 
 
 def body(
@@ -761,11 +818,8 @@
     )
     rhs = lax.all_to_all(rhs, FREQ, 0, 0, tiled=True)
     rhs, residuals = lax.optimization_barrier((rhs, residuals))
-    rhs = rhs.sum(axis=0)
-    sums = arrived.sum(axis=0) / lax.axis_size(BL)
-    gram = [[sums[2 + i * (i + 1) // 2 + j] for j in range(i + 1)] for i in range(NPOLY)]
-    solved = jnp.stack(cholesky_solve(gram, [rhs[j] for j in range(NPOLY)]))
-    everyone = sent_to_all(solved, FREQ)
+    solved = consensus_call(rhs, arrived, lax.axis_size(BL))
+    everyone = lax.all_to_all(solved, FREQ, 0, 0, tiled=True)
     new_consensus, new_dual = finish_call(everyone, new_gains, scaled_dual, channel_ratio)
     return (new_gains, new_consensus, new_dual, residuals)
 

time: 162 us -> 155 us (0.957)
  local copies, waits for them, and re-layouts: 7.45 us -> 1.98 us
  Pallas kernels: 54.7 us -> 58.7 us
  between operations: 4.84 us -> 0.84 us
  other arithmetic: 3.43 us -> 1.34 us
    pallas_call x1 -> x3, Pallas kernels: 0.99 us -> 4.94 us  [the longest x1 2.67 us: packed(): pl.pallas_call(pack_kernel, grid=(2,), in_specs=[pl.BlockSpec((2, TIMES,...]
    convert_element_type x2 -> x0, other arithmetic: 1.75 us -> none  [the longest x1 0.97 us: packed(): flags.astype(F32).reshape(TIMES, PARTS, FEW, LOCAL).transpose(1, 0, 2, 3)]
where the time goes in v6:
time: 155 us; the launch traced here: 154 us
  blocking collectives  60.5 us (39%)
  Pallas kernels  58.7 us (38%)
  waiting for transfers between devices  15.8 us (10%)
  starting transfers between devices  14.5 us (9%)
  local copies, waits for them, and re-layouts  1.98 us (1%)
    all_to_all x2, blocking collectives, body(): squares = lax.all_to_all(misfit[:, None], ALL, 0, 0, tiled=True)[:, 0]  27.4 us
    pallas_call x2, Pallas kernels, middle_call(): pl.pallas_call(middle_kernel, in_specs=[ON_CHIP] * 10, out_specs=[ON_CHIP...  22.7 us
    all_to_all x1, blocking collectives, body(): arrived = lax.all_to_all(payload[:, None], ALL, 0, 0, tiled=True)[:, 0]  18.2 us
    pallas_call x2, Pallas kernels, wide_model(): pl.pallas_call(functools.partial(wide_kernel, residual_out=residual_out,...  17 us
    all_to_all x1, blocking collectives, body(): everyone = lax.all_to_all(solved, FREQ, 0, 0, tiled=True)  14.8 us
    all_to_all x1, waiting for transfers between devices, body(): gathered = lax.all_to_all(gains, BL, 0, 0, tiled=True)  8.62 us
    pallas_call x1, Pallas kernels, last_call(): pl.pallas_call(last_kernel, in_specs=[ON_CHIP] * 10, out_specs=ON_CHIP, o...  8.1 us
    all_to_all x1, waiting for transfers between devices, body(): lax.all_to_all(send, BL, 0, 0, tiled=True).reshape(PARTS, ROWS, LOCAL)  7.19 us
  transfers between devices with their start and end apart: 3, of which 2 were waited for; matrix products, arithmetic and copies ran while one was open for 1% of the time, Pallas kernels for 11%

profile of v6, /device:TPU:1, one launch (start us, length us, event | category | flops | bytes accessed | tf_op | source)
XLA Modules:
  0.0 153.6 jit_solution(8186880634224850861)
XLA Ops:
  0.7 2.7 %pack.1 = f32[8,18,16,128]{3,2,1,0:T(8,128)} custom-call(f32[2,2,16,2048]{3,2,1,0:T(8,128)} %vis_ref.5, s32[2,16,2048]{2,1,0:T(8,128)} %flag_ref.5, s32[2,2048]{1,0:T(2,128)} %pair_ref.5, f32[2,2,2048]{2,1,0:T(2,128)} %coord_ref.5), custom_call_target="tpu_custom_call" | custom-call | flops 8000000 | bytes 1048576 | tf_op jit(solution)/shard_map/pack/pallas_call | solution.py:715
  3.4 6.0 %all-to-all-start = ((f32[8,288,128]{2,1,0:T(8,128)}), f32[8,288,128]{2,1,0:T(8,128)S(1)}, u32[]{:S(2)}, u32[]{:S(2)}) async-start(f32[8,288,128]{2,1,0:T(8,128)} %bitcast.53), calls=%async_computation | async-start | bytes 2359296 | tf_op jit(solution)/shard_map/all_to_all | solution.py:764
  9.5 1.0 dynamic-slice_bitcast_fusion
  10.7 0.1 bitcast_subtract_fusion
  11.0 8.5 %wide_misfit.1 = f32[128,128]{1,0:T(8,128)} custom-call(f32[256,512]{1,0:T(8,128)} %bitcast.55, f32[2,2,16,2048]{3,2,1,0:T(8,128)} %vis_ref.5, s32[2,16,2048]{2,1,0:T(8,128)} %flag_ref.5, s32[2,2048]{1,0:T(2,128)} %pair_ref.5, f32[2,2,2048]{2,1,0:T(2,128)} %coord_ref.5, f32[2,8]{1,0:T(2,128)} %dirs_ref.3, f32[8,16]{1,0:T(8,128)} %flux_ref.3, f32[1,16]{1,0:T(1,128)} %bitcast.58), custom_call_target="tpu_custom_call" | custom-call | flops 32000000 | bytes 1048576 | tf_op jit(solution)/shard_map/wide_misfit/pallas_call | solution.py:203
  19.5 7.2 %all-to-all-done = f32[8,288,128]{2,1,0:T(8,128)S(1)} async-done(((f32[8,288,128]{2,1,0:T(8,128)}), f32[8,288,128]{2,1,0:T(8,128)S(1)}, u32[]{:S(2)}, u32[]{:S(2)}) %all-to-all-start) | async-done | bytes 1179680 | tf_op jit(solution)/shard_map/all_to_all | solution.py:764
  26.7 0.2 reshape.45.data_ref
  26.9 5.9 %first_model.1 = (f32[8,32,2048]{2,1,0:T(8,128)S(1)}, f32[8,32,2048]{2,1,0:T(8,128)S(1)}, f32[8,8,2048]{2,1,0:T(8,128)S(1)}, f32[8,2,2,2,8,2048]{5,4,3,2,1,0:T(8,128)S(1)}) custom-call(f32[8,18,2048]{2,1,0:T(8,128)S(1)} %reshape.45.data_ref, f32[32,512]{1,0:T(8,128)S(1)} %bitcast.43, f32[8,8]{1,0:T(8,128)S(1)} %concatenate.3.geo_ref), custom_call_target="tpu_custom_call" | custom-call | flops 24000000 | bytes 1048576 | tf_op jit(solution)/shard_map/first_model/pallas_call | solution.py:544
  32.8 18.2 %all_to_all.35 = f32[128,1,128]{2,1,0:T(1,128)S(1)} all-to-all(f32[128,1,128]{2,1,0:T(1,128)S(1)} %bitcast.56), channel_id=1, replica_groups=mesh['bl_0'=4,'bl_1'=2,'freq_0'=4,'freq_1'=2,'freq_2'=2] {'bl_0','bl_1',..., dimensions={0} | all-to-all | bytes 131072 | tf_op jit(solution)/shard_map/all_to_all | solution.py:794
  51.1 11.3 %normal_and_model.2 = (f32[32,512]{1,0:T(8,128)S(1)}, f32[8,32,2048]{2,1,0:T(8,128)S(1)}, f32[8,32,2048]{2,1,0:T(8,128)S(1)}, f32[8,8,2048]{2,1,0:T(8,128)S(1)}, f32[128,128]{1,0:T(8,128)S(1)}) custom-call(f32[128,128]{1,0:T(8,128)S(1)} %bitcast.35, f32[128,128]{1,0:T(8,128)S(1)} %bitcast.36, f32[8,18,2048]{2,1,0:T(8,128)S(1)} %reshape.45.data_ref, ...), custom_call_target="tpu_custom_call" | custom-call | flops 56000000 | bytes 1048576 | tf_op jit(solution)/shard_map/normal_and_model/pallas_call | solution.py:562
  62.4 13.7 %all_to_all.36 = f32[128,1,128]{2,1,0:T(1,128)S(1)} all-to-all(f32[128,1,128]{2,1,0:T(1,128)S(1)} %bitcast.48), channel_id=1, replica_groups=mesh['bl_0'=4,'bl_1'=2,'freq_0'=4,'freq_1'=2,'freq_2'=2] {'bl_0','bl_1',..., dimensions={0} | all-to-all | bytes 131072 | tf_op jit(solution)/shard_map/all_to_all | solution.py:800
  76.1 11.3 %normal_and_model.3 = (f32[32,512]{1,0:T(8,128)S(1)}, f32[8,32,2048]{2,1,0:T(8,128)S(1)}, f32[8,32,2048]{2,1,0:T(8,128)S(1)}, f32[8,8,2048]{2,1,0:T(8,128)S(1)}, f32[128,128]{1,0:T(8,128)S(1)}) custom-call(f32[128,128]{1,0:T(8,128)S(1)} %bitcast.45, f32[128,128]{1,0:T(8,128)S(1)} %bitcast.37, f32[8,18,2048]{2,1,0:T(8,128)S(1)} %reshape.45.data_ref, ...), custom_call_target="tpu_custom_call" | custom-call | flops 56000000 | bytes 1048576 | tf_op jit(solution)/shard_map/normal_and_model/pallas_call | solution.py:562
  87.5 13.7 %all_to_all.37 = f32[128,1,128]{2,1,0:T(1,128)S(1)} all-to-all(f32[128,1,128]{2,1,0:T(1,128)S(1)} %bitcast.47), channel_id=1, replica_groups=mesh['bl_0'=4,'bl_1'=2,'freq_0'=4,'freq_1'=2,'freq_2'=2] {'bl_0','bl_1',..., dimensions={0} | all-to-all | bytes 131072 | tf_op jit(solution)/shard_map/all_to_all | solution.py:800
  101.2 8.1 %normal_last.1 = f32[8,32,512]{2,1,0:T(8,128)} custom-call(f32[128,128]{1,0:T(8,128)S(1)} %bitcast.46, f32[128,128]{1,0:T(8,128)S(1)} %bitcast.38, f32[8,18,2048]{2,1,0:T(8,128)S(1)} %reshape.45.data_ref, f32[8,32,2048]{2,1,0:T(8,128)S(1)} %get-tuple-element.38.left_ref, f32[8,32,2048]{2,1,0:T(8,128)S(1)} %get-tuple-element.39.right_ref, ...), custom_call_target="tpu_custom_call" | custom-call | flops 32000000 | bytes 1048576 | tf_op jit(solution)/shard_map/normal_last/pallas_call | solution.py:581
  109.3 3.5 %all-to-all-start.4 = ((f32[8,32,512]{2,1,0:T(8,128)}), f32[8,32,512]{2,1,0:T(8,128)S(1)}, u32[]{:S(2)}, u32[]{:S(2)}) async-start(f32[8,32,512]{2,1,0:T(8,128)} %normal_last.1), calls=%async_computation.4 | async-start | bytes 1048576 | tf_op jit(solution)/shard_map/all_to_all | solution.py:803
  112.8 8.6 %all-to-all-done.4 = f32[8,32,512]{2,1,0:T(8,128)S(1)} async-done(((f32[8,32,512]{2,1,0:T(8,128)}), f32[8,32,512]{2,1,0:T(8,128)S(1)}, u32[]{:S(2)}, u32[]{:S(2)}) %all-to-all-start.4) | async-done | bytes 524320 | tf_op jit(solution)/shard_map/all_to_all | solution.py:803
  121.4 0.3 copy.33
  121.7 0.4 add_reduce_fusion
  122.3 0.7 pad_maximum_fusion
  123.0 5.0 %all-to-all-start.5 = ((f32[16,3,512]{2,1,0:T(4,128)}), f32[16,3,512]{2,1,0:T(4,128)S(1)}, u32[]{:S(2)}, u32[]{:S(2)}) async-start(f32[16,3,512]{2,1,0:T(4,128)} %pad_maximum_fusion), calls=%async_computation.5 | async-start | bytes 262144 | tf_op jit(solution)/shard_map/all_to_all | solution.py:819
  128.0 8.5 %wide_residual.1 = f32[2,2,16,2048]{3,2,1,0:T(8,128)} custom-call(f32[256,512]{1,0:T(8,128)} %bitcast.50, f32[2,2,16,2048]{3,2,1,0:T(8,128)} %vis_ref.5, s32[2,16,2048]{2,1,0:T(8,128)} %flag_ref.5, s32[2,2048]{1,0:T(2,128)} %pair_ref.5, f32[2,2,2048]{2,1,0:T(2,128)} %coord_ref.5, f32[2,8]{1,0:T(2,128)} %dirs_ref.3, f32[8,16]{1,0:T(8,128)} %flux_ref.3, ...), custom_call_target="tpu_custom_call" | custom-call | flops 32000000 | bytes 1048576 | tf_op jit(solution)/shard_map/wide_residual/pallas_call | solution.py:203
  136.5 0.2 consensus.1
  136.7 14.8 %all_to_all.38.solved_ref = f32[16,3,512]{2,1,0:T(4,128)} all-to-all(f32[16,3,512]{2,1,0:T(4,128)S(1)} %consensus.1), channel_id=1, replica_groups=mesh['bl_0'=4,'bl_1'=2,'freq_0'=4,'freq_1'=2,'freq_2'=2] {'freq_0','freq..., dimensions={0} | all-to-all | bytes 196608 | tf_op jit(solution)/shard_map/all_to_all | solution.py:822
  151.5 2.1 %finish.1 = (f32[2,3,8,512]{3,2,1,0:T(8,128)}, f32[2,8,16,512]{3,2,1,0:T(8,128)}) custom-call(f32[16,3,512]{2,1,0:T(4,128)} %all_to_all.38.solved_ref, f32[2,8,16,512]{3,2,1,0:T(8,128)} %bitcast.51, f32[2,8,16,512]{3,2,1,0:T(8,128)} %dual_ref.1, f32[1,16]{1,0:T(1,128)} %bitcast.60), custom_call_target="tpu_custom_call" | custom-call | flops 4000000 | bytes 1048576 | tf_op jit(solution)/shard_map/finish/pallas_call | solution.py:664
  (35 shorter events, 0.6 us)
Async XLA Ops:
  0.6 8.7 %copy-start.8 = (f32[8]{0:T(128)S(1)}, f32[8]{0:T(128)}, u32[]{:S(2)}) copy-start(f32[8]{0:T(128)} %param.21) | copy-start | bytes 100
  0.6 8.8 %copy-start.5 = (f32[2,8]{1,0:T(2,128)S(1)}, f32[2,8]{1,0:T(2,128)}, u32[]{:S(2)}) copy-start(f32[2,8]{1,0:T(2,128)} %dirs_ref.3) | copy-start | bytes 196
  0.7 9.9 %copy-start.6 = (f32[16]{0:T(128)S(1)}, f32[16]{0:T(128)}, u32[]{:S(2)}) copy-start(f32[16]{0:T(128)} %param.17) | copy-start | bytes 196
  0.7 10.0 %copy-start.3 = (f32[2,3,8,512]{3,2,1,0:T(8,128)S(1)}, f32[2,3,8,512]{3,2,1,0:T(8,128)}, u32[]{:S(2)}) copy-start(f32[2,3,8,512]{3,2,1,0:T(8,128)} %param.20) | copy-start | bytes 294916
  0.7 10.0 %copy-start.1 = (f32[2,8,16,512]{3,2,1,0:T(8,128)S(1)}, f32[2,8,16,512]{3,2,1,0:T(8,128)}, u32[]{:S(2)}) copy-start(f32[2,8,16,512]{3,2,1,0:T(8,128)} %dual_ref.1) | copy-start | bytes 1572868
  3.4 7.5 %copy-start.4 = (f32[8,16]{1,0:T(8,128)S(1)}, f32[8,16]{1,0:T(8,128)}, u32[]{:S(2)}) copy-start(f32[8,16]{1,0:T(8,128)} %flux_ref.3) | copy-start | bytes 1540
  3.4 23.3 %all-to-all-start = ((f32[8,288,128]{2,1,0:T(8,128)}), f32[8,288,128]{2,1,0:T(8,128)S(1)}, u32[]{:S(2)}, u32[]{:S(2)}) async-start(f32[8,288,128]{2,1,0:T(8,128)} %bitcast.53), calls=%async_computation | async-start | bytes 2359296 | tf_op jit(solution)/shard_map/all_to_all | solution.py:764
  19.5 13.3 %copy-start.2 = (f32[128,128]{1,0:T(8,128)S(1)}, f32[128,128]{1,0:T(8,128)}, u32[]{:S(2)}) copy-start(f32[128,128]{1,0:T(8,128)} %wide_misfit.1) | copy-start | bytes 196612
  101.2 11.6 %copy-start.7 = (f32[16]{0:T(128)S(1)}, f32[16]{0:T(128)}, u32[]{:S(2)}) copy-start(f32[16]{0:T(128)} %param.17) | copy-start | bytes 196
  109.3 12.1 %all-to-all-start.4 = ((f32[8,32,512]{2,1,0:T(8,128)}), f32[8,32,512]{2,1,0:T(8,128)S(1)}, u32[]{:S(2)}, u32[]{:S(2)}) async-start(f32[8,32,512]{2,1,0:T(8,128)} %normal_last.1), calls=%async_computation.4 | async-start | bytes 1048576 | tf_op jit(solution)/shard_map/all_to_all | solution.py:803
  121.7 6.3 %copy-start = (f32[16,2,8,512]{3,0,2,1:T(8,128)}, f32[16,2,8,512]{3,0,2,1:T(8,128)S(1)}, u32[]{:S(2)}) copy-start(f32[16,2,8,512]{3,0,2,1:T(8,128)S(1)} %copy.33) | copy-start | bytes 1572868
  123.0 13.5 %all-to-all-start.5 = ((f32[16,3,512]{2,1,0:T(4,128)}), f32[16,3,512]{2,1,0:T(4,128)S(1)}, u32[]{:S(2)}, u32[]{:S(2)}) async-start(f32[16,3,512]{2,1,0:T(4,128)} %pad_maximum_fusion), calls=%async_computation.5 | async-start | bytes 262144 | tf_op jit(solution)/shard_map/all_to_all | solution.py:819

commit v7 on v6

--- a/solution.py
+++ b/solution.py
@@ -23,7 +23,7 @@
 LOCAL = BASELINES // PARTS
 SUB = 256
 MODEL_RUNS = 8
-NORMAL_RUNS = 4
+NORMAL_RUNS = 8
 
 robust_dof = 2.0
 small_term = 1e-06
@@ -790,7 +790,10 @@
     )
 
     left, right, error, sky = first_call(data, gains, geo)
-    payload, error, anchor = lax.optimization_barrier((payload, error, anchor))
+    all_basis = legendre(channel_ratio)
+    payload, error, anchor, *all_basis = lax.optimization_barrier(
+        (payload, error, anchor, *all_basis)
+    )
     arrived = lax.all_to_all(payload[:, None], ALL, 0, 0, tiled=True)[:, 0]
     squares = arrived
     for iteration in range(ITERS - 1):
@@ -800,6 +803,7 @@
         squares = lax.all_to_all(misfit[:, None], ALL, 0, 0, tiled=True)[:, 0]
     gains = last_call(squares, arrived, data, (left, right, error, sky), gains, anchor, geo)
 
+    gains, *all_basis = lax.optimization_barrier((gains, *all_basis))
     gathered = lax.all_to_all(gains, BL, 0, 0, tiled=True)
     new_gains = (
         gathered.reshape(PARTS * FEW, 2, DIRS, STATIONS).transpose(1, 2, 0, 3)
@@ -807,7 +811,6 @@
     new_gains = lax.optimization_barrier(new_gains)
     residuals = wide(new_gains.reshape(-1, STATIONS), residual_out=True)
 
-    all_basis = legendre(channel_ratio)
     lifted = new_gains + scaled_dual
     rhs = jnp.stack(
         [

time: 155 us -> 153 us (0.987)
  blocking collectives: 60.5 us -> 71.6 us
  waiting for transfers between devices: 15.8 us -> 7.16 us
  starting transfers between devices: 14.5 us -> 11.7 us
  Pallas kernels: 58.7 us -> 56.8 us
    all_to_all x0 -> x1, blocking collectives: none -> 11.3 us  [body(): gathered = lax.all_to_all(gains, BL, 0, 0, tiled=True)]
    all_to_all x1 -> x0, waiting for transfers between devices: 8.62 us -> none  [body(): gathered = lax.all_to_all(gains, BL, 0, 0, tiled=True)]
    all_to_all x1 -> x0, starting transfers between devices: 3.49 us -> none  [body(): gathered = lax.all_to_all(gains, BL, 0, 0, tiled=True)]
  transfers between devices with their start and end apart: 3 -> 2, of which waited for: 2 -> 1; matrix products, arithmetic and copies ran while one was open for 1% -> 1% of each run, Pallas kernels for 11% -> 11%
where the time goes in v7:
time: 153 us; the launch traced here: 151 us
  blocking collectives  71.6 us (47%)
  Pallas kernels  56.8 us (37%)
  starting transfers between devices  11.7 us (8%)
  waiting for transfers between devices  7.16 us (5%)
  local copies, waits for them, and re-layouts  1.99 us (1%)
    all_to_all x2, blocking collectives, body(): squares = lax.all_to_all(misfit[:, None], ALL, 0, 0, tiled=True)[:, 0]  27.4 us
    pallas_call x2, Pallas kernels, middle_call(): pl.pallas_call(middle_kernel, in_specs=[ON_CHIP] * 10, out_specs=[ON_CHIP...  22 us
    all_to_all x1, blocking collectives, body(): arrived = lax.all_to_all(payload[:, None], ALL, 0, 0, tiled=True)[:, 0]  18.2 us
    pallas_call x2, Pallas kernels, wide_model(): pl.pallas_call(functools.partial(wide_kernel, residual_out=residual_out,...  17 us
    all_to_all x1, blocking collectives, body(): everyone = lax.all_to_all(solved, FREQ, 0, 0, tiled=True)  14.7 us
    all_to_all x1, blocking collectives, body(): gathered = lax.all_to_all(gains, BL, 0, 0, tiled=True)  11.3 us
    all_to_all x1, waiting for transfers between devices, body(): lax.all_to_all(send, BL, 0, 0, tiled=True).reshape(PARTS, ROWS, LOCAL)  7.16 us
    pallas_call x1, Pallas kernels, last_call(): pl.pallas_call(last_kernel, in_specs=[ON_CHIP] * 10, out_specs=ON_CHIP, o...  6.94 us
  transfers between devices with their start and end apart: 2, of which 1 were waited for; matrix products, arithmetic and copies ran while one was open for 1% of the time, Pallas kernels for 11%

profile of v7, /device:TPU:1, one launch (start us, length us, event | category | flops | bytes accessed | tf_op | source)
XLA Modules:
  0.0 151.5 jit_solution(6721238275949773616)
XLA Ops:
  0.7 2.7 %pack.1 = f32[8,18,16,128]{3,2,1,0:T(8,128)} custom-call(f32[2,2,16,2048]{3,2,1,0:T(8,128)} %vis_ref.5, s32[2,16,2048]{2,1,0:T(8,128)} %flag_ref.5, s32[2,2048]{1,0:T(2,128)} %pair_ref.5, f32[2,2,2048]{2,1,0:T(2,128)} %coord_ref.5), custom_call_target="tpu_custom_call" | custom-call | flops 8000000 | bytes 1048576 | tf_op jit(solution)/shard_map/pack/pallas_call | solution.py:715
  3.4 6.0 %all-to-all-start = ((f32[8,288,128]{2,1,0:T(8,128)}), f32[8,288,128]{2,1,0:T(8,128)S(1)}, u32[]{:S(2)}, u32[]{:S(2)}) async-start(f32[8,288,128]{2,1,0:T(8,128)} %bitcast.53), calls=%async_computation | async-start | bytes 2359296 | tf_op jit(solution)/shard_map/all_to_all | solution.py:764
  9.4 1.0 dynamic-slice_bitcast_fusion
  10.4 0.1 add_multiply_fusion.3
  10.7 0.1 bitcast_subtract_fusion
  11.0 8.5 %wide_misfit.1 = f32[128,128]{1,0:T(8,128)} custom-call(f32[256,512]{1,0:T(8,128)} %bitcast.55, f32[2,2,16,2048]{3,2,1,0:T(8,128)} %vis_ref.5, s32[2,16,2048]{2,1,0:T(8,128)} %flag_ref.5, s32[2,2048]{1,0:T(2,128)} %pair_ref.5, f32[2,2,2048]{2,1,0:T(2,128)} %coord_ref.5, f32[2,8]{1,0:T(2,128)} %dirs_ref.3, f32[8,16]{1,0:T(8,128)} %flux_ref.3, f32[1,16]{1,0:T(1,128)} %bitcast.58), custom_call_target="tpu_custom_call" | custom-call | flops 32000000 | bytes 1048576 | tf_op jit(solution)/shard_map/wide_misfit/pallas_call | solution.py:203
  19.6 7.2 %all-to-all-done = f32[8,288,128]{2,1,0:T(8,128)S(1)} async-done(((f32[8,288,128]{2,1,0:T(8,128)}), f32[8,288,128]{2,1,0:T(8,128)S(1)}, u32[]{:S(2)}, u32[]{:S(2)}) %all-to-all-start) | async-done | bytes 1179680 | tf_op jit(solution)/shard_map/all_to_all | solution.py:764
  26.7 0.2 reshape.46.data_ref
  26.9 5.9 %first_model.1 = (f32[8,32,2048]{2,1,0:T(8,128)S(1)}, f32[8,32,2048]{2,1,0:T(8,128)S(1)}, f32[8,8,2048]{2,1,0:T(8,128)S(1)}, f32[8,2,2,2,8,2048]{5,4,3,2,1,0:T(8,128)S(1)}) custom-call(f32[8,18,2048]{2,1,0:T(8,128)S(1)} %reshape.46.data_ref, f32[32,512]{1,0:T(8,128)S(1)} %bitcast.43, f32[8,8]{1,0:T(8,128)S(1)} %concatenate.3.geo_ref), custom_call_target="tpu_custom_call" | custom-call | flops 24000000 | bytes 1048576 | tf_op jit(solution)/shard_map/first_model/pallas_call | solution.py:544
  32.8 18.2 %all_to_all.35 = f32[128,1,128]{2,1,0:T(1,128)S(1)} all-to-all(f32[128,1,128]{2,1,0:T(1,128)S(1)} %bitcast.56), channel_id=1, replica_groups=mesh['bl_0'=4,'bl_1'=2,'freq_0'=4,'freq_1'=2,'freq_2'=2] {'bl_0','bl_1',..., dimensions={0} | all-to-all | bytes 131072 | tf_op jit(solution)/shard_map/all_to_all | solution.py:797
  51.1 11.0 %normal_and_model.2 = (f32[32,512]{1,0:T(8,128)S(1)}, f32[8,32,2048]{2,1,0:T(8,128)S(1)}, f32[8,32,2048]{2,1,0:T(8,128)S(1)}, f32[8,8,2048]{2,1,0:T(8,128)S(1)}, f32[128,128]{1,0:T(8,128)S(1)}) custom-call(f32[128,128]{1,0:T(8,128)S(1)} %bitcast.35, f32[128,128]{1,0:T(8,128)S(1)} %bitcast.36, f32[8,18,2048]{2,1,0:T(8,128)S(1)} %reshape.46.data_ref, ...), custom_call_target="tpu_custom_call" | custom-call | flops 56000000 | bytes 1048576 | tf_op jit(solution)/shard_map/normal_and_model/pallas_call | solution.py:562
  62.1 13.7 %all_to_all.36 = f32[128,1,128]{2,1,0:T(1,128)S(1)} all-to-all(f32[128,1,128]{2,1,0:T(1,128)S(1)} %bitcast.48), channel_id=1, replica_groups=mesh['bl_0'=4,'bl_1'=2,'freq_0'=4,'freq_1'=2,'freq_2'=2] {'bl_0','bl_1',..., dimensions={0} | all-to-all | bytes 131072 | tf_op jit(solution)/shard_map/all_to_all | solution.py:803
  75.8 11.0 %normal_and_model.3 = (f32[32,512]{1,0:T(8,128)S(1)}, f32[8,32,2048]{2,1,0:T(8,128)S(1)}, f32[8,32,2048]{2,1,0:T(8,128)S(1)}, f32[8,8,2048]{2,1,0:T(8,128)S(1)}, f32[128,128]{1,0:T(8,128)S(1)}) custom-call(f32[128,128]{1,0:T(8,128)S(1)} %bitcast.45, f32[128,128]{1,0:T(8,128)S(1)} %bitcast.37, f32[8,18,2048]{2,1,0:T(8,128)S(1)} %reshape.46.data_ref, ...), custom_call_target="tpu_custom_call" | custom-call | flops 56000000 | bytes 1048576 | tf_op jit(solution)/shard_map/normal_and_model/pallas_call | solution.py:562
  86.8 13.7 %all_to_all.37 = f32[128,1,128]{2,1,0:T(1,128)S(1)} all-to-all(f32[128,1,128]{2,1,0:T(1,128)S(1)} %bitcast.47), channel_id=1, replica_groups=mesh['bl_0'=4,'bl_1'=2,'freq_0'=4,'freq_1'=2,'freq_2'=2] {'bl_0','bl_1',..., dimensions={0} | all-to-all | bytes 131072 | tf_op jit(solution)/shard_map/all_to_all | solution.py:803
  100.5 6.9 %normal_last.1 = f32[8,32,512]{2,1,0:T(8,128)S(1)} custom-call(f32[128,128]{1,0:T(8,128)S(1)} %bitcast.46, f32[128,128]{1,0:T(8,128)S(1)} %bitcast.38, f32[8,18,2048]{2,1,0:T(8,128)S(1)} %reshape.46.data_ref, f32[8,32,2048]{2,1,0:T(8,128)S(1)} %get-tuple-element.45.left_ref, f32[8,32,2048]{2,1,0:T(8,128)S(1)} %get-tuple-element.46.right_ref, ...), custom_call_target="tpu_custom_call" | custom-call | flops 32000000 | bytes 1048576 | tf_op jit(solution)/shard_map/normal_last/pallas_call | solution.py:581
  107.5 11.3 %all_to_all.38 = f32[8,32,512]{2,1,0:T(8,128)S(1)} all-to-all(f32[8,32,512]{2,1,0:T(8,128)S(1)} %normal_last.1), channel_id=1, replica_groups=mesh['bl_0'=4,'bl_1'=2,'freq_0'=4,'freq_1'=2,'freq_2'=2] {'bl_0','bl_1'}, dimensions={0} | all-to-all | bytes 1048576 | tf_op jit(solution)/shard_map/all_to_all | solution.py:807
  118.7 0.3 copy.33
  119.0 0.4 multiply_reduce_fusion.2
  119.6 0.7 pad_maximum_fusion
  120.3 5.7 %all-to-all-start.5 = ((f32[16,3,512]{2,1,0:T(4,128)}), f32[16,3,512]{2,1,0:T(4,128)S(1)}, u32[]{:S(2)}, u32[]{:S(2)}) async-start(f32[16,3,512]{2,1,0:T(4,128)} %pad_maximum_fusion), calls=%async_computation.5 | async-start | bytes 262144 | tf_op jit(solution)/shard_map/all_to_all | solution.py:822
  126.0 8.5 %wide_residual.1 = f32[2,2,16,2048]{3,2,1,0:T(8,128)} custom-call(f32[256,512]{1,0:T(8,128)} %bitcast.50, f32[2,2,16,2048]{3,2,1,0:T(8,128)} %vis_ref.5, s32[2,16,2048]{2,1,0:T(8,128)} %flag_ref.5, s32[2,2048]{1,0:T(2,128)} %pair_ref.5, f32[2,2,2048]{2,1,0:T(2,128)} %coord_ref.5, f32[2,8]{1,0:T(2,128)} %dirs_ref.3, f32[8,16]{1,0:T(8,128)} %flux_ref.3, ...), custom_call_target="tpu_custom_call" | custom-call | flops 32000000 | bytes 1048576 | tf_op jit(solution)/shard_map/wide_residual/pallas_call | solution.py:203
  134.5 0.2 consensus.1
  134.7 14.7 %all_to_all.39.solved_ref = f32[16,3,512]{2,1,0:T(4,128)} all-to-all(f32[16,3,512]{2,1,0:T(4,128)S(1)} %consensus.1), channel_id=1, replica_groups=mesh['bl_0'=4,'bl_1'=2,'freq_0'=4,'freq_1'=2,'freq_2'=2] {'freq_0','freq..., dimensions={0} | all-to-all | bytes 196608 | tf_op jit(solution)/shard_map/all_to_all | solution.py:825
  149.4 2.1 %finish.1 = (f32[2,3,8,512]{3,2,1,0:T(8,128)}, f32[2,8,16,512]{3,2,1,0:T(8,128)}) custom-call(f32[16,3,512]{2,1,0:T(4,128)} %all_to_all.39.solved_ref, f32[2,8,16,512]{3,2,1,0:T(8,128)} %bitcast.51, f32[2,8,16,512]{3,2,1,0:T(8,128)} %dual_ref.1, f32[1,16]{1,0:T(1,128)} %bitcast.60), custom_call_target="tpu_custom_call" | custom-call | flops 4000000 | bytes 1048576 | tf_op jit(solution)/shard_map/finish/pallas_call | solution.py:664
  (35 shorter events, 0.5 us)
Async XLA Ops:
  0.6 8.7 %copy-start.8 = (f32[8]{0:T(128)S(1)}, f32[8]{0:T(128)}, u32[]{:S(2)}) copy-start(f32[8]{0:T(128)} %param.21) | copy-start | bytes 100
  0.6 9.7 %copy-start.6 = (f32[16]{0:T(128)S(1)}, f32[16]{0:T(128)}, u32[]{:S(2)}) copy-start(f32[16]{0:T(128)} %param.17) | copy-start | bytes 196
  0.7 9.9 %copy-start.5 = (f32[2,8]{1,0:T(2,128)S(1)}, f32[2,8]{1,0:T(2,128)}, u32[]{:S(2)}) copy-start(f32[2,8]{1,0:T(2,128)} %dirs_ref.3) | copy-start | bytes 196
  0.7 10.0 %copy-start.3 = (f32[2,3,8,512]{3,2,1,0:T(8,128)S(1)}, f32[2,3,8,512]{3,2,1,0:T(8,128)}, u32[]{:S(2)}) copy-start(f32[2,3,8,512]{3,2,1,0:T(8,128)} %param.20) | copy-start | bytes 294916
  0.7 10.0 %copy-start.1 = (f32[2,8,16,512]{3,2,1,0:T(8,128)S(1)}, f32[2,8,16,512]{3,2,1,0:T(8,128)}, u32[]{:S(2)}) copy-start(f32[2,8,16,512]{3,2,1,0:T(8,128)} %dual_ref.1) | copy-start | bytes 1572868
  3.4 7.5 %copy-start.4 = (f32[8,16]{1,0:T(8,128)S(1)}, f32[8,16]{1,0:T(8,128)}, u32[]{:S(2)}) copy-start(f32[8,16]{1,0:T(8,128)} %flux_ref.3) | copy-start | bytes 1540
  3.4 16.2 %copy-start.7 = (f32[16]{0:T(128)S(1)}, f32[16]{0:T(128)}, u32[]{:S(2)}) copy-start(f32[16]{0:T(128)} %param.17) | copy-start | bytes 196
  3.4 23.3 %all-to-all-start = ((f32[8,288,128]{2,1,0:T(8,128)}), f32[8,288,128]{2,1,0:T(8,128)S(1)}, u32[]{:S(2)}, u32[]{:S(2)}) async-start(f32[8,288,128]{2,1,0:T(8,128)} %bitcast.53), calls=%async_computation | async-start | bytes 2359296 | tf_op jit(solution)/shard_map/all_to_all | solution.py:764
  19.5 13.3 %copy-start.2 = (f32[128,128]{1,0:T(8,128)S(1)}, f32[128,128]{1,0:T(8,128)}, u32[]{:S(2)}) copy-start(f32[128,128]{1,0:T(8,128)} %wide_misfit.1) | copy-start | bytes 196612
  119.0 7.0 %copy-start = (f32[16,2,8,512]{3,0,2,1:T(8,128)}, f32[16,2,8,512]{3,0,2,1:T(8,128)S(1)}, u32[]{:S(2)}) copy-start(f32[16,2,8,512]{3,0,2,1:T(8,128)S(1)} %copy.33) | copy-start | bytes 1572868
  120.3 14.2 %all-to-all-start.5 = ((f32[16,3,512]{2,1,0:T(4,128)}), f32[16,3,512]{2,1,0:T(4,128)S(1)}, u32[]{:S(2)}, u32[]{:S(2)}) async-start(f32[16,3,512]{2,1,0:T(4,128)} %pad_maximum_fusion), calls=%async_computation.5 | async-start | bytes 262144 | tf_op jit(solution)/shard_map/all_to_all | solution.py:822

commit v8 on v7

--- a/solution.py
+++ b/solution.py
@@ -790,7 +790,7 @@
     )
 
     left, right, error, sky = first_call(data, gains, geo)
-    all_basis = legendre(channel_ratio)
+    all_basis = [jnp.stack(legendre(channel_ratio))]
     payload, error, anchor, *all_basis = lax.optimization_barrier(
         (payload, error, anchor, *all_basis)
     )
@@ -812,13 +812,8 @@
     residuals = wide(new_gains.reshape(-1, STATIONS), residual_out=True)
 
     lifted = new_gains + scaled_dual
-    rhs = jnp.stack(
-        [
-            (all_basis[j][None, None, :, None] * lifted).sum(axis=2).reshape(-1, STATIONS)
-            for j in range(NPOLY)
-        ],
-        axis=1,
-    )
+    wide_basis = all_basis[0][None, :, :, None]
+    rhs = (wide_basis * lifted.reshape(-1, 1, *lifted.shape[2:])).sum(axis=2)
     rhs = lax.all_to_all(rhs, FREQ, 0, 0, tiled=True)
     rhs, residuals = lax.optimization_barrier((rhs, residuals))
     solved = consensus_call(rhs, arrived, lax.axis_size(BL))

time: 153 us -> 152 us (level)
  no operation moved by 1% of the time
where the time goes in v8:
time: 152 us; the launch traced here: 151 us
  blocking collectives  71.5 us (47%)
  Pallas kernels  56.8 us (37%)
  starting transfers between devices  11.7 us (8%)
  waiting for transfers between devices  7.09 us (5%)
  local copies, waits for them, and re-layouts  1.86 us (1%)
    all_to_all x2, blocking collectives, body(): squares = lax.all_to_all(misfit[:, None], ALL, 0, 0, tiled=True)[:, 0]  27.4 us
    pallas_call x2, Pallas kernels, middle_call(): pl.pallas_call(middle_kernel, in_specs=[ON_CHIP] * 10, out_specs=[ON_CHIP...  22 us
    all_to_all x1, blocking collectives, body(): arrived = lax.all_to_all(payload[:, None], ALL, 0, 0, tiled=True)[:, 0]  18.2 us
    pallas_call x2, Pallas kernels, wide_model(): pl.pallas_call(functools.partial(wide_kernel, residual_out=residual_out,...  17 us
    all_to_all x1, blocking collectives, body(): everyone = lax.all_to_all(solved, FREQ, 0, 0, tiled=True)  14.7 us
    all_to_all x1, blocking collectives, body(): gathered = lax.all_to_all(gains, BL, 0, 0, tiled=True)  11.1 us
    all_to_all x1, waiting for transfers between devices, body(): lax.all_to_all(send, BL, 0, 0, tiled=True).reshape(PARTS, ROWS, LOCAL)  7.09 us
    pallas_call x1, Pallas kernels, last_call(): pl.pallas_call(last_kernel, in_specs=[ON_CHIP] * 10, out_specs=ON_CHIP, o...  6.94 us
  transfers between devices with their start and end apart: 2, of which 1 were waited for; matrix products, arithmetic and copies ran while one was open for 1% of the time, Pallas kernels for 11%

profile of v8, /device:TPU:1, one launch (start us, length us, event | category | flops | bytes accessed | tf_op | source)
XLA Modules:
  0.0 151.2 jit_solution(10939756223450475517)
XLA Ops:
  0.7 2.7 %pack.1 = f32[8,18,16,128]{3,2,1,0:T(8,128)} custom-call(f32[2,2,16,2048]{3,2,1,0:T(8,128)} %vis_ref.5, s32[2,16,2048]{2,1,0:T(8,128)} %flag_ref.5, s32[2,2048]{1,0:T(2,128)} %pair_ref.5, f32[2,2,2048]{2,1,0:T(2,128)} %coord_ref.5), custom_call_target="tpu_custom_call" | custom-call | flops 8000000 | bytes 1048576 | tf_op jit(solution)/shard_map/pack/pallas_call | solution.py:715
  3.4 6.0 %all-to-all-start = ((f32[8,288,128]{2,1,0:T(8,128)}), f32[8,288,128]{2,1,0:T(8,128)S(1)}, u32[]{:S(2)}, u32[]{:S(2)}) async-start(f32[8,288,128]{2,1,0:T(8,128)} %bitcast.59), calls=%async_computation | async-start | bytes 2359296 | tf_op jit(solution)/shard_map/all_to_all | solution.py:764
  9.5 1.0 dynamic-slice_bitcast_fusion
  10.4 0.1 copy.34
  10.7 0.1 bitcast_subtract_fusion
  11.0 8.5 %wide_misfit.1 = f32[128,128]{1,0:T(8,128)} custom-call(f32[256,512]{1,0:T(8,128)} %bitcast.62, f32[2,2,16,2048]{3,2,1,0:T(8,128)} %vis_ref.5, s32[2,16,2048]{2,1,0:T(8,128)} %flag_ref.5, s32[2,2048]{1,0:T(2,128)} %pair_ref.5, f32[2,2,2048]{2,1,0:T(2,128)} %coord_ref.5, f32[2,8]{1,0:T(2,128)} %dirs_ref.3, f32[8,16]{1,0:T(8,128)} %flux_ref.3, f32[1,16]{1,0:T(1,128)} %bitcast.65), custom_call_target="tpu_custom_call" | custom-call | flops 32000000 | bytes 1048576 | tf_op jit(solution)/shard_map/wide_misfit/pallas_call | solution.py:203
  19.6 7.1 %all-to-all-done = f32[8,288,128]{2,1,0:T(8,128)S(1)} async-done(((f32[8,288,128]{2,1,0:T(8,128)}), f32[8,288,128]{2,1,0:T(8,128)S(1)}, u32[]{:S(2)}, u32[]{:S(2)}) %all-to-all-start) | async-done | bytes 1179680 | tf_op jit(solution)/shard_map/all_to_all | solution.py:764
  26.7 0.2 reshape.46.data_ref
  26.9 5.9 %first_model.1 = (f32[8,32,2048]{2,1,0:T(8,128)S(1)}, f32[8,32,2048]{2,1,0:T(8,128)S(1)}, f32[8,8,2048]{2,1,0:T(8,128)S(1)}, f32[8,2,2,2,8,2048]{5,4,3,2,1,0:T(8,128)S(1)}) custom-call(f32[8,18,2048]{2,1,0:T(8,128)S(1)} %reshape.46.data_ref, f32[32,512]{1,0:T(8,128)S(1)} %bitcast.49, f32[8,8]{1,0:T(8,128)S(1)} %concatenate.3.geo_ref), custom_call_target="tpu_custom_call" | custom-call | flops 24000000 | bytes 1048576 | tf_op jit(solution)/shard_map/first_model/pallas_call | solution.py:544
  32.8 18.2 %all_to_all.35 = f32[128,1,128]{2,1,0:T(1,128)S(1)} all-to-all(f32[128,1,128]{2,1,0:T(1,128)S(1)} %bitcast.63), channel_id=1, replica_groups=mesh['bl_0'=4,'bl_1'=2,'freq_0'=4,'freq_1'=2,'freq_2'=2] {'bl_0','bl_1',..., dimensions={0} | all-to-all | bytes 131072 | tf_op jit(solution)/shard_map/all_to_all | solution.py:797
  51.1 11.0 %normal_and_model.2 = (f32[32,512]{1,0:T(8,128)S(1)}, f32[8,32,2048]{2,1,0:T(8,128)S(1)}, f32[8,32,2048]{2,1,0:T(8,128)S(1)}, f32[8,8,2048]{2,1,0:T(8,128)S(1)}, f32[128,128]{1,0:T(8,128)S(1)}) custom-call(f32[128,128]{1,0:T(8,128)S(1)} %bitcast.41, f32[128,128]{1,0:T(8,128)S(1)} %bitcast.42, f32[8,18,2048]{2,1,0:T(8,128)S(1)} %reshape.46.data_ref, ...), custom_call_target="tpu_custom_call" | custom-call | flops 56000000 | bytes 1048576 | tf_op jit(solution)/shard_map/normal_and_model/pallas_call | solution.py:562
  62.1 13.7 %all_to_all.36 = f32[128,1,128]{2,1,0:T(1,128)S(1)} all-to-all(f32[128,1,128]{2,1,0:T(1,128)S(1)} %bitcast.54), channel_id=1, replica_groups=mesh['bl_0'=4,'bl_1'=2,'freq_0'=4,'freq_1'=2,'freq_2'=2] {'bl_0','bl_1',..., dimensions={0} | all-to-all | bytes 131072 | tf_op jit(solution)/shard_map/all_to_all | solution.py:803
  75.8 11.0 %normal_and_model.3 = (f32[32,512]{1,0:T(8,128)S(1)}, f32[8,32,2048]{2,1,0:T(8,128)S(1)}, f32[8,32,2048]{2,1,0:T(8,128)S(1)}, f32[8,8,2048]{2,1,0:T(8,128)S(1)}, f32[128,128]{1,0:T(8,128)S(1)}) custom-call(f32[128,128]{1,0:T(8,128)S(1)} %bitcast.51, f32[128,128]{1,0:T(8,128)S(1)} %bitcast.43, f32[8,18,2048]{2,1,0:T(8,128)S(1)} %reshape.46.data_ref, ...), custom_call_target="tpu_custom_call" | custom-call | flops 56000000 | bytes 1048576 | tf_op jit(solution)/shard_map/normal_and_model/pallas_call | solution.py:562
  86.8 13.7 %all_to_all.37 = f32[128,1,128]{2,1,0:T(1,128)S(1)} all-to-all(f32[128,1,128]{2,1,0:T(1,128)S(1)} %bitcast.53), channel_id=1, replica_groups=mesh['bl_0'=4,'bl_1'=2,'freq_0'=4,'freq_1'=2,'freq_2'=2] {'bl_0','bl_1',..., dimensions={0} | all-to-all | bytes 131072 | tf_op jit(solution)/shard_map/all_to_all | solution.py:803
  100.5 6.9 %normal_last.1 = f32[8,32,512]{2,1,0:T(8,128)S(1)} custom-call(f32[128,128]{1,0:T(8,128)S(1)} %bitcast.52, f32[128,128]{1,0:T(8,128)S(1)} %bitcast.44, f32[8,18,2048]{2,1,0:T(8,128)S(1)} %reshape.46.data_ref, f32[8,32,2048]{2,1,0:T(8,128)S(1)} %get-tuple-element.41.left_ref, f32[8,32,2048]{2,1,0:T(8,128)S(1)} %get-tuple-element.42.right_ref, ...), custom_call_target="tpu_custom_call" | custom-call | flops 32000000 | bytes 1048576 | tf_op jit(solution)/shard_map/normal_last/pallas_call | solution.py:581
  107.5 11.1 %all_to_all.38 = f32[8,32,512]{2,1,0:T(8,128)S(1)} all-to-all(f32[8,32,512]{2,1,0:T(8,128)S(1)} %normal_last.1), channel_id=1, replica_groups=mesh['bl_0'=4,'bl_1'=2,'freq_0'=4,'freq_1'=2,'freq_2'=2] {'bl_0','bl_1'}, dimensions={0} | all-to-all | bytes 1048576 | tf_op jit(solution)/shard_map/all_to_all | solution.py:807
  118.5 0.3 copy.41
  118.9 0.1 add.26
  119.0 1.0 multiply_reduce_fusion
  120.0 5.7 %all-to-all-start.5 = ((f32[16,3,512]{2,1,0:T(4,128)}), f32[16,3,512]{2,1,0:T(4,128)S(1)}, u32[]{:S(2)}, u32[]{:S(2)}) async-start(f32[16,3,512]{2,1,0:T(4,128)} %multiply_reduce_fusion), calls=%async_computation.5 | async-start | bytes 262144 | tf_op jit(solution)/shard_map/all_to_all | solution.py:817
  125.7 8.5 %wide_residual.1 = f32[2,2,16,2048]{3,2,1,0:T(8,128)} custom-call(f32[256,512]{1,0:T(8,128)} %bitcast.56, f32[2,2,16,2048]{3,2,1,0:T(8,128)} %vis_ref.5, s32[2,16,2048]{2,1,0:T(8,128)} %flag_ref.5, s32[2,2048]{1,0:T(2,128)} %pair_ref.5, f32[2,2,2048]{2,1,0:T(2,128)} %coord_ref.5, f32[2,8]{1,0:T(2,128)} %dirs_ref.3, f32[8,16]{1,0:T(8,128)} %flux_ref.3, ...), custom_call_target="tpu_custom_call" | custom-call | flops 32000000 | bytes 1048576 | tf_op jit(solution)/shard_map/wide_residual/pallas_call | solution.py:203
  134.1 0.2 consensus.1
  134.3 14.7 %all_to_all.39.solved_ref = f32[16,3,512]{2,1,0:T(4,128)} all-to-all(f32[16,3,512]{2,1,0:T(4,128)S(1)} %consensus.1), channel_id=1, replica_groups=mesh['bl_0'=4,'bl_1'=2,'freq_0'=4,'freq_1'=2,'freq_2'=2] {'freq_0','freq..., dimensions={0} | all-to-all | bytes 196608 | tf_op jit(solution)/shard_map/all_to_all | solution.py:820
  149.1 2.1 %finish.1 = (f32[2,3,8,512]{3,2,1,0:T(8,128)}, f32[2,8,16,512]{3,2,1,0:T(8,128)}) custom-call(f32[16,3,512]{2,1,0:T(4,128)} %all_to_all.39.solved_ref, f32[2,8,16,512]{3,2,1,0:T(8,128)} %bitcast.57, f32[2,8,16,512]{3,2,1,0:T(8,128)} %dual_ref.1, f32[1,16]{1,0:T(1,128)} %bitcast.67), custom_call_target="tpu_custom_call" | custom-call | flops 4000000 | bytes 1048576 | tf_op jit(solution)/shard_map/finish/pallas_call | solution.py:664
  (33 shorter events, 0.5 us)
Async XLA Ops:
  0.6 8.7 %copy-start.8 = (f32[8]{0:T(128)S(1)}, f32[8]{0:T(128)}, u32[]{:S(2)}) copy-start(f32[8]{0:T(128)} %param.21) | copy-start | bytes 100
  0.6 8.7 %copy-start.6 = (f32[16]{0:T(128)S(1)}, f32[16]{0:T(128)}, u32[]{:S(2)}) copy-start(f32[16]{0:T(128)} %param.17) | copy-start | bytes 196
  0.7 9.9 %copy-start.5 = (f32[2,8]{1,0:T(2,128)S(1)}, f32[2,8]{1,0:T(2,128)}, u32[]{:S(2)}) copy-start(f32[2,8]{1,0:T(2,128)} %dirs_ref.3) | copy-start | bytes 196
  0.7 10.0 %copy-start.3 = (f32[2,3,8,512]{3,2,1,0:T(8,128)S(1)}, f32[2,3,8,512]{3,2,1,0:T(8,128)}, u32[]{:S(2)}) copy-start(f32[2,3,8,512]{3,2,1,0:T(8,128)} %param.20) | copy-start | bytes 294916
  0.7 10.0 %copy-start.1 = (f32[2,8,16,512]{3,2,1,0:T(8,128)S(1)}, f32[2,8,16,512]{3,2,1,0:T(8,128)}, u32[]{:S(2)}) copy-start(f32[2,8,16,512]{3,2,1,0:T(8,128)} %dual_ref.1) | copy-start | bytes 1572868
  3.3 7.5 %copy-start.4 = (f32[8,16]{1,0:T(8,128)S(1)}, f32[8,16]{1,0:T(8,128)}, u32[]{:S(2)}) copy-start(f32[8,16]{1,0:T(8,128)} %flux_ref.3) | copy-start | bytes 1540
  3.4 16.2 %copy-start.7 = (f32[16]{0:T(128)S(1)}, f32[16]{0:T(128)}, u32[]{:S(2)}) copy-start(f32[16]{0:T(128)} %param.17) | copy-start | bytes 196
  3.4 23.3 %all-to-all-start = ((f32[8,288,128]{2,1,0:T(8,128)}), f32[8,288,128]{2,1,0:T(8,128)S(1)}, u32[]{:S(2)}, u32[]{:S(2)}) async-start(f32[8,288,128]{2,1,0:T(8,128)} %bitcast.59), calls=%async_computation | async-start | bytes 2359296 | tf_op jit(solution)/shard_map/all_to_all | solution.py:764
  19.6 13.2 %copy-start.2 = (f32[128,128]{1,0:T(8,128)S(1)}, f32[128,128]{1,0:T(8,128)}, u32[]{:S(2)}) copy-start(f32[128,128]{1,0:T(8,128)} %wide_misfit.1) | copy-start | bytes 196612
  118.9 6.8 %copy-start = (f32[16,2,8,512]{3,0,2,1:T(8,128)}, f32[16,2,8,512]{3,0,2,1:T(8,128)S(1)}, u32[]{:S(2)}) copy-start(f32[16,2,8,512]{3,0,2,1:T(8,128)S(1)} %copy.41) | copy-start | bytes 1572868
  120.0 14.2 %all-to-all-start.5 = ((f32[16,3,512]{2,1,0:T(4,128)}), f32[16,3,512]{2,1,0:T(4,128)S(1)}, u32[]{:S(2)}, u32[]{:S(2)}) async-start(f32[16,3,512]{2,1,0:T(4,128)} %multiply_reduce_fusion), calls=%async_computation.5 | async-start | bytes 262144 | tf_op jit(solution)/shard_map/all_to_all | solution.py:817
